TPU v7x, 512 devices: a whole 4x4x16 slice. The times are simulated.
512 devices in a mesh: hel: 16 (over y, x_hi, core), rad: 32 (over z, x_lo).
Axes of the slice: x: 4 (x_hi: 2, x_lo: 2; x = x_hi * 2 + x_lo), y: 4, z: 16, core: 2. Of those that a mesh axis runs over, the one named last changes fastest.
Arguments:
- older_packet: float32 [16, 512, 8, 1024], P('hel', 'rad'), may hold values from -6 to 6
- newer_packet: float32 [16, 512, 8, 1024], P('hel', 'rad'), may hold values from -6 to 6
- kinetic: bfloat16 [512, 512], replicated, may hold values from -1 to 1, as said below
- transform: bfloat16 [16, 1024, 1024], P('hel'), may hold values from -0.1875 to 0.1875
- potential: bfloat16 [512, 8, 1024], P('rad'), may hold values from -2 to 2
- coupling: bfloat16 [16, 1024], P('hel'), may hold values from 0.29882812 to 1.5
- radial_weight: float32 [512], replicated, may hold values from 0.3 to 2
- damping: float32 [512], P('rad'), may hold values from 0.6 to 1
Outputs:
- older_out: float32 [16, 512, 8, 1024], P('hel', 'rad')
- newer_out: float32 [16, 512, 8, 1024], P('hel', 'rad')
Inputs may be any that keep to these rules, and one draw needn't show every extreme that they name: kinetic is symmetric.
All inputs are finite; a program needn't handle non-finite values.
Results may differ from a plain program's by a relative error of at most 0.014.
Values may be sent and summed in bfloat16 or wider, within the bound.
No kernel may reach another device: no remote copies, remote signals or barrier semaphores. Data moves between devices by JAX's collectives and lax.ppermute only.
A program may use at most 64 MiB of HBM per device.

v0:
```python
import jax
import jax.numpy as jnp
from jax import lax
from jax.sharding import Mesh
from jax.sharding import PartitionSpec as P

STEPS = 3
RAD = ("rad_0", "rad_1")


SCALE_FACTOR = 0.35


def from_behind(array, axis, by):
    devices = lax.axis_size(axis)
    pairs = [(i, i + by) for i in range(devices) if 0 <= i + by < devices]
    return lax.ppermute(array, axis, pairs)


def in_blocks(array, dim, devices):
    shape = array.shape
    tiles = array.reshape(*shape[:dim], devices, shape[dim] // devices, *shape[dim + 1 :])
    return jnp.moveaxis(tiles, dim, 0)


def in_order(tiles, dim):
    shape = list(tiles.shape[1:])
    shape[dim] *= tiles.shape[0]
    return jnp.moveaxis(tiles, 0, dim).reshape(shape)


def turned_blocks(tiles, axes, order):
    shape = [lax.axis_size(a) for a in axes]
    tiles = tiles.reshape(*shape, *tiles.shape[1:])
    for k in order:
        tiles = lax.all_to_all(tiles, axes[k], split_axis=k, concat_axis=k, tiled=True)
    return tiles.reshape(-1, *tiles.shape[len(axes) :])


def stepwise_exchange(array, axes, order, split_dim, concat_dim):
    tiles = in_blocks(array, split_dim, lax.axis_size(axes))
    return in_order(turned_blocks(tiles, axes, order), concat_dim)


def coriolis_term(block, coefs, weights):
    lower_block, lower_coefs = from_behind((block, coefs), "hel", 1)
    upper_block = from_behind(block, "hel", -1)
    below = jnp.concatenate([lower_block, block[:-1]], axis=0).astype(jnp.float32)
    below_coefs = jnp.concatenate([lower_coefs, coefs[:-1]], axis=0).astype(jnp.float32)
    above = jnp.concatenate([block[1:], upper_block], axis=0).astype(jnp.float32)
    mixed = below_coefs[:, None, :] * below + coefs.astype(jnp.float32)[:, None, :] * above
    return weights[None, :, None] * mixed


def body(
    older_packet, newer_packet, kinetic, transform, potential, coupling, radial_weight, damping
):
    hel_rows, rad_rows, vib_count, ang_count = newer_packet.shape
    flat_width = vib_count * ang_count
    rank = lax.axis_index(RAD)
    previous = older_packet.reshape(hel_rows, rad_rows, flat_width)
    current = newer_packet.reshape(hel_rows, rad_rows, flat_width)
    potential_flat = potential.astype(jnp.float32).reshape(1, rad_rows * vib_count, ang_count)
    tiled_coefs = jnp.tile(coupling, (1, vib_count))
    damp = damping[None, :, None]
    for _ in range(STEPS):
        rounded = current.astype(jnp.bfloat16)
        regrouped = stepwise_exchange(rounded, RAD, (0, 1), 2, 1)
        kinetic_term = jnp.einsum(
            "rs,ksc->krc", kinetic, regrouped, preferred_element_type=jnp.float32
        )
        returned = lax.all_to_all(kinetic_term, RAD, split_axis=1, concat_axis=2, tiled=True)
        start = rank * rad_rows
        local_weights = lax.dynamic_slice_in_dim(radial_weight, start, rad_rows, 0)
        summed = returned + coriolis_term(rounded, tiled_coefs, local_weights)
        off_grid = summed.astype(jnp.bfloat16).astype(jnp.float32)
        angular_rows = rounded.reshape(hel_rows, rad_rows * vib_count, ang_count)
        grid = jnp.einsum(
            "kna,kag->kng", angular_rows, transform, preferred_element_type=jnp.float32
        )
        grid_values = (grid * potential_flat).astype(jnp.bfloat16)
        angular_part = jnp.einsum(
            "kng,kag->kna", grid_values, transform, preferred_element_type=jnp.float32
        )
        applied = SCALE_FACTOR * (off_grid + angular_part.reshape(hel_rows, rad_rows, flat_width))
        following = damp * (2.0 * applied - damp * previous)
        previous = current
        current = following
    shape = (hel_rows, rad_rows, vib_count, ang_count)
    return (previous.reshape(shape), current.reshape(shape))


def solution(mesh):
    finer = Mesh(mesh.devices.reshape(mesh.shape["hel"], 16, 2), ("hel", "rad_0", "rad_1"))
    return jax.shard_map(
        body,
        mesh=finer,
        in_specs=(
            P("hel", RAD, None, None),
            P("hel", RAD, None, None),
            P(),
            P("hel", None, None),
            P(RAD, None, None),
            P("hel", None),
            P(),
            P(RAD),
        ),
        out_specs=(P("hel", RAD, None, None), P("hel", RAD, None, None)),
        check_vma=False,
    )
```

profile of v0, /device:TPU:6, one launch (start us, length us, event | category | flops | bytes accessed | tf_op | source)
XLA Modules:
  0.0 228.7 jit_solution(10470657694024460079)
XLA Ops:
  2.2 33.4 %all_to_all.84 = bf16[16,2,1,16,256]{4,3,1,2,0:T(8,128)(2,1)S(1)} all-to-all(bf16[16,2,1,16,256]{4,3,1,2,0:T(8,128)(2,1)S(1)} %bitcast.145), channel_id=1, replica_groups=mesh['hel'=16,'rad_0'=16,'rad_1'=2] {'rad_0'}, dimensions={0} | all-to-all | bytes 524288 | tf_op jit(solution)/shard_map/all_to_all | solution.py:36
  35.6 6.4 %all_to_all.85 = bf16[16,2,1,16,256]{4,3,0,2,1:T(8,128)(2,1)S(1)} all-to-all(bf16[16,2,1,16,256]{4,3,0,2,1:T(8,128)(2,1)S(1)} %copy.22), channel_id=1, replica_groups=mesh['hel'=16,'rad_0'=16,'rad_1'=2] {'rad_1'}, dimensions={1} | all-to-all | bytes 524288 | tf_op jit(solution)/shard_map/all_to_all | solution.py:36
  43.5 8.1 %all-to-all-start.2 = ((f32[1,512,256]{2,0,1:T(1,128)}), f32[1,512,256]{2,0,1:T(1,128)}, u32[]{:S(2)}, u32[]{:S(2)}) async-start(f32[1,512,256]{2,0,1:T(1,128)} %copy.24), calls=%async_computation.2 | async-start | bytes 1048576 | tf_op jit(solution)/shard_map/all_to_all | solution.py:72
  53.5 1.9 collective-permute-start.2
  55.4 2.4 %collective-permute-start.1 = (bf16[1,16,8192]{2,1,0:T(8,128)(2,1)}, bf16[1,16,8192]{2,1,0:T(8,128)(2,1)}, u32[]{:S(2)}, u32[]{:S(2)}) collective-permute-start(bf16[1,16,8192]{2,1,0:T(8,128)(2,1)} %convert_element_type.103), channel_id=1, source_target_pairs={{0,32},{32,64},{64,96},{96,128},{128,160},{160,192},{192,224},{224... | collective-permute-start | bytes 786440 | tf_op jit(solution)/shard_map/ppermute | solution.py:17
  57.9 3.9 %collective-permute-start = (bf16[1,8192]{1,0:T(2,128)(2,1)S(1)}, bf16[1,8192]{1,0:T(2,128)(2,1)S(1)}, u32[]{:S(2)}, u32[]{:S(2)}) collective-permute-start(bf16[1,8192]{1,0:T(2,128)(2,1)S(1)} %bitcast.158), channel_id=1, source_target_pairs={{0,32},{32,64},{64,96},{96,128},{128,160},{160,192},{192,224},{224... | collective-permute-start | bytes 49160 | tf_op jit(solution)/shard_map/ppermute | solution.py:17
  61.8 2.9 %fusion.8 = f32[128,1024]{1,0:T(8,128)} fusion(bf16[1,1024,1024]{2,1,0:T(8,128)(2,1)S(1)} %copy-done, bf16[16,8,1024]{2,1,0:T(8,128)(2,1)S(1)} %copy-done.2, bf16[1,16,8,1024]{3,2,1,0:T(8,128)(2,1)} %copy-done.3), kind=kOutput, calls=%fused_computation.8 | convolution fusion | flops 537264128 | bytes 3145728 | tf_op jit(solution)/shard_map/kng,kag->kna/dot_general | solution.py:82
  64.7 1.9 reshape.224
  66.7 1.9 reshape.225
  69.4 14.0 %all-to-all-done.2 = f32[1,512,256]{2,0,1:T(1,128)} async-done(((f32[1,512,256]{2,0,1:T(1,128)}), f32[1,512,256]{2,0,1:T(1,128)}, u32[]{:S(2)}, u32[]{:S(2)}) %all-to-all-start.2) | async-done | bytes 524320 | tf_op jit(solution)/shard_map/all_to_all | solution.py:72
  84.8 2.1 fusion.45
  87.8 20.0 %all_to_all.86 = bf16[16,2,1,16,256]{4,3,1,2,0:T(8,128)(2,1)S(1)} all-to-all(bf16[16,2,1,16,256]{4,3,1,2,0:T(8,128)(2,1)S(1)} %bitcast.146), channel_id=1, replica_groups=mesh['hel'=16,'rad_0'=16,'rad_1'=2] {'rad_0'}, dimensions={0} | all-to-all | bytes 524288 | tf_op jit(solution)/shard_map/all_to_all | solution.py:36
  107.9 6.2 %all_to_all.87 = bf16[16,2,1,16,256]{4,3,0,2,1:T(8,128)(2,1)S(1)} all-to-all(bf16[16,2,1,16,256]{4,3,0,2,1:T(8,128)(2,1)S(1)} %copy.27), channel_id=1, replica_groups=mesh['hel'=16,'rad_0'=16,'rad_1'=2] {'rad_1'}, dimensions={1} | all-to-all | bytes 524288 | tf_op jit(solution)/shard_map/all_to_all | solution.py:36
  115.3 1.9 copy.29
  117.2 7.6 %all-to-all-start.5 = ((f32[1,512,256]{2,0,1:T(1,128)}), f32[1,512,256]{2,0,1:T(1,128)}, u32[]{:S(2)}, u32[]{:S(2)}) async-start(f32[1,512,256]{2,0,1:T(1,128)} %copy.29), calls=%async_computation.5 | async-start | bytes 1048576 | tf_op jit(solution)/shard_map/all_to_all | solution.py:72
  124.8 1.8 reshape.229
  126.6 1.9 collective-permute-start.4
  128.5 2.4 %collective-permute-start.3 = (bf16[1,16,8192]{2,1,0:T(8,128)(2,1)}, bf16[1,16,8192]{2,1,0:T(8,128)(2,1)}, u32[]{:S(2)}, u32[]{:S(2)}) collective-permute-start(bf16[1,16,8192]{2,1,0:T(8,128)(2,1)} %copy-done.6), channel_id=1, source_target_pairs={{0,32},{32,64},{64,96},{96,128},{128,160},{160,192},{192,224},{224... | collective-permute-start | bytes 786440 | tf_op jit(solution)/shard_map/ppermute | solution.py:17
  130.9 2.9 %fusion.4 = f32[128,1024]{1,0:T(8,128)} fusion(bf16[1,1024,1024]{2,1,0:T(8,128)(2,1)S(1)} %copy-done, bf16[128,1024]{1,0:T(8,128)(2,1)} %reshape.229, bf16[16,8,1024]{2,1,0:T(8,128)(2,1)S(1)} %copy-done.2), kind=kOutput, calls=%fused_computation.4 | convolution fusion | flops 537264128 | bytes 3145728 | tf_op jit(solution)/shard_map/kng,kag->kna/dot_general | solution.py:82
  133.8 1.9 reshape.230
  135.7 19.1 %all-to-all-done.5 = f32[1,512,256]{2,0,1:T(1,128)} async-done(((f32[1,512,256]{2,0,1:T(1,128)}), f32[1,512,256]{2,0,1:T(1,128)}, u32[]{:S(2)}, u32[]{:S(2)}) %all-to-all-start.5) | async-done | bytes 524320 | tf_op jit(solution)/shard_map/all_to_all | solution.py:72
  156.1 2.1 fusion.44
  159.1 19.2 %all_to_all.88 = bf16[16,2,1,16,256]{4,3,1,2,0:T(8,128)(2,1)S(1)} all-to-all(bf16[16,2,1,16,256]{4,3,1,2,0:T(8,128)(2,1)S(1)} %bitcast.147), channel_id=1, replica_groups=mesh['hel'=16,'rad_0'=16,'rad_1'=2] {'rad_0'}, dimensions={0} | all-to-all | bytes 524288 | tf_op jit(solution)/shard_map/all_to_all | solution.py:36
  178.3 6.2 %all_to_all.89 = bf16[16,2,1,16,256]{4,3,0,2,1:T(8,128)(2,1)S(1)} all-to-all(bf16[16,2,1,16,256]{4,3,0,2,1:T(8,128)(2,1)S(1)} %copy.32), channel_id=1, replica_groups=mesh['hel'=16,'rad_0'=16,'rad_1'=2] {'rad_1'}, dimensions={1} | all-to-all | bytes 524288 | tf_op jit(solution)/shard_map/all_to_all | solution.py:36
  185.7 1.9 copy.34
  187.7 7.6 %all-to-all-start.8 = ((f32[1,512,256]{2,0,1:T(1,128)}), f32[1,512,256]{2,0,1:T(1,128)}, u32[]{:S(2)}, u32[]{:S(2)}) async-start(f32[1,512,256]{2,0,1:T(1,128)} %copy.34), calls=%async_computation.8 | async-start | bytes 1048576 | tf_op jit(solution)/shard_map/all_to_all | solution.py:72
  195.4 1.9 collective-permute-start.6
  197.3 2.4 %collective-permute-start.5 = (bf16[1,16,8192]{2,1,0:T(8,128)(2,1)S(1)}, bf16[1,16,8192]{2,1,0:T(8,128)(2,1)}, u32[]{:S(2)}, u32[]{:S(2)}) collective-permute-start(bf16[1,16,8192]{2,1,0:T(8,128)(2,1)S(1)} %copy-done.5), channel_id=1, source_target_pairs={{0,32},{32,64},{64,96},{96,128},{128,160},{160,192},{192,224},{224... | collective-permute-start | bytes 786440 | tf_op jit(solution)/shard_map/ppermute | solution.py:17
  199.7 2.1 copy.45
  201.9 1.9 fusion
  204.9 20.2 %all-to-all-done.8 = f32[1,512,256]{2,0,1:T(1,128)} async-done(((f32[1,512,256]{2,0,1:T(1,128)}), f32[1,512,256]{2,0,1:T(1,128)}, u32[]{:S(2)}, u32[]{:S(2)}) %all-to-all-start.8) | async-done | bytes 524320 | tf_op jit(solution)/shard_map/all_to_all | solution.py:72
  226.2 1.3 subtract_multiply_fusion
  (69 shorter events, 16.0 us)
Async XLA Ops:
  0.6 61.2 %copy-start = (bf16[1,1024,1024]{2,1,0:T(8,128)(2,1)S(1)}, bf16[1,1024,1024]{2,1,0:T(8,128)(2,1)}, u32[]{:S(2)}) copy-start(bf16[1,1024,1024]{2,1,0:T(8,128)(2,1)} %param.11) | copy-start | bytes 6291460
  0.6 41.4 %copy-start.1 = (bf16[512,512]{1,0:T(8,128)(2,1)S(1)}, bf16[512,512]{1,0:T(8,128)(2,1)}, u32[]{:S(2)}) copy-start(bf16[512,512]{1,0:T(8,128)(2,1)} %param.10) | copy-start | bytes 1572868
  1.9 40.1 %copy-start.3 = (bf16[1,16,8,1024]{3,2,1,0:T(8,128)(2,1)}, bf16[1,16,8,1024]{3,2,1,0:T(8,128)(2,1)S(1)}, u32[]{:S(2)}) copy-start(bf16[1,16,8,1024]{3,2,1,0:T(8,128)(2,1)S(1)} %convert_element_type.101) | copy-start | bytes 786436
  42.4 15.4 %copy-start.11 = (bf16[1,1024]{1,0:T(2,128)(2,1)S(1)}, bf16[1,1024]{1,0:T(2,128)(2,1)}, u32[]{:S(2)}) copy-start(bf16[1,1024]{1,0:T(2,128)(2,1)} %param.13) | copy-start | bytes 6148
  42.4 19.4 %copy-start.2 = (bf16[16,8,1024]{2,1,0:T(8,128)(2,1)S(1)}, bf16[16,8,1024]{2,1,0:T(8,128)(2,1)}, u32[]{:S(2)}) copy-start(bf16[16,8,1024]{2,1,0:T(8,128)(2,1)} %param.12) | copy-start | bytes 786436
  43.5 39.9 %all-to-all-start.2 = ((f32[1,512,256]{2,0,1:T(1,128)}), f32[1,512,256]{2,0,1:T(1,128)}, u32[]{:S(2)}, u32[]{:S(2)}) async-start(f32[1,512,256]{2,0,1:T(1,128)} %copy.24), calls=%async_computation.2 | async-start | bytes 1048576 | tf_op jit(solution)/shard_map/all_to_all | solution.py:72
  53.5 31.2 %collective-permute-start.2 = (bf16[1,16,8192]{2,1,0:T(8,128)(2,1)}, bf16[1,16,8192]{2,1,0:T(8,128)(2,1)}, u32[]{:S(2)}, u32[]{:S(2)}) collective-permute-start(bf16[1,16,8192]{2,1,0:T(8,128)(2,1)} %convert_element_type.103), channel_id=1, source_target_pairs={{32,0},{64,32},{96,64},{128,96},{160,128},{192,160},{224,192},{256... | collective-permute-start | bytes 786440 | tf_op jit(solution)/shard_map/ppermute | solution.py:17
  55.4 29.3 %collective-permute-start.1 = (bf16[1,16,8192]{2,1,0:T(8,128)(2,1)}, bf16[1,16,8192]{2,1,0:T(8,128)(2,1)}, u32[]{:S(2)}, u32[]{:S(2)}) collective-permute-start(bf16[1,16,8192]{2,1,0:T(8,128)(2,1)} %convert_element_type.103), channel_id=1, source_target_pairs={{0,32},{32,64},{64,96},{96,128},{128,160},{160,192},{192,224},{224... | collective-permute-start | bytes 786440 | tf_op jit(solution)/shard_map/ppermute | solution.py:17
  57.9 11.5 %collective-permute-start = (bf16[1,8192]{1,0:T(2,128)(2,1)S(1)}, bf16[1,8192]{1,0:T(2,128)(2,1)S(1)}, u32[]{:S(2)}, u32[]{:S(2)}) collective-permute-start(bf16[1,8192]{1,0:T(2,128)(2,1)S(1)} %bitcast.158), channel_id=1, source_target_pairs={{0,32},{32,64},{64,96},{96,128},{128,160},{160,192},{192,224},{224... | collective-permute-start | bytes 49160 | tf_op jit(solution)/shard_map/ppermute | solution.py:17
  64.7 20.0 %copy-start.10 = (f32[16]{0:T(128)S(1)}, f32[16]{0:T(128)}, u32[]{:S(2)}) copy-start(f32[16]{0:T(128)} %param.15) | copy-start | bytes 196
  83.4 1.2 copy-start.7
  83.4 1.4 copy-start.8
  86.9 0.7 copy-start.6
  117.2 37.6 %all-to-all-start.5 = ((f32[1,512,256]{2,0,1:T(1,128)}), f32[1,512,256]{2,0,1:T(1,128)}, u32[]{:S(2)}, u32[]{:S(2)}) async-start(f32[1,512,256]{2,0,1:T(1,128)} %copy.29), calls=%async_computation.5 | async-start | bytes 1048576 | tf_op jit(solution)/shard_map/all_to_all | solution.py:72
  126.6 29.4 %collective-permute-start.4 = (bf16[1,16,8192]{2,1,0:T(8,128)(2,1)}, bf16[1,16,8192]{2,1,0:T(8,128)(2,1)}, u32[]{:S(2)}, u32[]{:S(2)}) collective-permute-start(bf16[1,16,8192]{2,1,0:T(8,128)(2,1)} %copy-done.6), channel_id=1, source_target_pairs={{32,0},{64,32},{96,64},{128,96},{160,128},{192,160},{224,192},{256... | collective-permute-start | bytes 786440 | tf_op jit(solution)/shard_map/ppermute | solution.py:17
  128.5 27.5 %collective-permute-start.3 = (bf16[1,16,8192]{2,1,0:T(8,128)(2,1)}, bf16[1,16,8192]{2,1,0:T(8,128)(2,1)}, u32[]{:S(2)}, u32[]{:S(2)}) collective-permute-start(bf16[1,16,8192]{2,1,0:T(8,128)(2,1)} %copy-done.6), channel_id=1, source_target_pairs={{0,32},{32,64},{64,96},{96,128},{128,160},{160,192},{192,224},{224... | collective-permute-start | bytes 786440 | tf_op jit(solution)/shard_map/ppermute | solution.py:17
  154.8 1.2 copy-start.9
  158.2 0.7 copy-start.4
  184.6 10.7 %copy-start.5 = (bf16[1,16,8192]{2,1,0:T(8,128)(2,1)S(1)}, bf16[1,16,8192]{2,1,0:T(8,128)(2,1)}, u32[]{:S(2)}) copy-start(bf16[1,16,8192]{2,1,0:T(8,128)(2,1)} %copy-done.4) | copy-start | bytes 786436
  187.7 37.4 %all-to-all-start.8 = ((f32[1,512,256]{2,0,1:T(1,128)}), f32[1,512,256]{2,0,1:T(1,128)}, u32[]{:S(2)}, u32[]{:S(2)}) async-start(f32[1,512,256]{2,0,1:T(1,128)} %copy.34), calls=%async_computation.8 | async-start | bytes 1048576 | tf_op jit(solution)/shard_map/all_to_all | solution.py:72
  195.4 30.8 %collective-permute-start.6 = (bf16[1,16,8192]{2,1,0:T(8,128)(2,1)S(1)}, bf16[1,16,8192]{2,1,0:T(8,128)(2,1)S(1)}, u32[]{:S(2)}, u32[]{:S(2)}) collective-permute-start(bf16[1,16,8192]{2,1,0:T(8,128)(2,1)S(1)} %copy-done.5), channel_id=1, source_target_pairs={{32,0},{64,32},{96,64},{128,96},{160,128},{192,160},{224,192},{256... | collective-permute-start | bytes 786440 | tf_op jit(solution)/shard_map/ppermute | solution.py:17
  197.3 28.9 %collective-permute-start.5 = (bf16[1,16,8192]{2,1,0:T(8,128)(2,1)S(1)}, bf16[1,16,8192]{2,1,0:T(8,128)(2,1)}, u32[]{:S(2)}, u32[]{:S(2)}) collective-permute-start(bf16[1,16,8192]{2,1,0:T(8,128)(2,1)S(1)} %copy-done.5), channel_id=1, source_target_pairs={{0,32},{32,64},{64,96},{96,128},{128,160},{160,192},{192,224},{224... | collective-permute-start | bytes 786440 | tf_op jit(solution)/shard_map/ppermute | solution.py:17
where the time goes:
time: 230 us; the launch traced here: 229 us
  blocking collectives  91.5 us (40%)
  waiting for transfers between devices  53.3 us (23%)
  starting transfers between devices  40.1 us (17%)
  local copies, waits for them, and re-layouts  24.9 us (11%)
  matrix products  10.3 us (4%)
  other arithmetic  7.54 us (3%)
    all_to_all x6, blocking collectives, turned_blocks(): lax.all_to_all(tiles, axes[k], split_axis=k, concat_axis=k, tiled=True)  91.5 us
    all_to_all x3, waiting for transfers between devices, body(): lax.all_to_all(kinetic_term, RAD, split_axis=1, concat_axis=2, tiled=True)  53.3 us
    all_to_all x3, starting transfers between devices, body(): lax.all_to_all(kinetic_term, RAD, split_axis=1, concat_axis=2, tiled=True)  23.3 us
    ppermute x7, starting transfers between devices, from_behind(): return lax.ppermute(array, axis, pairs)  16.9 us
    unnamed x35, local copies, waits for them, and re-layouts  8.34 us
    dot_general x3, matrix products, body(): jnp.einsum('kng,kag->kna', grid_values, transform, preferred_element_type...  7.66 us
    convert_element_type x4, other arithmetic, body(): rounded = current.astype(jnp.bfloat16)  6.14 us
    reshape x3, local copies, waits for them, and re-layouts, body(): angular_part.reshape(hel_rows, rad_rows, flat_width)  5.01 us
  transfers between devices with their start and end apart: 10, of which 3 were waited for; matrix products, arithmetic and copies ran while one was open for 11% of the time, Pallas kernels for 0%

commit v1 on v0

v1 whole, which is shorter than its diff:
```python
import functools

import jax
import jax.numpy as jnp
from jax import lax
from jax.experimental import pallas as pl
from jax.experimental.pallas import tpu as pltpu
from jax.sharding import PartitionSpec as P

SCALE_FACTOR = 0.35
GAIN = 2.0 * SCALE_FACTOR
F32, BF16 = jnp.float32, jnp.bfloat16


def call(kernel, outs, *args, flops=0):
    shapes = [jax.ShapeDtypeStruct(s, d) for s, d in outs]
    moved = sum(a.size * a.dtype.itemsize for a in args) + sum(s.size * s.dtype.itemsize for s in shapes)
    single = len(shapes) == 1
    return pl.pallas_call(
        kernel,
        out_shape=shapes[0] if single else shapes,
        in_specs=[pl.BlockSpec(memory_space=pltpu.VMEM)] * len(args),
        out_specs=pl.BlockSpec(memory_space=pltpu.VMEM) if single else [pl.BlockSpec(memory_space=pltpu.VMEM)] * len(shapes),
        cost_estimate=pl.CostEstimate(flops=max(flops, 8 * moved), bytes_accessed=moved, transcendentals=0),
        name=kernel.func.__name__ if isinstance(kernel, functools.partial) else kernel.__name__,
    )(*args)


def natural(quarters, piece, width):
    return slice(None), piece // quarters, pl.ds((piece % quarters) * width, width)


def pack(vib, x_ref, o_ref):
    pieces, rows, width = o_ref.shape
    for p in range(pieces):
        o_ref[p] = x_ref[natural(pieces // vib, p, width)].astype(BF16)


def angular(vib, x_ref, t_ref, v_ref, grid_ref, put):
    pieces, rows, width = x_ref.shape
    quarters = pieces // vib
    sources = [
        jnp.concatenate([x_ref[v * quarters + q] for v in range(vib)], axis=0) for q in range(quarters)
    ]
    for g in range(quarters):
        cols = pl.ds(g * width, width)
        total = jnp.zeros((vib * rows, width), F32)
        for q in range(quarters):
            total += jnp.dot(sources[q], t_ref[pl.ds(q * width, width), cols], preferred_element_type=F32)
        grid_ref[:, cols] = (total * v_ref[:, cols].astype(F32)).astype(BF16)
    for q in range(quarters):
        put(q, lax.dot_general(
            grid_ref[...], t_ref[pl.ds(q * width, width), :], (((1,), (1,)), ((), ())), preferred_element_type=F32
        ))


def first_rest(vib, x_ref, t_ref, v_ref, lo_ref, hi_ref, clo_ref, chi_ref, gw_ref, g_ref, dd_ref, old_ref, z_ref, zb_ref, grid_ref):
    pieces, rows, width = x_ref.shape
    quarters = pieces // vib

    def put(q, part):
        for v in range(vib):
            p = v * quarters + q
            mixed = clo_ref[q : q + 1] * lo_ref[p].astype(F32) + chi_ref[q : q + 1] * hi_ref[p].astype(F32)
            old = old_ref[natural(quarters, p, width)]
            z = g_ref[...] * part[v * rows : (v + 1) * rows] + gw_ref[...] * mixed - dd_ref[...] * old
            z_ref[p] = z
            zb_ref[p] = z.astype(BF16)

    angular(vib, x_ref, t_ref, v_ref, grid_ref, put)


def radial(k_ref, x, gall_ref, pieces, put):
    size = k_ref.shape[0]
    rows = size // pieces
    step = 128
    for s in range(0, size, step):
        y = jnp.dot(k_ref[s : s + step], x, preferred_element_type=F32) * gall_ref[s : s + step]
        for i in range(step // rows):
            put(s // rows + i, y[i * rows : (i + 1) * rows])


def first_radial(k_ref, x_ref, gall_ref, zb_ref, kx_ref, out_ref):
    pieces, rows, width = x_ref.shape

    def put(p, y):
        kx_ref[p] = y
        out_ref[p, :rows] = y.astype(BF16)
        out_ref[p, rows:] = zb_ref[p]

    radial(k_ref, x_ref[...].reshape(pieces * rows, width), gall_ref, pieces, put)


def second(vib, r_ref, z_ref, kx_ref, k_ref, gall_ref, t_ref, v_ref, g_ref, dd_ref, new_ref,
           x1_ref, xb_ref, cb_ref, kx1_ref, z1_ref, out_ref, grid_ref):
    pieces, rows, width = z_ref.shape
    quarters = pieces // vib
    for p in range(pieces):
        x = z_ref[p] + r_ref[p, :rows].astype(F32)
        x1_ref[p] = x
        xb_ref[p] = x.astype(BF16)
        cb_ref[p] = (r_ref[p, rows:].astype(F32) + kx_ref[p]).astype(BF16)

    def put_radial(p, y):
        kx1_ref[p] = y
        out_ref[p, :rows] = y.astype(BF16)

    radial(k_ref, cb_ref[...].reshape(pieces * rows, width), gall_ref, pieces, put_radial)

    def put(q, part):
        for v in range(vib):
            p = v * quarters + q
            z = g_ref[...] * part[v * rows : (v + 1) * rows] - dd_ref[...] * new_ref[natural(quarters, p, width)]
            z1_ref[p] = z
            out_ref[p, rows:] = z.astype(BF16)

    angular(vib, xb_ref, t_ref, v_ref, grid_ref, put)


def third(vib, r_ref, z_ref, kx_ref, lo_ref, hi_ref, clo_ref, chi_ref, gw_ref,
          clow_ref, chiw_ref, cclo_ref, cchi_ref, gwall_ref, k_ref, gall_ref, x2_ref, xb_ref, out_ref, cb_ref):
    pieces, rows, width = z_ref.shape
    quarters = pieces // vib
    for p in range(pieces):
        mixed = cclo_ref[...] * clow_ref[p].astype(F32) + cchi_ref[...] * chiw_ref[p].astype(F32)
        c = r_ref[p, rows:].astype(F32) + kx_ref[p] + gwall_ref[p * rows : (p + 1) * rows] * mixed
        cb_ref[p * rows : (p + 1) * rows] = c.astype(BF16)

    def put_radial(p, y):
        out_ref[p] = y.astype(BF16)

    radial(k_ref, cb_ref[...], gall_ref, pieces, put_radial)
    for p in range(pieces):
        q = p % quarters
        mixed = clo_ref[q : q + 1] * lo_ref[p].astype(F32) + chi_ref[q : q + 1] * hi_ref[p].astype(F32)
        x = z_ref[p] + r_ref[p, :rows].astype(F32) + gw_ref[...] * mixed
        x2_ref[natural(quarters, p, width)] = x
        xb_ref[p] = x.astype(BF16)


def last_rest(vib, x_ref, t_ref, v_ref, g_ref, dd_ref, x1_ref, z_ref, grid_ref):
    pieces, rows, width = x_ref.shape
    quarters = pieces // vib

    def put(q, part):
        for v in range(vib):
            p = v * quarters + q
            z_ref[p] = g_ref[...] * part[v * rows : (v + 1) * rows] - dd_ref[...] * x1_ref[p]

    angular(vib, x_ref, t_ref, v_ref, grid_ref, put)


def last(vib, r_ref, z_ref, lo_ref, hi_ref, clo_ref, chi_ref, gw_ref, x3_ref):
    pieces, rows, width = z_ref.shape
    quarters = pieces // vib
    for p in range(pieces):
        q = p % quarters
        mixed = clo_ref[q : q + 1] * lo_ref[p].astype(F32) + chi_ref[q : q + 1] * hi_ref[p].astype(F32)
        x3_ref[natural(quarters, p, width)] = z_ref[p] + r_ref[p].astype(F32) + gw_ref[...] * mixed


def with_grid(kernel, outs, scratch, *args, flops=0):
    return call(kernel, [*outs, *scratch], *args, flops=flops)[: len(outs)]


def exchange(blocks):
    return lax.all_to_all(blocks, "rad", 0, 0, tiled=True)


def neighbours(array):
    devices = lax.axis_size("hel")
    up = [(i, i + 1) for i in range(devices - 1)]
    return lax.ppermute(array, "hel", up), lax.ppermute(array, "hel", [(j, i) for i, j in up])


def body(older, newer, kinetic, transform, potential, coupling, radial_weight, damping):
    _, rows, vib, ang = newer.shape
    pieces = lax.axis_size("rad")
    quarters = pieces // vib
    width = ang // quarters
    size = rows * pieces
    rank = lax.axis_index("rad")
    flat = (rows * vib, ang)
    packed = (pieces, rows, width)
    double = (pieces, 2 * rows, width)
    old, new = older[0], newer[0]
    table = transform[0]
    pot = jnp.swapaxes(potential, 0, 1).reshape(flat)
    work = [(flat, BF16)]
    k_flops = 2 * size * size * width
    a_flops = 4 * flat[0] * ang * ang

    x0 = call(functools.partial(pack, vib), [(packed, BF16)], new)
    r1 = exchange(x0)
    lo, hi = neighbours(x0)
    coef = coupling.astype(F32)
    below = lax.ppermute(coupling, "hel", [(i, i + 1) for i in range(lax.axis_size("hel") - 1)]).astype(F32)
    all_damp = lax.all_gather(damping, "rad", tiled=True)

    chi, clo = coef.reshape(quarters, width), below.reshape(quarters, width)
    cchi = lax.dynamic_slice_in_dim(coef, (rank % quarters) * width, width, 1)
    cclo = lax.dynamic_slice_in_dim(below, (rank % quarters) * width, width, 1)
    weight = lax.dynamic_slice_in_dim(radial_weight, rank * rows, rows, 0)
    wide = lambda column: jnp.broadcast_to(column[:, None], (rows, width))
    g, gw, dd = wide(GAIN * damping), wide(GAIN * damping * weight), wide(damping * damping)
    gall, gwall = (GAIN * all_damp)[:, None], (GAIN * all_damp * radial_weight)[:, None]

    z0, z0b = with_grid(functools.partial(first_rest, vib), [(packed, F32), (packed, BF16)], work,
                        x0, table, pot, lo, hi, clo, chi, gw, g, dd, old, flops=a_flops)
    kx0, send = call(first_radial, [(packed, F32), (double, BF16)], kinetic, r1, gall, z0b, flops=k_flops)
    r2 = exchange(send)
    x1, x1b, c1b, kx1, z1, send = with_grid(
        functools.partial(second, vib),
        [(packed, F32), (packed, BF16), (packed, BF16), (packed, F32), (packed, F32), (double, BF16)], work,
        r2, z0, kx0, kinetic, gall, table, pot, g, dd, new, flops=a_flops + k_flops)
    r3 = exchange(send)
    lo, hi = neighbours(x1b)
    clow, chiw = neighbours(c1b)
    x2, x2b, send = with_grid(
        functools.partial(third, vib), [(old.shape, F32), (packed, BF16), (packed, BF16)], [((size, width), BF16)],
        r3, z1, kx1, lo, hi, clo, chi, gw, clow, chiw, cclo, cchi, gwall, kinetic, gall, flops=k_flops)
    r4 = exchange(send)
    lo, hi = neighbours(x2b)
    (z2,) = with_grid(functools.partial(last_rest, vib), [(packed, F32)], work, x2b, table, pot, g, dd, x1, flops=a_flops)
    x3 = call(functools.partial(last, vib), [(old.shape, F32)], r4, z2, lo, hi, clo, chi, gw)
    return x2.reshape(newer.shape), x3.reshape(newer.shape)


def solution(mesh):
    return jax.shard_map(
        body,
        mesh=mesh,
        in_specs=(
            P("hel", "rad", None, None),
            P("hel", "rad", None, None),
            P(),
            P("hel", None, None),
            P("rad", None, None),
            P("hel", None),
            P(),
            P("rad"),
        ),
        out_specs=(P("hel", "rad", None, None), P("hel", "rad", None, None)),
        check_vma=False,
    )
```

time: 230 us -> 215 us (0.935)
  waiting for transfers between devices: 53.3 us -> 22.7 us
  Pallas kernels: 0 us -> 23.9 us
  starting transfers between devices: 40.1 us -> 54 us
  local copies, waits for them, and re-layouts: 24.9 us -> 12.3 us
  matrix products: 10.3 us -> 0 us
  other arithmetic: 7.54 us -> 2.18 us
  blocking collectives: 91.5 us -> 96.6 us
    unnamed x0 -> x1, blocking collectives: none -> 60.6 us
    all_to_all x6 -> x1, blocking collectives: 91.5 us -> 36 us  [exchange(): return lax.all_to_all(blocks, 'rad', 0, 0, tiled=True)]
    all_to_all x3, waiting for transfers between devices: 53.3 us -> 13.1 us  [exchange(): return lax.all_to_all(blocks, 'rad', 0, 0, tiled=True)]
    pallas_call x0 -> x7, Pallas kernels: none -> 23.9 us  [call(): pl.pallas_call(kernel, out_shape=shapes[0] if single else shapes, in_spec...]
    dot_general x6 -> x0, matrix products: 10.3 us -> none  [the longest x3 7.66 us: body(): jnp.einsum('kng,kag->kna', grid_values, transform, preferred_element_type...]
    ppermute x7 -> x9, waiting for transfers between devices: 0.02 us -> 9.63 us  [the longest x4 8.98 us: neighbours(): lax.ppermute(array, 'hel', up)]
    ppermute x7 -> x9, starting transfers between devices: 16.9 us -> 24.4 us  [the longest x4 10.7 us: neighbours(): lax.ppermute(array, 'hel', [(j, i) for i, j in up])]
    reshape x5 -> x2, local copies, waits for them, and re-layouts: 8.08 us -> 1.21 us  [body(): chi, clo = (coef.reshape(quarters, width), below.reshape(quarters, width))]
  transfers between devices with their start and end apart: 10 -> 12, of which waited for: 3 -> 5; matrix products, arithmetic and copies ran while one was open for 11% -> 6% of each run, Pallas kernels for 0% -> 4%
where the time goes in v1:
time: 215 us; the launch traced here: 213 us
  blocking collectives  96.6 us (45%)
  starting transfers between devices  54 us (25%)
  Pallas kernels  23.9 us (11%)
  waiting for transfers between devices  22.7 us (11%)
  local copies, waits for them, and re-layouts  12.3 us (6%)
  other arithmetic  2.18 us (1%)
    unnamed x1, blocking collectives  60.6 us
    all_to_all x1, blocking collectives, exchange(): return lax.all_to_all(blocks, 'rad', 0, 0, tiled=True)  36 us
    all_to_all x3, starting transfers between devices, exchange(): return lax.all_to_all(blocks, 'rad', 0, 0, tiled=True)  29.7 us
    pallas_call x7, Pallas kernels, call(): pl.pallas_call(kernel, out_shape=shapes[0] if single else shapes, in_spec...  23.9 us
    all_to_all x3, waiting for transfers between devices, exchange(): return lax.all_to_all(blocks, 'rad', 0, 0, tiled=True)  13.1 us
    ppermute x4, starting transfers between devices, neighbours(): lax.ppermute(array, 'hel', [(j, i) for i, j in up])  10.7 us
    ppermute x4, waiting for transfers between devices, neighbours(): lax.ppermute(array, 'hel', up)  8.98 us
    ppermute x4, starting transfers between devices, neighbours(): lax.ppermute(array, 'hel', up)  8.86 us
  transfers between devices with their start and end apart: 12, of which 5 were waited for; matrix products, arithmetic and copies ran while one was open for 6% of the time, Pallas kernels for 4%

profile of v1, /device:TPU:6, one launch (start us, length us, event | category | flops | bytes accessed | tf_op | source)
XLA Modules:
  0.0 213.2 jit_solution(4496383314081103159)
XLA Ops:
  0.6 2.3 %pack.1.x_ref = bf16[32,16,256]{2,1,0:T(8,128)(2,1)} custom-call(f32[16,8,1024]{2,1,0:T(8,128)} %bitcast.16), custom_call_target="tpu_custom_call" | custom-call | flops 6291456 | bytes 786432 | tf_op jit(solution)/shard_map/pack/pallas_call | solution.py:19
  2.9 16.7 %all-to-all-start = ((bf16[32,16,256]{2,1,0:T(8,128)(2,1)}), bf16[32,16,256]{2,1,0:T(8,128)(2,1)S(1)}, u32[]{:S(2)}, u32[]{:S(2)}) async-start(bf16[32,16,256]{2,1,0:T(8,128)(2,1)} %pack.1.x_ref), calls=%async_computation | async-start | bytes 524288 | tf_op jit(solution)/shard_map/all_to_all | solution.py:167
  19.6 2.2 %collective-permute-start.1 = (bf16[32,16,256]{2,1,0:T(8,128)(2,1)}, bf16[32,16,256]{2,1,0:T(8,128)(2,1)S(1)}, u32[]{:S(2)}, u32[]{:S(2)}) collective-permute-start(bf16[32,16,256]{2,1,0:T(8,128)(2,1)} %pack.1.x_ref), channel_id=1, source_target_pairs={{32,0},{64,32},{96,64},{128,96},{160,128},{192,160},{224,192},{256... | collective-permute-start | bytes 786440 | tf_op jit(solution)/shard_map/ppermute | solution.py:173
  21.8 2.1 %collective-permute-start = (bf16[32,16,256]{2,1,0:T(8,128)(2,1)}, bf16[32,16,256]{2,1,0:T(8,128)(2,1)S(1)}, u32[]{:S(2)}, u32[]{:S(2)}) collective-permute-start(bf16[32,16,256]{2,1,0:T(8,128)(2,1)} %pack.1.x_ref), channel_id=1, source_target_pairs={{0,32},{32,64},{64,96},{96,128},{128,160},{160,192},{192,224},{224... | collective-permute-start | bytes 786440 | tf_op jit(solution)/shard_map/ppermute | solution.py:173
  23.9 4.8 %collective-permute-start.2 = (bf16[1,1024]{1,0:T(2,128)(2,1)}, bf16[1,1024]{1,0:T(2,128)(2,1)S(1)}, u32[]{:S(2)}, u32[]{:S(2)}) collective-permute-start(bf16[1,1024]{1,0:T(2,128)(2,1)} %param.13), channel_id=1, source_target_pairs={{0,32},{32,64},{64,96},{96,128},{128,160},{160,192},{192,224},{224... | collective-permute-start | bytes 6152 | tf_op jit(solution)/shard_map/ppermute | solution.py:197
  28.8 1.3 dynamic-slice
  30.7 0.9 dynamic-update-slice
  31.6 60.6 %all-reduce = f32[512]{0:T(512)S(1)} all-reduce(f32[512]{0:T(512)S(1)} %dynamic-update-slice), channel_id=1, replica_groups=mesh['hel'=16,'rad'=32] {'rad'}, use_global_device_ids=true, to_apply=%add | all-reduce | flops 512 | bytes 4096
  92.8 0.8 broadcast_multiply_fusion.1
  94.9 0.9 copy.12.gall_ref
  95.8 1.8 copy.11
  98.2 0.8 broadcast_in_dim.12.g_ref
  100.3 4.3 %first_rest.1 = (f32[32,16,256]{2,1,0:T(8,128)}, bf16[32,16,256]{2,1,0:T(8,128)(2,1)}, bf16[128,1024]{1,0:T(8,128)(2,1)}) custom-call(bf16[32,16,256]{2,1,0:T(8,128)(2,1)} %pack.1.x_ref, bf16[1024,1024]{1,0:T(8,128)(2,1)} %bitcast.10, bf16[128,1024]{1,0:T(8,128)(2,1)} %bitcast.13, bf16[32,16,256]{2,1,0:T(8,128)(2,1)} %copy-done.4, ...), custom_call_target="tpu_custom_call" | custom-call | flops 536870912 | bytes 4775936 | tf_op jit(solution)/shard_map/first_rest/pallas_call | solution.py:19
  105.3 2.6 %first_radial.1 = (f32[32,16,256]{2,1,0:T(8,128)}, bf16[32,32,256]{2,1,0:T(8,128)(2,1)}) custom-call(bf16[512,512]{1,0:T(8,128)(2,1)} %k_ref.5, bf16[32,16,256]{2,1,0:T(8,128)(2,1)} %copy-done.1, f32[512,1]{1,0:T(8,128)} %copy.12.gall_ref, bf16[32,16,256]{2,1,0:T(8,128)(2,1)} %get-tuple-element.16.zb_ref), custom_call_target="tpu_custom_call" | custom-call | flops 134217728 | bytes 2099200 | tf_op jit(solution)/shard_map/first_radial/pallas_call | solution.py:19
  107.9 36.0 %all_to_all.20.r_ref = bf16[32,32,256]{2,1,0:T(8,128)(2,1)} all-to-all(bf16[32,32,256]{2,1,0:T(8,128)(2,1)} %get-tuple-element.17), channel_id=1, replica_groups=mesh['hel'=16,'rad'=32] {'rad'}, dimensions={0} | all-to-all | bytes 1048576 | tf_op jit(solution)/shard_map/all_to_all | solution.py:167
  143.9 4.9 %second.1 = (f32[32,16,256]{2,1,0:T(8,128)}, bf16[32,16,256]{2,1,0:T(8,128)(2,1)}, bf16[32,16,256]{2,1,0:T(8,128)(2,1)}, f32[32,16,256]{2,1,0:T(8,128)}, f32[32,...) custom-call(bf16[32,32,256]{2,1,0:T(8,128)(2,1)} %all_to_all.20.r_ref, ...), custom_call_target="tpu_custom_call" | custom-call | flops 671088640 | bytes 7899136 | tf_op jit(solution)/shard_map/second/pallas_call | solution.py:19
  148.8 4.4 %all-to-all-start.2 = ((bf16[32,32,256]{2,1,0:T(8,128)(2,1)}), bf16[32,32,256]{2,1,0:T(8,128)(2,1)S(1)}, u32[]{:S(2)}, u32[]{:S(2)}) async-start(bf16[32,32,256]{2,1,0:T(8,128)(2,1)} %get-tuple-element.20), calls=%async_computation.2 | async-start | bytes 1048576 | tf_op jit(solution)/shard_map/all_to_all | solution.py:167
  153.2 1.9 collective-permute-start.4
  155.1 2.4 %collective-permute-start.3 = (bf16[32,16,256]{2,1,0:T(8,128)(2,1)}, bf16[32,16,256]{2,1,0:T(8,128)(2,1)S(1)}, u32[]{:S(2)}, u32[]{:S(2)}) collective-permute-start(bf16[32,16,256]{2,1,0:T(8,128)(2,1)} %get-tuple-element.23), channel_id=1, source_target_pairs={{0,32},{32,64},{64,96},{96,128},{128,160},{160,192},{192,224},{224... | collective-permute-start | bytes 786440 | tf_op jit(solution)/shard_map/ppermute | solution.py:173
  157.5 4.7 %collective-permute-start.6 = (bf16[32,16,256]{2,1,0:T(8,128)(2,1)}, bf16[32,16,256]{2,1,0:T(8,128)(2,1)S(1)}, u32[]{:S(2)}, u32[]{:S(2)}) collective-permute-start(bf16[32,16,256]{2,1,0:T(8,128)(2,1)} %get-tuple-element.24), channel_id=1, source_target_pairs={{32,0},{64,32},{96,64},{128,96},{160,128},{192,160},{224,192},{256... | collective-permute-start | bytes 786440 | tf_op jit(solution)/shard_map/ppermute | solution.py:173
  162.2 1.9 collective-permute-start.5
  164.2 0.9 copy.14.gwall_ref
  166.8 5.3 %collective-permute-done.5.clow_ref = bf16[32,16,256]{2,1,0:T(8,128)(2,1)S(1)} collective-permute-done((bf16[32,16,256]{2,1,0:T(8,128)(2,1)}, bf16[32,16,256]{2,1,0:T(8,128)(2,1)S(1)}, u32[]{:S(2)}, u32[]{:S(2)}) %collective-permute-start.5) | collective-permute-done | bytes 262176 | tf_op jit(solution)/shard_map/ppermute | solution.py:173
  172.1 4.2 %all-to-all-done.2.r_ref = bf16[32,32,256]{2,1,0:T(8,128)(2,1)S(1)} async-done(((bf16[32,32,256]{2,1,0:T(8,128)(2,1)}), bf16[32,32,256]{2,1,0:T(8,128)(2,1)S(1)}, u32[]{:S(2)}, u32[]{:S(2)}) %all-to-all-start.2) | async-done | bytes 524320 | tf_op jit(solution)/shard_map/all_to_all | solution.py:167
  177.1 3.7 %third.1 = (f32[16,8,1024]{2,1,0:T(8,128)}, bf16[32,16,256]{2,1,0:T(8,128)(2,1)}, bf16[32,16,256]{2,1,0:T(8,128)(2,1)}, bf16[512,256]{1,0:T(8,128)(2,1)}) custom-call(bf16[32,32,256]{2,1,0:T(8,128)(2,1)} %copy-done, f32[32,16,256]{2,1,0:T(8,128)} %get-tuple-element.21.z_ref, f32[32,16,256]{2,1,0:T(8,128)} %get-tuple-element.22.kx_ref, ...), custom_call_target="tpu_custom_call" | custom-call | flops 134217728 | bytes 4487168 | tf_op jit(solution)/shard_map/third/pallas_call | solution.py:19
  180.8 8.5 %all-to-all-start.3 = ((bf16[32,16,256]{2,1,0:T(8,128)(2,1)}), bf16[32,16,256]{2,1,0:T(8,128)(2,1)S(1)}, u32[]{:S(2)}, u32[]{:S(2)}) async-start(bf16[32,16,256]{2,1,0:T(8,128)(2,1)} %get-tuple-element.26), calls=%async_computation.3 | async-start | bytes 524288 | tf_op jit(solution)/shard_map/all_to_all | solution.py:167
  189.4 1.9 collective-permute-start.8
  191.3 2.4 %collective-permute-start.7 = (bf16[32,16,256]{2,1,0:T(8,128)(2,1)}, bf16[32,16,256]{2,1,0:T(8,128)(2,1)S(1)}, u32[]{:S(2)}, u32[]{:S(2)}) collective-permute-start(bf16[32,16,256]{2,1,0:T(8,128)(2,1)} %get-tuple-element.27.x_ref), channel_id=1, source_target_pairs={{0,32},{32,64},{64,96},{96,128},{128,160},{160,192},{192,224},{224... | collective-permute-start | bytes 786440 | tf_op jit(solution)/shard_map/ppermute | solution.py:173
  193.7 3.8 %last_rest.1 = (f32[32,16,256]{2,1,0:T(8,128)}, bf16[128,1024]{1,0:T(8,128)(2,1)}) custom-call(bf16[32,16,256]{2,1,0:T(8,128)(2,1)} %get-tuple-element.27.x_ref, bf16[1024,1024]{1,0:T(8,128)(2,1)} %bitcast.12, bf16[128,1024]{1,0:T(8,128)(2,1)} %bitcast.15, f32[16,256]{1,0:T(8,128)} %broadcast_in_dim.12.g_ref, f32[16,256]{1,0:T(8,128)} %broadcast_in_dim.13.dd_ref, ...), custom_call_target="tpu_custom_call" | custom-call | flops 536870912 | bytes 3964928 | tf_op jit(solution)/shard_map/last_rest/pallas_call | solution.py:19
  197.5 3.7 %collective-permute-done.7.lo_ref = bf16[32,16,256]{2,1,0:T(8,128)(2,1)S(1)} collective-permute-done((bf16[32,16,256]{2,1,0:T(8,128)(2,1)}, bf16[32,16,256]{2,1,0:T(8,128)(2,1)S(1)}, u32[]{:S(2)}, u32[]{:S(2)}) %collective-permute-start.7) | collective-permute-done | bytes 262176 | tf_op jit(solution)/shard_map/ppermute | solution.py:173
  201.2 8.9 %all-to-all-done.3.r_ref = bf16[32,16,256]{2,1,0:T(8,128)(2,1)S(1)} async-done(((bf16[32,16,256]{2,1,0:T(8,128)(2,1)}), bf16[32,16,256]{2,1,0:T(8,128)(2,1)S(1)}, u32[]{:S(2)}, u32[]{:S(2)}) %all-to-all-start.3) | async-done | bytes 262176 | tf_op jit(solution)/shard_map/all_to_all | solution.py:167
  210.8 2.4 %last.1 = f32[16,8,1024]{2,1,0:T(8,128)} custom-call(bf16[32,16,256]{2,1,0:T(8,128)(2,1)} %copy-done.2, f32[32,16,256]{2,1,0:T(8,128)} %get-tuple-element.29.z_ref, bf16[32,16,256]{2,1,0:T(8,128)(2,1)} %copy-done.10, bf16[32,16,256]{2,1,0:T(8,128)(2,1)} %copy-done.9, f32[4,256]{1,0:T(4,128)} %reshape.23.clo_ref, f32[4,256]{1,0:T(4,128)} %reshape.24.chi_ref, ...), custom_call_target="tpu_custom_call" | custom-call | flops 14876672 | bytes 1859584 | tf_op jit(solution)/shard_map/last/pallas_call | solution.py:19
  (44 shorter events, 8.0 us)
Async XLA Ops:
  2.9 101.7 %all-to-all-start = ((bf16[32,16,256]{2,1,0:T(8,128)(2,1)}), bf16[32,16,256]{2,1,0:T(8,128)(2,1)S(1)}, u32[]{:S(2)}, u32[]{:S(2)}) async-start(bf16[32,16,256]{2,1,0:T(8,128)(2,1)} %pack.1.x_ref), calls=%async_computation | async-start | bytes 524288 | tf_op jit(solution)/shard_map/all_to_all | solution.py:167
  19.6 78.6 %collective-permute-start.1 = (bf16[32,16,256]{2,1,0:T(8,128)(2,1)}, bf16[32,16,256]{2,1,0:T(8,128)(2,1)S(1)}, u32[]{:S(2)}, u32[]{:S(2)}) collective-permute-start(bf16[32,16,256]{2,1,0:T(8,128)(2,1)} %pack.1.x_ref), channel_id=1, source_target_pairs={{32,0},{64,32},{96,64},{128,96},{160,128},{192,160},{224,192},{256... | collective-permute-start | bytes 786440 | tf_op jit(solution)/shard_map/ppermute | solution.py:173
  21.8 76.4 %collective-permute-start = (bf16[32,16,256]{2,1,0:T(8,128)(2,1)}, bf16[32,16,256]{2,1,0:T(8,128)(2,1)S(1)}, u32[]{:S(2)}, u32[]{:S(2)}) collective-permute-start(bf16[32,16,256]{2,1,0:T(8,128)(2,1)} %pack.1.x_ref), channel_id=1, source_target_pairs={{0,32},{32,64},{64,96},{96,128},{128,160},{160,192},{192,224},{224... | collective-permute-start | bytes 786440 | tf_op jit(solution)/shard_map/ppermute | solution.py:173
  23.9 73.6 %collective-permute-start.2 = (bf16[1,1024]{1,0:T(2,128)(2,1)}, bf16[1,1024]{1,0:T(2,128)(2,1)S(1)}, u32[]{:S(2)}, u32[]{:S(2)}) collective-permute-start(bf16[1,1024]{1,0:T(2,128)(2,1)} %param.13), channel_id=1, source_target_pairs={{0,32},{32,64},{64,96},{96,128},{128,160},{160,192},{192,224},{224... | collective-permute-start | bytes 6152 | tf_op jit(solution)/shard_map/ppermute | solution.py:197
  98.2 2.1 copy-start.3
  98.2 2.1 copy-start.4
  104.6 0.7 copy-start.1
  143.9 20.2 %copy-start.11 = (bf16[1,1024]{1,0:T(2,128)(2,1)S(1)}, bf16[1,1024]{1,0:T(2,128)(2,1)}, u32[]{:S(2)}) copy-start(bf16[1,1024]{1,0:T(2,128)(2,1)} %param.13) | copy-start | bytes 6148
  148.8 27.5 %all-to-all-start.2 = ((bf16[32,32,256]{2,1,0:T(8,128)(2,1)}), bf16[32,32,256]{2,1,0:T(8,128)(2,1)S(1)}, u32[]{:S(2)}, u32[]{:S(2)}) async-start(bf16[32,32,256]{2,1,0:T(8,128)(2,1)} %get-tuple-element.20), calls=%async_computation.2 | async-start | bytes 1048576 | tf_op jit(solution)/shard_map/all_to_all | solution.py:167
  153.2 13.0 %collective-permute-start.4 = (bf16[32,16,256]{2,1,0:T(8,128)(2,1)}, bf16[32,16,256]{2,1,0:T(8,128)(2,1)S(1)}, u32[]{:S(2)}, u32[]{:S(2)}) collective-permute-start(bf16[32,16,256]{2,1,0:T(8,128)(2,1)} %get-tuple-element.23), channel_id=1, source_target_pairs={{32,0},{64,32},{96,64},{128,96},{160,128},{192,160},{224,192},{256... | collective-permute-start | bytes 786440 | tf_op jit(solution)/shard_map/ppermute | solution.py:173
  155.1 11.1 %collective-permute-start.3 = (bf16[32,16,256]{2,1,0:T(8,128)(2,1)}, bf16[32,16,256]{2,1,0:T(8,128)(2,1)S(1)}, u32[]{:S(2)}, u32[]{:S(2)}) collective-permute-start(bf16[32,16,256]{2,1,0:T(8,128)(2,1)} %get-tuple-element.23), channel_id=1, source_target_pairs={{0,32},{32,64},{64,96},{96,128},{128,160},{160,192},{192,224},{224... | collective-permute-start | bytes 786440 | tf_op jit(solution)/shard_map/ppermute | solution.py:173
  157.5 9.3 %collective-permute-start.6 = (bf16[32,16,256]{2,1,0:T(8,128)(2,1)}, bf16[32,16,256]{2,1,0:T(8,128)(2,1)S(1)}, u32[]{:S(2)}, u32[]{:S(2)}) collective-permute-start(bf16[32,16,256]{2,1,0:T(8,128)(2,1)} %get-tuple-element.24), channel_id=1, source_target_pairs={{32,0},{64,32},{96,64},{128,96},{160,128},{192,160},{224,192},{256... | collective-permute-start | bytes 786440 | tf_op jit(solution)/shard_map/ppermute | solution.py:173
  162.2 9.9 %collective-permute-start.5 = (bf16[32,16,256]{2,1,0:T(8,128)(2,1)}, bf16[32,16,256]{2,1,0:T(8,128)(2,1)S(1)}, u32[]{:S(2)}, u32[]{:S(2)}) collective-permute-start(bf16[32,16,256]{2,1,0:T(8,128)(2,1)} %get-tuple-element.24), channel_id=1, source_target_pairs={{0,32},{32,64},{64,96},{96,128},{128,160},{160,192},{192,224},{224... | collective-permute-start | bytes 786440 | tf_op jit(solution)/shard_map/ppermute | solution.py:173
  166.2 10.1 %copy-start.5 = (bf16[32,16,256]{2,1,0:T(8,128)(2,1)}, bf16[32,16,256]{2,1,0:T(8,128)(2,1)S(1)}, u32[]{:S(2)}) copy-start(bf16[32,16,256]{2,1,0:T(8,128)(2,1)S(1)} %collective-permute-done.4.hi_ref) | copy-start | bytes 786436
  166.2 10.1 %copy-start.6 = (bf16[32,16,256]{2,1,0:T(8,128)(2,1)}, bf16[32,16,256]{2,1,0:T(8,128)(2,1)S(1)}, u32[]{:S(2)}) copy-start(bf16[32,16,256]{2,1,0:T(8,128)(2,1)S(1)} %collective-permute-done.3.lo_ref) | copy-start | bytes 786436
  166.8 9.5 %copy-start.7 = (bf16[32,16,256]{2,1,0:T(8,128)(2,1)}, bf16[32,16,256]{2,1,0:T(8,128)(2,1)S(1)}, u32[]{:S(2)}) copy-start(bf16[32,16,256]{2,1,0:T(8,128)(2,1)S(1)} %collective-permute-done.6.chiw_ref) | copy-start | bytes 786436
  172.1 4.2 %copy-start.8 = (bf16[32,16,256]{2,1,0:T(8,128)(2,1)}, bf16[32,16,256]{2,1,0:T(8,128)(2,1)S(1)}, u32[]{:S(2)}) copy-start(bf16[32,16,256]{2,1,0:T(8,128)(2,1)S(1)} %collective-permute-done.5.clow_ref) | copy-start | bytes 786436
  176.3 0.8 copy-start
  180.8 29.3 %all-to-all-start.3 = ((bf16[32,16,256]{2,1,0:T(8,128)(2,1)}), bf16[32,16,256]{2,1,0:T(8,128)(2,1)S(1)}, u32[]{:S(2)}, u32[]{:S(2)}) async-start(bf16[32,16,256]{2,1,0:T(8,128)(2,1)} %get-tuple-element.26), calls=%async_computation.3 | async-start | bytes 524288 | tf_op jit(solution)/shard_map/all_to_all | solution.py:167
  189.4 8.1 %collective-permute-start.8 = (bf16[32,16,256]{2,1,0:T(8,128)(2,1)}, bf16[32,16,256]{2,1,0:T(8,128)(2,1)S(1)}, u32[]{:S(2)}, u32[]{:S(2)}) collective-permute-start(bf16[32,16,256]{2,1,0:T(8,128)(2,1)} %get-tuple-element.27.x_ref), channel_id=1, source_target_pairs={{32,0},{64,32},{96,64},{128,96},{160,128},{192,160},{224,192},{256... | collective-permute-start | bytes 786440 | tf_op jit(solution)/shard_map/ppermute | solution.py:173
  191.3 9.9 %collective-permute-start.7 = (bf16[32,16,256]{2,1,0:T(8,128)(2,1)}, bf16[32,16,256]{2,1,0:T(8,128)(2,1)S(1)}, u32[]{:S(2)}, u32[]{:S(2)}) collective-permute-start(bf16[32,16,256]{2,1,0:T(8,128)(2,1)} %get-tuple-element.27.x_ref), channel_id=1, source_target_pairs={{0,32},{32,64},{64,96},{96,128},{128,160},{160,192},{192,224},{224... | collective-permute-start | bytes 786440 | tf_op jit(solution)/shard_map/ppermute | solution.py:173
  197.5 12.6 %copy-start.9 = (bf16[32,16,256]{2,1,0:T(8,128)(2,1)}, bf16[32,16,256]{2,1,0:T(8,128)(2,1)S(1)}, u32[]{:S(2)}) copy-start(bf16[32,16,256]{2,1,0:T(8,128)(2,1)S(1)} %collective-permute-done.8.hi_ref) | copy-start | bytes 786436
  201.2 8.9 %copy-start.10 = (bf16[32,16,256]{2,1,0:T(8,128)(2,1)}, bf16[32,16,256]{2,1,0:T(8,128)(2,1)S(1)}, u32[]{:S(2)}) copy-start(bf16[32,16,256]{2,1,0:T(8,128)(2,1)S(1)} %collective-permute-done.7.lo_ref) | copy-start | bytes 786436
  210.1 0.7 copy-start.2

commit v2 on v1

v2 whole, which is shorter than its diff:
```python
import functools

import jax
import jax.numpy as jnp
from jax import lax
from jax.experimental import pallas as pl
from jax.experimental.pallas import tpu as pltpu
from jax.sharding import PartitionSpec as P

SCALE_FACTOR = 0.35
GAIN = 2.0 * SCALE_FACTOR
F32, BF16 = jnp.float32, jnp.bfloat16


def call(kernel, outs, *args, flops=0, scalars=(), room=()):
    shapes = [jax.ShapeDtypeStruct(s, d) for s, d in outs]
    moved = sum(a.size * a.dtype.itemsize for a in args) + sum(s.size * s.dtype.itemsize for s in shapes)
    vmem = pl.BlockSpec(memory_space=pltpu.VMEM)
    return pl.pallas_call(
        kernel,
        out_shape=shapes,
        in_specs=[pl.BlockSpec(memory_space=pltpu.SMEM)] * len(scalars) + [vmem] * len(args),
        out_specs=[vmem] * len(shapes),
        scratch_shapes=[pltpu.VMEM(s, d) for s, d in room],
        cost_estimate=pl.CostEstimate(flops=max(flops, 8 * moved), bytes_accessed=moved, transcendentals=0),
        name=kernel.func.__name__,
    )(*scalars, *args)


def natural(quarters, piece, width):
    return slice(None), piece // quarters, pl.ds((piece % quarters) * width, width)


def column(values, shape):
    row = lax.broadcasted_iota(jnp.int32, shape, 0)
    out = jnp.full(shape, values[0], F32)
    for i, value in enumerate(values[1:], 1):
        out = jnp.where(row == i, value, out)
    return out


def own_columns(rows, width, rank_ref, d_ref, w_ref):
    damp = [d_ref[i] for i in range(rows)]
    weight = [w_ref[rank_ref[0] * rows + i] for i in range(rows)]
    d = column(damp, (rows, width))
    return GAIN * d, GAIN * d * column(weight, (rows, width)), d * d


def pack(vib, d_ref, x_ref, c_ref, sent_ref, x0_ref):
    pieces, rows, width = x0_ref.shape
    pieces -= 1
    quarters, half = pieces // vib, width // 2
    for p in range(pieces):
        x = x_ref[natural(quarters, p, width)].astype(BF16)
        x0_ref[p] = x
        sent_ref[p, :rows] = x[:, :half]
        sent_ref[p, rows : 2 * rows] = x[:, half:]
    c = c_ref[...].astype(F32)
    x0_ref[pieces] = column([c[:, q * width : (q + 1) * width] for q in range(quarters)], (rows, width)).astype(BF16)
    tile = (rows // 2, half)
    lane = lax.broadcasted_iota(jnp.int32, tile, 1)
    fine = [column([d_ref[h * rows // 2 + i] for i in range(rows // 2)], tile) for h in range(2)]
    high = [f.astype(BF16).astype(F32) for f in fine]
    low = [f - h for f, h in zip(fine, high)]
    mixed = jnp.where(lane < half // 2, jnp.where(lane < half // 4, high[0], low[0]), jnp.where(lane < 3 * half // 4, high[1], low[1]))
    for p in range(pieces):
        sent_ref[p, 2 * rows :] = mixed.astype(BF16)


def angular(vib, x_ref, t_ref, v_ref, grid_ref, put):
    rows, width = x_ref.shape[1:]
    quarters = t_ref.shape[0] // width
    sources = [
        jnp.concatenate([x_ref[v * quarters + q] for v in range(vib)], axis=0) for q in range(quarters)
    ]
    for g in range(quarters):
        cols = pl.ds(g * width, width)
        total = jnp.zeros((vib * rows, width), F32)
        for q in range(quarters):
            total += jnp.dot(sources[q], t_ref[pl.ds(q * width, width), cols], preferred_element_type=F32)
        grid_ref[:, cols] = (total * v_ref[:, cols].astype(F32)).astype(BF16)
    for q in range(quarters):
        put(q, lax.dot_general(
            grid_ref[...], t_ref[pl.ds(q * width, width), :], (((1,), (1,)), ((), ())), preferred_element_type=F32
        ))


def mixer(lo_ref, hi_ref, below_ref, c_ref, rows, width):
    pieces = lo_ref.shape[0]
    quarters = c_ref.shape[1] // width
    clo = below_ref[below_ref.shape[0] - 1].astype(F32)
    below = [jnp.broadcast_to(clo[q : q + 1], (rows, width)) for q in range(quarters)]
    own = [jnp.broadcast_to(c_ref[:, q * width : (q + 1) * width].astype(F32), (rows, width)) for q in range(quarters)]

    def mixed(p, q=None, lo=lo_ref, hi=hi_ref):
        q = p % quarters if q is None else q
        if isinstance(q, int):
            return below[q] * lo[p].astype(F32) + own[q] * hi[p].astype(F32)
        under, over = below[0], own[0]
        for i in range(1, quarters):
            under, over = jnp.where(q == i, below[i], under), jnp.where(q == i, own[i], over)
        return under * lo[p].astype(F32) + over * hi[p].astype(F32)

    return mixed


def first_rest(vib, rank_ref, d_ref, w_ref, x_ref, t_ref, v_ref, lo_ref, hi_ref, c_ref, old_ref, z_ref, zb_ref, wall_ref, grid_ref):
    pieces, rows, width = z_ref.shape
    quarters = pieces // vib
    g, gw, dd = own_columns(rows, width, rank_ref, d_ref, w_ref)
    mixed = mixer(lo_ref, hi_ref, lo_ref, c_ref, rows, width)
    for p in range(pieces):
        wall_ref[p] = column([w_ref[p * rows + i] for i in range(rows)], wall_ref.shape[1:])

    def put(q, part):
        for v in range(vib):
            p = v * quarters + q
            z = g * part[v * rows : (v + 1) * rows] + gw * mixed(p) - dd * old_ref[natural(quarters, p, width)]
            z_ref[p] = z
            zb_ref[p] = z.astype(BF16)

    angular(vib, x_ref, t_ref, v_ref, grid_ref, put)


def radial(k_ref, x, gall_ref, put):
    pieces, rows, _ = gall_ref.shape
    step = 128 // rows
    for s in range(0, pieces, step):
        y = jnp.dot(k_ref[s * rows : (s + step) * rows], x, preferred_element_type=F32)
        for i in range(step):
            g = gall_ref[s + i]
            put(s + i, y[i * rows : (i + 1) * rows] * jnp.concatenate([g, g], axis=1))


def first_radial(k_ref, r_ref, zb_ref, kx_ref, gall_ref, out_ref, x_ref):
    pieces, rows, width = zb_ref.shape
    half = width // 2
    for p in range(pieces):
        at = slice(p * rows, (p + 1) * rows)
        x_ref[at, :half] = r_ref[p, :rows]
        x_ref[at, half:] = r_ref[p, rows : 2 * rows]
        tile = r_ref[p, 2 * rows :].astype(F32)
        for h in range(2):
            lane = h * half // 2
            d = tile[:, lane : lane + 1] + tile[:, lane + half // 4 : lane + half // 4 + 1]
            gall_ref[p, h * rows // 2 : (h + 1) * rows // 2] = jnp.broadcast_to(GAIN * d, (rows // 2, half))

    def put(p, y):
        kx_ref[p] = y
        out_ref[p, :rows] = y.astype(BF16)
        out_ref[p, rows:] = zb_ref[p]

    radial(k_ref, x_ref[...], gall_ref, put)


def second(vib, rank_ref, d_ref, w_ref, r_ref, z_ref, kx_ref, k_ref, gall_ref, t_ref, v_ref, new_ref,
           x1_ref, xb_ref, cb_ref, kx1_ref, z1_ref, out_ref, grid_ref):
    pieces, rows, width = z_ref.shape
    quarters = pieces // vib
    g, _, dd = own_columns(rows, width, rank_ref, d_ref, w_ref)
    for p in range(pieces):
        x = z_ref[p] + r_ref[p, :rows].astype(F32)
        x1_ref[p] = x
        xb_ref[p] = x.astype(BF16)
        cb_ref[p] = (r_ref[p, rows:].astype(F32) + kx_ref[p]).astype(BF16)

    def put_radial(p, y):
        kx1_ref[p] = y
        out_ref[p, :rows] = y.astype(BF16)

    radial(k_ref, cb_ref[...].reshape(pieces * rows, width), gall_ref, put_radial)

    def put(q, part):
        for v in range(vib):
            p = v * quarters + q
            z = g * part[v * rows : (v + 1) * rows] - dd * new_ref[natural(quarters, p, width)]
            z1_ref[p] = z
            out_ref[p, rows:] = z.astype(BF16)

    angular(vib, xb_ref, t_ref, v_ref, grid_ref, put)


def third(vib, rank_ref, d_ref, w_ref, r_ref, z_ref, kx_ref, lo_ref, hi_ref, low_ref, hiw_ref, below_ref, c_ref,
          wall_ref, k_ref, gall_ref, x2_ref, xb_ref, out_ref, cb_ref):
    pieces, rows, width = z_ref.shape
    quarters = pieces // vib
    _, gw, _ = own_columns(rows, width, rank_ref, d_ref, w_ref)
    mixed = mixer(lo_ref, hi_ref, below_ref, c_ref, rows, width)
    own = lax.rem(rank_ref[0], quarters)
    for p in range(pieces):
        gwall = gall_ref[p] * wall_ref[p]
        gwall = jnp.concatenate([gwall, gwall], axis=1)
        c = r_ref[p, rows:].astype(F32) + kx_ref[p] + gwall * mixed(p, own, low_ref, hiw_ref)
        cb_ref[p * rows : (p + 1) * rows] = c.astype(BF16)

    def put_radial(p, y):
        out_ref[p] = y.astype(BF16)

    radial(k_ref, cb_ref[...], gall_ref, put_radial)
    for p in range(pieces):
        x = z_ref[p] + r_ref[p, :rows].astype(F32) + gw * mixed(p)
        x2_ref[natural(quarters, p, width)] = x
        xb_ref[p] = x.astype(BF16)


def last_rest(vib, rank_ref, d_ref, w_ref, x_ref, t_ref, v_ref, x1_ref, z_ref, grid_ref):
    pieces, rows, width = x_ref.shape
    quarters = pieces // vib
    g, _, dd = own_columns(rows, width, rank_ref, d_ref, w_ref)

    def put(q, part):
        for v in range(vib):
            p = v * quarters + q
            z_ref[p] = g * part[v * rows : (v + 1) * rows] - dd * x1_ref[p]

    angular(vib, x_ref, t_ref, v_ref, grid_ref, put)


def last(vib, rank_ref, d_ref, w_ref, r_ref, z_ref, lo_ref, hi_ref, below_ref, c_ref, x3_ref):
    pieces, rows, width = z_ref.shape
    quarters = pieces // vib
    _, gw, _ = own_columns(rows, width, rank_ref, d_ref, w_ref)
    mixed = mixer(lo_ref, hi_ref, below_ref, c_ref, rows, width)
    for p in range(pieces):
        x3_ref[natural(quarters, p, width)] = z_ref[p] + r_ref[p].astype(F32) + gw * mixed(p)


def exchange(blocks):
    return lax.all_to_all(blocks, "rad", 0, 0, tiled=True)


def neighbours(array):
    devices = lax.axis_size("hel")
    up = [(i, i + 1) for i in range(devices - 1)]
    return lax.ppermute(array, "hel", up), lax.ppermute(array, "hel", [(j, i) for i, j in up])


def body(older, newer, kinetic, transform, potential, coupling, radial_weight, damping):
    _, rows, vib, ang = newer.shape
    pieces = lax.axis_size("rad")
    width = ang // (pieces // vib)
    size = rows * pieces
    flat = (rows * vib, ang)
    packed, double = (pieces, rows, width), (pieces, 2 * rows, width)
    old, new = older[0], newer[0]
    table = transform[0]
    pot = jnp.swapaxes(potential, 0, 1).reshape(flat)
    own = (lax.axis_index("rad").astype(jnp.int32).reshape(1), damping, radial_weight)
    grid = (flat, BF16)
    k_flops = 2 * size * size * width
    a_flops = 4 * flat[0] * ang * ang
    part = lambda kernel: functools.partial(kernel, vib)

    sent, x0 = call(
        part(pack), [((pieces, 5 * rows // 2, width // 2), BF16), ((pieces + 1, rows, width), BF16)],
        new, coupling, scalars=(damping,))
    r1 = exchange(sent)
    lo, hi = neighbours(x0)
    below = lo
    z0, z0b, wall = call(
        part(first_rest), [(packed, F32), (packed, BF16), ((pieces, rows, width // 2), F32)],
        x0, table, pot, lo, hi, coupling, old, scalars=own, room=[grid], flops=a_flops)
    kx0, gall, sent = call(
        functools.partial(first_radial), [(packed, F32), ((pieces, rows, width // 2), F32), (double, BF16)],
        kinetic, r1, z0b, room=[((size, width), BF16)], flops=k_flops)
    r2 = exchange(sent)
    x1, x1b, c1b, kx1, z1, sent = call(
        part(second), [(packed, F32), (packed, BF16), (packed, BF16), (packed, F32), (packed, F32), (double, BF16)],
        r2, z0, kx0, kinetic, gall, table, pot, new, scalars=own, room=[grid], flops=a_flops + k_flops)
    r3 = exchange(sent)
    lo, hi = neighbours(x1b)
    low, hiw = neighbours(c1b)
    x2, x2b, sent = call(
        part(third), [(old.shape, F32), (packed, BF16), (packed, BF16)],
        r3, z1, kx1, lo, hi, low, hiw, below, coupling, wall, kinetic, gall,
        scalars=own, room=[((size, width), BF16)], flops=k_flops)
    r4 = exchange(sent)
    lo, hi = neighbours(x2b)
    (z2,) = call(part(last_rest), [(packed, F32)], x2b, table, pot, x1, scalars=own, room=[grid], flops=a_flops)
    (x3,) = call(part(last), [(old.shape, F32)], r4, z2, lo, hi, below, coupling, scalars=own)
    return x2.reshape(newer.shape), x3.reshape(newer.shape)


def solution(mesh):
    return jax.shard_map(
        body,
        mesh=mesh,
        in_specs=(
            P("hel", "rad", None, None),
            P("hel", "rad", None, None),
            P(),
            P("hel", None, None),
            P("rad", None, None),
            P("hel", None),
            P(),
            P("rad"),
        ),
        out_specs=(P("hel", "rad", None, None), P("hel", "rad", None, None)),
        check_vma=False,
    )
```

time: 215 us -> 160 us (0.74)
  blocking collectives: 96.6 us -> 38.7 us
  waiting for transfers between devices: 22.7 us -> 46.6 us
  starting transfers between devices: 54 us -> 44.4 us
  local copies, waits for them, and re-layouts: 12.3 us -> 4.76 us
  other arithmetic: 2.18 us -> 0 us
    unnamed x1 -> x0, blocking collectives: 60.6 us -> none
    all_to_all x3, waiting for transfers between devices: 13.1 us -> 27.7 us  [exchange(): return lax.all_to_all(blocks, 'rad', 0, 0, tiled=True)]
    ppermute x4, waiting for transfers between devices: 8.98 us -> 15.7 us  [neighbours(): lax.ppermute(array, 'hel', up)]
    ppermute x1 -> x0, starting transfers between devices: 4.82 us -> none  [body(): lax.ppermute(coupling, 'hel', [(i, i + 1) for i in range(lax.axis_size('h...]
    all_to_all x3, starting transfers between devices: 29.7 us -> 24.9 us  [exchange(): return lax.all_to_all(blocks, 'rad', 0, 0, tiled=True)]
    broadcast_in_dim x5 -> x0, local copies, waits for them, and re-layouts: 3.83 us -> none  [the longest x3 2.11 us: body(): wide = lambda column: jnp.broadcast_to(column[:, None], (rows, width))]
    all_to_all x1, blocking collectives: 36 us -> 38.7 us  [exchange(): return lax.all_to_all(blocks, 'rad', 0, 0, tiled=True)]
    ppermute x4, waiting for transfers between devices: 0.64 us -> 3.16 us  [neighbours(): lax.ppermute(array, 'hel', [(j, i) for i, j in up])]
  transfers between devices with their start and end apart: 12 -> 11, of which waited for: 5 -> 9; matrix products, arithmetic and copies ran while one was open for 6% -> 1% of each run, Pallas kernels for 4% -> 5%
where the time goes in v2:
time: 160 us; the launch traced here: 159 us
  waiting for transfers between devices  46.6 us (29%)
  starting transfers between devices  44.4 us (28%)
  blocking collectives  38.7 us (24%)
  Pallas kernels  24.1 us (15%)
  local copies, waits for them, and re-layouts  4.76 us (3%)
    all_to_all x1, blocking collectives, exchange(): return lax.all_to_all(blocks, 'rad', 0, 0, tiled=True)  38.7 us
    all_to_all x3, waiting for transfers between devices, exchange(): return lax.all_to_all(blocks, 'rad', 0, 0, tiled=True)  27.7 us
    all_to_all x3, starting transfers between devices, exchange(): return lax.all_to_all(blocks, 'rad', 0, 0, tiled=True)  24.9 us
    pallas_call x7, Pallas kernels, call(): pl.pallas_call(kernel, out_shape=shapes, in_specs=[pl.BlockSpec(memory_sp...  24.1 us
    ppermute x4, waiting for transfers between devices, neighbours(): lax.ppermute(array, 'hel', up)  15.7 us
    ppermute x4, starting transfers between devices, neighbours(): lax.ppermute(array, 'hel', [(j, i) for i, j in up])  10.7 us
    ppermute x4, starting transfers between devices, neighbours(): lax.ppermute(array, 'hel', up)  8.86 us
  transfers between devices with their start and end apart: 11, of which 9 were waited for; matrix products, arithmetic and copies ran while one was open for 1% of the time, Pallas kernels for 5%

profile of v2, /device:TPU:6, one launch (start us, length us, event | category | flops | bytes accessed | tf_op | source)
XLA Modules:
  0.0 159.3 jit_solution(13729854219757772116)
XLA Ops:
  0.6 2.4 %pack.1 = (bf16[32,40,128]{2,1,0:T(8,128)(2,1)}, bf16[33,16,256]{2,1,0:T(8,128)(2,1)}) custom-call(f32[16]{0:T(128)} %d_ref.11, f32[16,8,1024]{2,1,0:T(8,128)} %bitcast.14, bf16[1,1024]{1,0:T(2,128)(2,1)} %c_ref.7), custom_call_target="tpu_custom_call" | custom-call | flops 8994816 | bytes 1124352 | tf_op jit(solution)/shard_map/pack/pallas_call | solution.py:19
  3.0 16.7 %all-to-all-start = ((bf16[32,40,128]{2,1,0:T(8,128)(2,1)}), bf16[32,40,128]{2,1,0:T(8,128)(2,1)S(1)}, u32[]{:S(2)}, u32[]{:S(2)}) async-start(bf16[32,40,128]{2,1,0:T(8,128)(2,1)} %get-tuple-element.19), calls=%async_computation | async-start | bytes 655360 | tf_op jit(solution)/shard_map/all_to_all | solution.py:229
  19.8 2.2 %collective-permute-start.1 = (bf16[33,16,256]{2,1,0:T(8,128)(2,1)}, bf16[33,16,256]{2,1,0:T(8,128)(2,1)S(1)}, u32[]{:S(2)}, u32[]{:S(2)}) collective-permute-start(bf16[33,16,256]{2,1,0:T(8,128)(2,1)} %get-tuple-element.20.x_ref), channel_id=1, source_target_pairs={{32,0},{64,32},{96,64},{128,96},{160,128},{192,160},{224,192},{256... | collective-permute-start | bytes 811016 | tf_op jit(solution)/shard_map/ppermute | solution.py:235
  22.0 2.1 %collective-permute-start = (bf16[33,16,256]{2,1,0:T(8,128)(2,1)}, bf16[33,16,256]{2,1,0:T(8,128)(2,1)S(1)}, u32[]{:S(2)}, u32[]{:S(2)}) collective-permute-start(bf16[33,16,256]{2,1,0:T(8,128)(2,1)} %get-tuple-element.20.x_ref), channel_id=1, source_target_pairs={{0,32},{32,64},{64,96},{96,128},{128,160},{160,192},{192,224},{224... | collective-permute-start | bytes 811016 | tf_op jit(solution)/shard_map/ppermute | solution.py:235
  24.1 1.8 %copy.10 = bf16[8,16,1024]{2,1,0:T(8,128)(2,1)} copy(bf16[8,16,1024]{2,0,1:T(8,128)(2,1)} %bitcast.18) | data formatting | bytes 524288 | tf_op jit(solution)/shard_map/transpose | solution.py:247
  26.5 6.2 %collective-permute-done.lo_ref.below_ref = bf16[33,16,256]{2,1,0:T(8,128)(2,1)S(1)} collective-permute-done((bf16[33,16,256]{2,1,0:T(8,128)(2,1)}, bf16[33,16,256]{2,1,0:T(8,128)(2,1)S(1)}, u32[]{:S(2)}, u32[]{:S(2)}) %collective-permute-start) | collective-permute-done | bytes 270368 | tf_op jit(solution)/shard_map/ppermute | solution.py:235
  32.7 0.7 copy-done
  33.4 4.3 %first_rest.1 = (f32[32,16,256]{2,1,0:T(8,128)}, bf16[32,16,256]{2,1,0:T(8,128)(2,1)}, f32[32,16,128]{2,1,0:T(8,128)}) custom-call(s32[1]{0:T(128)} %bitcast.rank_ref, f32[16]{0:T(128)} %d_ref.11, f32[512]{0:T(512)} %w_ref.9, bf16[33,16,256]{2,1,0:T(8,128)(2,1)} %get-tuple-element.20.x_ref, bf16[1024,1024]{1,0:T(8,128)(2,1)} %bitcast.8, ...), custom_call_target="tpu_custom_call" | custom-call | flops 536870912 | bytes 4745216 | tf_op jit(solution)/shard_map/first_rest/pallas_call | solution.py:19
  37.7 6.4 %all-to-all-done.r_ref = bf16[32,40,128]{2,1,0:T(8,128)(2,1)S(1)} async-done(((bf16[32,40,128]{2,1,0:T(8,128)(2,1)}), bf16[32,40,128]{2,1,0:T(8,128)(2,1)S(1)}, u32[]{:S(2)}, u32[]{:S(2)}) %all-to-all-start) | async-done | bytes 327712 | tf_op jit(solution)/shard_map/all_to_all | solution.py:229
  44.1 0.7 copy-done.2
  44.8 2.6 %first_radial.1 = (f32[32,16,256]{2,1,0:T(8,128)}, f32[32,16,128]{2,1,0:T(8,128)}, bf16[32,32,256]{2,1,0:T(8,128)(2,1)}) custom-call(bf16[512,512]{1,0:T(8,128)(2,1)} %k_ref.5, bf16[32,40,128]{2,1,0:T(8,128)(2,1)} %copy-done.2, bf16[32,16,256]{2,1,0:T(8,128)(2,1)} %get-tuple-element.21.zb_ref), custom_call_target="tpu_custom_call" | custom-call | flops 134217728 | bytes 2424832 | tf_op jit(solution)/shard_map/first_radial/pallas_call | solution.py:19
  47.4 38.7 %all_to_all.20.r_ref = bf16[32,32,256]{2,1,0:T(8,128)(2,1)} all-to-all(bf16[32,32,256]{2,1,0:T(8,128)(2,1)} %get-tuple-element.22), channel_id=1, replica_groups=mesh['hel'=16,'rad'=32] {'rad'}, dimensions={0} | all-to-all | bytes 1048576 | tf_op jit(solution)/shard_map/all_to_all | solution.py:229
  86.1 4.7 %second.1 = (f32[32,16,256]{2,1,0:T(8,128)}, bf16[32,16,256]{2,1,0:T(8,128)(2,1)}, bf16[32,16,256]{2,1,0:T(8,128)(2,1)}, f32[32,16,256]{2,1,0:T(8,128)}, f32[32,...) custom-call(s32[1]{0:T(128)} %bitcast.rank_ref, f32[16]{0:T(128)} %d_ref.11, f32[512]{0:T(512)} %w_ref.9, ...), custom_call_target="tpu_custom_call" | custom-call | flops 671088640 | bytes 7864320 | tf_op jit(solution)/shard_map/second/pallas_call | solution.py:19
  90.9 4.1 %all-to-all-start.2 = ((bf16[32,32,256]{2,1,0:T(8,128)(2,1)}), bf16[32,32,256]{2,1,0:T(8,128)(2,1)S(1)}, u32[]{:S(2)}, u32[]{:S(2)}) async-start(bf16[32,32,256]{2,1,0:T(8,128)(2,1)} %get-tuple-element.26), calls=%async_computation.2 | async-start | bytes 1048576 | tf_op jit(solution)/shard_map/all_to_all | solution.py:229
  95.0 1.9 %collective-permute-start.3 = (bf16[32,16,256]{2,1,0:T(8,128)(2,1)}, bf16[32,16,256]{2,1,0:T(8,128)(2,1)S(1)}, u32[]{:S(2)}, u32[]{:S(2)}) collective-permute-start(bf16[32,16,256]{2,1,0:T(8,128)(2,1)} %get-tuple-element.29), channel_id=1, source_target_pairs={{32,0},{64,32},{96,64},{128,96},{160,128},{192,160},{224,192},{256... | collective-permute-start | bytes 786440 | tf_op jit(solution)/shard_map/ppermute | solution.py:235
  96.9 2.4 %collective-permute-start.2 = (bf16[32,16,256]{2,1,0:T(8,128)(2,1)}, bf16[32,16,256]{2,1,0:T(8,128)(2,1)S(1)}, u32[]{:S(2)}, u32[]{:S(2)}) collective-permute-start(bf16[32,16,256]{2,1,0:T(8,128)(2,1)} %get-tuple-element.29), channel_id=1, source_target_pairs={{0,32},{32,64},{64,96},{96,128},{128,160},{160,192},{192,224},{224... | collective-permute-start | bytes 786440 | tf_op jit(solution)/shard_map/ppermute | solution.py:235
  99.3 4.7 %collective-permute-start.5 = (bf16[32,16,256]{2,1,0:T(8,128)(2,1)}, bf16[32,16,256]{2,1,0:T(8,128)(2,1)S(1)}, u32[]{:S(2)}, u32[]{:S(2)}) collective-permute-start(bf16[32,16,256]{2,1,0:T(8,128)(2,1)} %get-tuple-element.30), channel_id=1, source_target_pairs={{32,0},{64,32},{96,64},{128,96},{160,128},{192,160},{224,192},{256... | collective-permute-start | bytes 786440 | tf_op jit(solution)/shard_map/ppermute | solution.py:235
  104.0 1.9 %collective-permute-start.4 = (bf16[32,16,256]{2,1,0:T(8,128)(2,1)}, bf16[32,16,256]{2,1,0:T(8,128)(2,1)S(1)}, u32[]{:S(2)}, u32[]{:S(2)}) collective-permute-start(bf16[32,16,256]{2,1,0:T(8,128)(2,1)} %get-tuple-element.30), channel_id=1, source_target_pairs={{0,32},{32,64},{64,96},{96,128},{128,160},{160,192},{192,224},{224... | collective-permute-start | bytes 786440 | tf_op jit(solution)/shard_map/ppermute | solution.py:235
  105.9 0.9 collective-permute-done.2.lo_ref
  106.9 2.6 %collective-permute-done.5.hiw_ref = bf16[32,16,256]{2,1,0:T(8,128)(2,1)S(1)} collective-permute-done((bf16[32,16,256]{2,1,0:T(8,128)(2,1)}, bf16[32,16,256]{2,1,0:T(8,128)(2,1)S(1)}, u32[]{:S(2)}, u32[]{:S(2)}) %collective-permute-start.5) | collective-permute-done | bytes 262176 | tf_op jit(solution)/shard_map/ppermute | solution.py:235
  109.4 4.6 %collective-permute-done.4.low_ref = bf16[32,16,256]{2,1,0:T(8,128)(2,1)S(1)} collective-permute-done((bf16[32,16,256]{2,1,0:T(8,128)(2,1)}, bf16[32,16,256]{2,1,0:T(8,128)(2,1)S(1)}, u32[]{:S(2)}, u32[]{:S(2)}) %collective-permute-start.4) | collective-permute-done | bytes 262176 | tf_op jit(solution)/shard_map/ppermute | solution.py:235
  114.1 13.0 %all-to-all-done.2.r_ref = bf16[32,32,256]{2,1,0:T(8,128)(2,1)S(1)} async-done(((bf16[32,32,256]{2,1,0:T(8,128)(2,1)}), bf16[32,32,256]{2,1,0:T(8,128)(2,1)S(1)}, u32[]{:S(2)}, u32[]{:S(2)}) %all-to-all-start.2) | async-done | bytes 524320 | tf_op jit(solution)/shard_map/all_to_all | solution.py:229
  127.1 0.8 copy-done.1
  127.8 3.8 %third.1 = (f32[16,8,1024]{2,1,0:T(8,128)}, bf16[32,16,256]{2,1,0:T(8,128)(2,1)}, bf16[32,16,256]{2,1,0:T(8,128)(2,1)}) custom-call(s32[1]{0:T(128)} %bitcast.rank_ref, f32[16]{0:T(128)} %d_ref.11, f32[512]{0:T(512)} %w_ref.9, bf16[32,32,256]{2,1,0:T(8,128)(2,1)} %copy-done.1, f32[32,16,256]{2,1,0:T(8,128)} %get-tuple-element.27.z_ref, ...), custom_call_target="tpu_custom_call" | custom-call | flops 134217728 | bytes 4990976 | tf_op jit(solution)/shard_map/third/pallas_call | solution.py:19
  131.6 4.1 %all-to-all-start.3 = ((bf16[32,16,256]{2,1,0:T(8,128)(2,1)}), bf16[32,16,256]{2,1,0:T(8,128)(2,1)S(1)}, u32[]{:S(2)}, u32[]{:S(2)}) async-start(bf16[32,16,256]{2,1,0:T(8,128)(2,1)} %get-tuple-element.33), calls=%async_computation.3 | async-start | bytes 524288 | tf_op jit(solution)/shard_map/all_to_all | solution.py:229
  135.7 1.9 %collective-permute-start.7 = (bf16[32,16,256]{2,1,0:T(8,128)(2,1)}, bf16[32,16,256]{2,1,0:T(8,128)(2,1)S(1)}, u32[]{:S(2)}, u32[]{:S(2)}) collective-permute-start(bf16[32,16,256]{2,1,0:T(8,128)(2,1)} %get-tuple-element.34.x_ref), channel_id=1, source_target_pairs={{32,0},{64,32},{96,64},{128,96},{160,128},{192,160},{224,192},{256... | collective-permute-start | bytes 786440 | tf_op jit(solution)/shard_map/ppermute | solution.py:235
  137.6 2.4 %collective-permute-start.6 = (bf16[32,16,256]{2,1,0:T(8,128)(2,1)}, bf16[32,16,256]{2,1,0:T(8,128)(2,1)S(1)}, u32[]{:S(2)}, u32[]{:S(2)}) collective-permute-start(bf16[32,16,256]{2,1,0:T(8,128)(2,1)} %get-tuple-element.34.x_ref), channel_id=1, source_target_pairs={{0,32},{32,64},{64,96},{96,128},{128,160},{160,192},{192,224},{224... | collective-permute-start | bytes 786440 | tf_op jit(solution)/shard_map/ppermute | solution.py:235
  140.0 3.8 %last_rest.1.z_ref = f32[32,16,256]{2,1,0:T(8,128)} custom-call(s32[1]{0:T(128)} %bitcast.rank_ref, f32[16]{0:T(128)} %d_ref.11, f32[512]{0:T(512)} %w_ref.9, bf16[32,16,256]{2,1,0:T(8,128)(2,1)} %get-tuple-element.34.x_ref, bf16[1024,1024]{1,0:T(8,128)(2,1)} %bitcast.10, bf16[128,1024]{1,0:T(8,128)(2,1)} %bitcast.13, f32[32,16,256]{2,1,0:T(8,128)} %get-tuple-element.35.x1_ref), custom_call_target="tpu_custom_call" | custom-call | flops 536870912 | bytes 3670016 | tf_op jit(solution)/shard_map/last_rest/pallas_call | solution.py:19
  143.8 3.9 %collective-permute-done.6.lo_ref = bf16[32,16,256]{2,1,0:T(8,128)(2,1)S(1)} collective-permute-done((bf16[32,16,256]{2,1,0:T(8,128)(2,1)}, bf16[32,16,256]{2,1,0:T(8,128)(2,1)S(1)}, u32[]{:S(2)}, u32[]{:S(2)}) %collective-permute-start.6) | collective-permute-done | bytes 262176 | tf_op jit(solution)/shard_map/ppermute | solution.py:235
  147.8 8.4 %all-to-all-done.3.r_ref = bf16[32,16,256]{2,1,0:T(8,128)(2,1)S(1)} async-done(((bf16[32,16,256]{2,1,0:T(8,128)(2,1)}), bf16[32,16,256]{2,1,0:T(8,128)(2,1)S(1)}, u32[]{:S(2)}, u32[]{:S(2)}) %all-to-all-start.3) | async-done | bytes 262176 | tf_op jit(solution)/shard_map/all_to_all | solution.py:229
  156.1 0.7 copy-done.3
  156.8 2.5 %last.1 = f32[16,8,1024]{2,1,0:T(8,128)} custom-call(s32[1]{0:T(128)} %bitcast.rank_ref, f32[16]{0:T(128)} %d_ref.11, f32[512]{0:T(512)} %w_ref.9, bf16[32,16,256]{2,1,0:T(8,128)(2,1)} %copy-done.3, f32[32,16,256]{2,1,0:T(8,128)} %last_rest.1.z_ref, bf16[32,16,256]{2,1,0:T(8,128)(2,1)} %copy-done.10, bf16[32,16,256]{2,1,0:T(8,128)(2,1)} %copy-done.9, ...), custom_call_target="tpu_custom_call" | custom-call | flops 16859136 | bytes 2107392 | tf_op jit(solution)/shard_map/last/pallas_call | solution.py:19
  (21 shorter events, 0.6 us)
Async XLA Ops:
  3.0 41.0 %all-to-all-start = ((bf16[32,40,128]{2,1,0:T(8,128)(2,1)}), bf16[32,40,128]{2,1,0:T(8,128)(2,1)S(1)}, u32[]{:S(2)}, u32[]{:S(2)}) async-start(bf16[32,40,128]{2,1,0:T(8,128)(2,1)} %get-tuple-element.19), calls=%async_computation | async-start | bytes 655360 | tf_op jit(solution)/shard_map/all_to_all | solution.py:229
  19.8 6.7 %collective-permute-start.1 = (bf16[33,16,256]{2,1,0:T(8,128)(2,1)}, bf16[33,16,256]{2,1,0:T(8,128)(2,1)S(1)}, u32[]{:S(2)}, u32[]{:S(2)}) collective-permute-start(bf16[33,16,256]{2,1,0:T(8,128)(2,1)} %get-tuple-element.20.x_ref), channel_id=1, source_target_pairs={{32,0},{64,32},{96,64},{128,96},{160,128},{192,160},{224,192},{256... | collective-permute-start | bytes 811016 | tf_op jit(solution)/shard_map/ppermute | solution.py:235
  22.0 10.7 %collective-permute-start = (bf16[33,16,256]{2,1,0:T(8,128)(2,1)}, bf16[33,16,256]{2,1,0:T(8,128)(2,1)S(1)}, u32[]{:S(2)}, u32[]{:S(2)}) collective-permute-start(bf16[33,16,256]{2,1,0:T(8,128)(2,1)} %get-tuple-element.20.x_ref), channel_id=1, source_target_pairs={{0,32},{32,64},{64,96},{96,128},{128,160},{160,192},{192,224},{224... | collective-permute-start | bytes 811016 | tf_op jit(solution)/shard_map/ppermute | solution.py:235
  26.5 6.2 %copy-start.4 = (bf16[33,16,256]{2,1,0:T(8,128)(2,1)}, bf16[33,16,256]{2,1,0:T(8,128)(2,1)S(1)}, u32[]{:S(2)}) copy-start(bf16[33,16,256]{2,1,0:T(8,128)(2,1)S(1)} %collective-permute-done.1.hi_ref) | copy-start | bytes 811012
  32.7 0.7 copy-start
  44.1 0.7 copy-start.2
  90.9 36.2 %all-to-all-start.2 = ((bf16[32,32,256]{2,1,0:T(8,128)(2,1)}), bf16[32,32,256]{2,1,0:T(8,128)(2,1)S(1)}, u32[]{:S(2)}, u32[]{:S(2)}) async-start(bf16[32,32,256]{2,1,0:T(8,128)(2,1)} %get-tuple-element.26), calls=%async_computation.2 | async-start | bytes 1048576 | tf_op jit(solution)/shard_map/all_to_all | solution.py:229
  95.0 10.9 %collective-permute-start.3 = (bf16[32,16,256]{2,1,0:T(8,128)(2,1)}, bf16[32,16,256]{2,1,0:T(8,128)(2,1)S(1)}, u32[]{:S(2)}, u32[]{:S(2)}) collective-permute-start(bf16[32,16,256]{2,1,0:T(8,128)(2,1)} %get-tuple-element.29), channel_id=1, source_target_pairs={{32,0},{64,32},{96,64},{128,96},{160,128},{192,160},{224,192},{256... | collective-permute-start | bytes 786440 | tf_op jit(solution)/shard_map/ppermute | solution.py:235
  96.9 10.0 %collective-permute-start.2 = (bf16[32,16,256]{2,1,0:T(8,128)(2,1)}, bf16[32,16,256]{2,1,0:T(8,128)(2,1)S(1)}, u32[]{:S(2)}, u32[]{:S(2)}) collective-permute-start(bf16[32,16,256]{2,1,0:T(8,128)(2,1)} %get-tuple-element.29), channel_id=1, source_target_pairs={{0,32},{32,64},{64,96},{96,128},{128,160},{160,192},{192,224},{224... | collective-permute-start | bytes 786440 | tf_op jit(solution)/shard_map/ppermute | solution.py:235
  99.3 10.1 %collective-permute-start.5 = (bf16[32,16,256]{2,1,0:T(8,128)(2,1)}, bf16[32,16,256]{2,1,0:T(8,128)(2,1)S(1)}, u32[]{:S(2)}, u32[]{:S(2)}) collective-permute-start(bf16[32,16,256]{2,1,0:T(8,128)(2,1)} %get-tuple-element.30), channel_id=1, source_target_pairs={{32,0},{64,32},{96,64},{128,96},{160,128},{192,160},{224,192},{256... | collective-permute-start | bytes 786440 | tf_op jit(solution)/shard_map/ppermute | solution.py:235
  104.0 10.1 %collective-permute-start.4 = (bf16[32,16,256]{2,1,0:T(8,128)(2,1)}, bf16[32,16,256]{2,1,0:T(8,128)(2,1)S(1)}, u32[]{:S(2)}, u32[]{:S(2)}) collective-permute-start(bf16[32,16,256]{2,1,0:T(8,128)(2,1)} %get-tuple-element.30), channel_id=1, source_target_pairs={{0,32},{32,64},{64,96},{96,128},{128,160},{160,192},{192,224},{224... | collective-permute-start | bytes 786440 | tf_op jit(solution)/shard_map/ppermute | solution.py:235
  105.9 21.1 %copy-start.5 = (bf16[32,16,256]{2,1,0:T(8,128)(2,1)}, bf16[32,16,256]{2,1,0:T(8,128)(2,1)S(1)}, u32[]{:S(2)}) copy-start(bf16[32,16,256]{2,1,0:T(8,128)(2,1)S(1)} %collective-permute-done.3.hi_ref) | copy-start | bytes 786436
  106.9 20.2 %copy-start.6 = (bf16[32,16,256]{2,1,0:T(8,128)(2,1)}, bf16[32,16,256]{2,1,0:T(8,128)(2,1)S(1)}, u32[]{:S(2)}) copy-start(bf16[32,16,256]{2,1,0:T(8,128)(2,1)S(1)} %collective-permute-done.2.lo_ref) | copy-start | bytes 786436
  109.4 17.6 %copy-start.7 = (bf16[32,16,256]{2,1,0:T(8,128)(2,1)}, bf16[32,16,256]{2,1,0:T(8,128)(2,1)S(1)}, u32[]{:S(2)}) copy-start(bf16[32,16,256]{2,1,0:T(8,128)(2,1)S(1)} %collective-permute-done.5.hiw_ref) | copy-start | bytes 786436
  114.1 13.0 %copy-start.8 = (bf16[32,16,256]{2,1,0:T(8,128)(2,1)}, bf16[32,16,256]{2,1,0:T(8,128)(2,1)S(1)}, u32[]{:S(2)}) copy-start(bf16[32,16,256]{2,1,0:T(8,128)(2,1)S(1)} %collective-permute-done.4.low_ref) | copy-start | bytes 786436
  127.0 0.8 copy-start.1
  131.6 24.5 %all-to-all-start.3 = ((bf16[32,16,256]{2,1,0:T(8,128)(2,1)}), bf16[32,16,256]{2,1,0:T(8,128)(2,1)S(1)}, u32[]{:S(2)}, u32[]{:S(2)}) async-start(bf16[32,16,256]{2,1,0:T(8,128)(2,1)} %get-tuple-element.33), calls=%async_computation.3 | async-start | bytes 524288 | tf_op jit(solution)/shard_map/all_to_all | solution.py:229
  135.7 8.1 %collective-permute-start.7 = (bf16[32,16,256]{2,1,0:T(8,128)(2,1)}, bf16[32,16,256]{2,1,0:T(8,128)(2,1)S(1)}, u32[]{:S(2)}, u32[]{:S(2)}) collective-permute-start(bf16[32,16,256]{2,1,0:T(8,128)(2,1)} %get-tuple-element.34.x_ref), channel_id=1, source_target_pairs={{32,0},{64,32},{96,64},{128,96},{160,128},{192,160},{224,192},{256... | collective-permute-start | bytes 786440 | tf_op jit(solution)/shard_map/ppermute | solution.py:235
  137.6 10.1 %collective-permute-start.6 = (bf16[32,16,256]{2,1,0:T(8,128)(2,1)}, bf16[32,16,256]{2,1,0:T(8,128)(2,1)S(1)}, u32[]{:S(2)}, u32[]{:S(2)}) collective-permute-start(bf16[32,16,256]{2,1,0:T(8,128)(2,1)} %get-tuple-element.34.x_ref), channel_id=1, source_target_pairs={{0,32},{32,64},{64,96},{96,128},{128,160},{160,192},{192,224},{224... | collective-permute-start | bytes 786440 | tf_op jit(solution)/shard_map/ppermute | solution.py:235
  143.8 12.3 %copy-start.9 = (bf16[32,16,256]{2,1,0:T(8,128)(2,1)}, bf16[32,16,256]{2,1,0:T(8,128)(2,1)S(1)}, u32[]{:S(2)}) copy-start(bf16[32,16,256]{2,1,0:T(8,128)(2,1)S(1)} %collective-permute-done.7.hi_ref) | copy-start | bytes 786436
  147.7 8.4 %copy-start.10 = (bf16[32,16,256]{2,1,0:T(8,128)(2,1)}, bf16[32,16,256]{2,1,0:T(8,128)(2,1)S(1)}, u32[]{:S(2)}) copy-start(bf16[32,16,256]{2,1,0:T(8,128)(2,1)S(1)} %collective-permute-done.6.lo_ref) | copy-start | bytes 786436
  156.1 0.7 copy-start.3

commit v3 on v2

v3 whole, which is shorter than its diff:
```python
import functools

import jax
import jax.numpy as jnp
from jax import lax
from jax.experimental import pallas as pl
from jax.experimental.pallas import tpu as pltpu
from jax.sharding import PartitionSpec as P

SCALE_FACTOR = 0.35
GAIN = 2.0 * SCALE_FACTOR
F32, BF16 = jnp.float32, jnp.bfloat16
GRANT = 10 * 2**20


def call(kernel, outs, *args, flops=0, scalars=(), room=(), grant=None):
    shapes = [jax.ShapeDtypeStruct(s, d) for s, d in outs]
    moved = sum(a.size * a.dtype.itemsize for a in args) + sum(s.size * s.dtype.itemsize for s in shapes)
    vmem = pl.BlockSpec(memory_space=pltpu.VMEM)
    return pl.pallas_call(
        kernel,
        out_shape=shapes,
        in_specs=[pl.BlockSpec(memory_space=pltpu.SMEM)] * len(scalars) + [vmem] * len(args),
        out_specs=[vmem] * len(shapes),
        scratch_shapes=[pltpu.VMEM(s, d) for s, d in room],
        compiler_params=pltpu.CompilerParams(vmem_limit_bytes=grant),
        cost_estimate=pl.CostEstimate(flops=max(flops, 8 * moved), bytes_accessed=moved, transcendentals=0),
        name=kernel.func.__name__,
    )(*scalars, *args)


def natural(quarters, piece, width):
    return slice(None), piece // quarters, pl.ds((piece % quarters) * width, width)


def column(values, shape):
    row = lax.broadcasted_iota(jnp.int32, shape, 0)
    out = jnp.full(shape, values[0], F32)
    for i, value in enumerate(values[1:], 1):
        out = jnp.where(row == i, value, out)
    return out


def own_columns(rows, width, rank_ref, d_ref, w_ref):
    damp = [d_ref[i] for i in range(rows)]
    weight = [w_ref[rank_ref[0] * rows + i] for i in range(rows)]
    d = column(damp, (rows, width))
    return GAIN * d, GAIN * d * column(weight, (rows, width)), d * d


def pack(vib, d_ref, x_ref, c_ref, sent_ref, x0_ref):
    pieces, rows, width = x0_ref.shape
    pieces -= 1
    quarters, half = pieces // vib, width // 2
    for p in range(pieces):
        x = x_ref[natural(quarters, p, width)].astype(BF16)
        x0_ref[p] = x
        sent_ref[p, :rows] = x[:, :half]
        sent_ref[p, rows : 2 * rows] = x[:, half:]
    c = c_ref[...].astype(F32)
    x0_ref[pieces] = column([c[:, q * width : (q + 1) * width] for q in range(quarters)], (rows, width)).astype(BF16)
    tile = (rows // 2, half)
    lane = lax.broadcasted_iota(jnp.int32, tile, 1)
    fine = [column([d_ref[h * rows // 2 + i] for i in range(rows // 2)], tile) for h in range(2)]
    high = [f.astype(BF16).astype(F32) for f in fine]
    low = [f - h for f, h in zip(fine, high)]
    mixed = jnp.where(lane < half // 2, jnp.where(lane < half // 4, high[0], low[0]), jnp.where(lane < 3 * half // 4, high[1], low[1]))
    for p in range(pieces):
        sent_ref[p, 2 * rows :] = mixed.astype(BF16)


def angular(vib, x_ref, t_ref, v_ref, grid_ref, put):
    rows, width = x_ref.shape[1:]
    quarters = t_ref.shape[0] // width
    sources = [
        jnp.concatenate([x_ref[v * quarters + q] for v in range(vib)], axis=0) for q in range(quarters)
    ]
    for g in range(quarters):
        cols = pl.ds(g * width, width)
        total = jnp.zeros((vib * rows, width), F32)
        for q in range(quarters):
            total += jnp.dot(sources[q], t_ref[pl.ds(q * width, width), cols], preferred_element_type=F32)
        grid_ref[:, cols] = (total * v_ref[:, cols].astype(F32)).astype(BF16)
    for q in range(quarters):
        put(q, lax.dot_general(
            grid_ref[...], t_ref[pl.ds(q * width, width), :], (((1,), (1,)), ((), ())), preferred_element_type=F32
        ))


def mixed(consts_ref, p, quarters, lo_ref, hi_ref):
    q = p % quarters
    return consts_ref[5 + q] * lo_ref[p].astype(F32) + consts_ref[5 + quarters + q] * hi_ref[p].astype(F32)


def first_rest(vib, rank_ref, d_ref, w_ref, x_ref, t_ref, v_ref, lo_ref, hi_ref, c_ref, old_ref, z_ref, wall_ref, consts_ref, grid_ref):
    pieces, rows, width = z_ref.shape
    quarters = pieces // vib
    tile = (rows, width)
    g, gw, dd = own_columns(rows, width, rank_ref, d_ref, w_ref)
    consts_ref[0], consts_ref[1], consts_ref[2] = g, gw, dd
    below = lo_ref[pieces].astype(F32)
    own = lax.rem(rank_ref[0], quarters)
    under, over = jnp.zeros(tile, F32), jnp.zeros(tile, F32)
    for q in range(quarters):
        lower = jnp.broadcast_to(below[q : q + 1], tile)
        upper = jnp.broadcast_to(c_ref[:, q * width : (q + 1) * width].astype(F32), tile)
        consts_ref[5 + q], consts_ref[5 + quarters + q] = lower, upper
        under, over = jnp.where(own == q, lower, under), jnp.where(own == q, upper, over)
    consts_ref[3], consts_ref[4] = under, over
    for p in range(pieces):
        wall_ref[p] = column([w_ref[p * rows + i] for i in range(rows)], wall_ref.shape[1:])

    def put(q, part):
        for v in range(vib):
            p = v * quarters + q
            z = g * part[v * rows : (v + 1) * rows] + gw * mixed(consts_ref, p, quarters, lo_ref, hi_ref)
            z_ref[p] = (z - dd * old_ref[natural(quarters, p, width)]).astype(BF16)

    angular(vib, x_ref, t_ref, v_ref, grid_ref, put)


def radial(k_ref, x, pieces, put):
    rows = k_ref.shape[0] // pieces
    step = 128 // rows
    for s in range(0, pieces, step):
        y = jnp.dot(k_ref[s * rows : (s + step) * rows], x, preferred_element_type=F32)
        for i in range(step):
            put(s + i, y[i * rows : (i + 1) * rows])


def twice(half):
    return jnp.concatenate([half, half], axis=1)


def first_radial(k_ref, r_ref, z_ref, gall_ref, out_ref, x_ref):
    pieces, rows, width = z_ref.shape
    half = width // 2
    for p in range(pieces):
        at = slice(p * rows, (p + 1) * rows)
        x_ref[at, :half] = r_ref[p, :rows]
        x_ref[at, half:] = r_ref[p, rows : 2 * rows]
        tile = r_ref[p, 2 * rows :].astype(F32)
        for h in range(2):
            lane = h * half // 2
            d = tile[:, lane : lane + 1] + tile[:, lane + half // 4 : lane + half // 4 + 1]
            gall_ref[p, h * rows // 2 : (h + 1) * rows // 2] = jnp.broadcast_to(GAIN * d, (rows // 2, half))

    def put(p, y):
        out_ref[p, :rows] = (y * twice(gall_ref[p])).astype(BF16)
        out_ref[p, rows:] = z_ref[p]

    radial(k_ref, x_ref[...], pieces, put)


def second(vib, r_ref, s_ref, k_ref, gall_ref, wall_ref, t_ref, v_ref, x0_ref, consts_ref,
           xb_ref, cb_ref, out_ref, gwall_ref, grid_ref):
    pieces, rows, width = xb_ref.shape
    gwall_ref[...] = gall_ref[...] * wall_ref[...]
    quarters = pieces // vib
    g, dd = consts_ref[0], consts_ref[2]
    for p in range(pieces):
        xb_ref[p] = (s_ref[p, rows:].astype(F32) + r_ref[p, :rows].astype(F32)).astype(BF16)
        cb_ref[p] = (r_ref[p, rows:].astype(F32) + s_ref[p, :rows].astype(F32)).astype(BF16)

    def put_radial(p, y):
        out_ref[p, :rows] = (y * twice(gall_ref[p])).astype(BF16)

    radial(k_ref, cb_ref[...].reshape(pieces * rows, width), pieces, put_radial)

    def put(q, part):
        for v in range(vib):
            p = v * quarters + q
            out_ref[p, rows:] = (g * part[v * rows : (v + 1) * rows] - dd * x0_ref[p].astype(F32)).astype(BF16)

    angular(vib, xb_ref, t_ref, v_ref, grid_ref, put)


def third_columns(r_ref, s_ref, lo_ref, hi_ref, consts_ref, gwall_ref, k_ref, out_ref, cb_ref):
    pieces, rows, _ = out_ref.shape
    for p in range(pieces):
        mix = consts_ref[3] * lo_ref[p].astype(F32) + consts_ref[4] * hi_ref[p].astype(F32)
        c = r_ref[p, rows:].astype(F32) + s_ref[p, :rows].astype(F32) + twice(gwall_ref[p]) * mix
        cb_ref[p * rows : (p + 1) * rows] = c.astype(BF16)

    def put(p, y):
        out_ref[p] = y.astype(BF16)

    radial(k_ref, cb_ref[...], pieces, put)


def third_rows(vib, r_ref, s_ref, lo_ref, hi_ref, consts_ref, x2_ref, xb_ref):
    pieces, rows, width = xb_ref.shape
    quarters = pieces // vib
    for p in range(pieces):
        x = s_ref[p, rows:].astype(F32) + r_ref[p, :rows].astype(F32)
        x = x + consts_ref[1] * mixed(consts_ref, p, quarters, lo_ref, hi_ref)
        x2_ref[natural(quarters, p, width)] = x
        xb_ref[p] = x.astype(BF16)


def last_rest(vib, x_ref, t_ref, v_ref, x1_ref, consts_ref, z_ref, grid_ref):
    pieces, rows, width = x_ref.shape
    quarters = pieces // vib

    def put(q, part):
        for v in range(vib):
            p = v * quarters + q
            z_ref[p] = consts_ref[0] * part[v * rows : (v + 1) * rows] - consts_ref[2] * x1_ref[p].astype(F32)

    angular(vib, x_ref, t_ref, v_ref, grid_ref, put)


def last(vib, r_ref, z_ref, lo_ref, hi_ref, consts_ref, x3_ref):
    pieces, rows, width = z_ref.shape
    quarters = pieces // vib
    for p in range(pieces):
        x = z_ref[p] + consts_ref[0] * r_ref[p].astype(F32) + consts_ref[1] * mixed(consts_ref, p, quarters, lo_ref, hi_ref)
        x3_ref[natural(quarters, p, width)] = x


def exchange(blocks):
    return lax.all_to_all(blocks, "rad", 0, 0, tiled=True)


def neighbours(array):
    devices = lax.axis_size("hel")
    up = [(i, i + 1) for i in range(devices - 1)]
    return lax.ppermute(array, "hel", up), lax.ppermute(array, "hel", [(j, i) for i, j in up])


def body(older, newer, kinetic, transform, potential, coupling, radial_weight, damping):
    _, rows, vib, ang = newer.shape
    pieces = lax.axis_size("rad")
    width = ang // (pieces // vib)
    size = rows * pieces
    flat = (rows * vib, ang)
    packed, double = (pieces, rows, width), (pieces, 2 * rows, width)
    old, new = older[0], newer[0]
    table = transform[0]
    pot = jnp.swapaxes(potential, 0, 1).reshape(flat)
    own = (lax.axis_index("rad").astype(jnp.int32).reshape(1), damping, radial_weight)
    grid = (flat, BF16)
    k_flops = 2 * size * size * width
    a_flops = 4 * flat[0] * ang * ang
    part = lambda kernel: functools.partial(kernel, vib)

    sent, x0 = call(
        part(pack), [((pieces, 5 * rows // 2, width // 2), BF16), ((pieces + 1, rows, width), BF16)],
        new, coupling, scalars=(damping,))
    r1 = exchange(sent)
    lo, hi = neighbours(x0)
    quarters = pieces // vib
    z0, wall, consts = call(
        part(first_rest), [(packed, BF16), ((pieces, rows, width // 2), F32), ((5 + 2 * quarters, rows, width), F32)],
        x0, table, pot, lo, hi, coupling, old, scalars=own, room=[grid], flops=a_flops)
    gall, sent = call(
        functools.partial(first_radial), [((pieces, rows, width // 2), F32), (double, BF16)],
        kinetic, r1, z0, room=[((size, width), BF16)], flops=k_flops, grant=GRANT)
    r2 = exchange(sent)
    x1, c1, sent, gwall = call(
        part(second), [(packed, BF16), (packed, BF16), (double, BF16), (gall.shape, F32)],
        r2, sent, kinetic, gall, wall, table, pot, x0, consts, room=[grid], flops=a_flops + k_flops, grant=GRANT)
    r3 = exchange(sent)
    lo, hi = neighbours(x1)
    low, hiw = neighbours(c1)
    r3, lo, hi = lax.optimization_barrier((r3, lo, hi))
    (sent4,) = call(
        functools.partial(third_columns), [(packed, BF16)],
        r3, sent, low, hiw, consts, gwall, kinetic, room=[((size, width), BF16)], flops=k_flops, grant=GRANT)
    r4 = exchange(sent4)
    x2, x2b = call(part(third_rows), [(old.shape, F32), (packed, BF16)], r3, sent, lo, hi, consts, grant=GRANT)
    lo, hi = neighbours(x2b)
    (z2,) = call(part(last_rest), [(packed, F32)], x2b, table, pot, x1, consts, room=[grid], flops=a_flops)
    (x3,) = call(part(last), [(old.shape, F32)], r4, z2, lo, hi, consts, grant=GRANT)
    return x2.reshape(newer.shape), x3.reshape(newer.shape)


def solution(mesh):
    return jax.shard_map(
        body,
        mesh=mesh,
        in_specs=(
            P("hel", "rad", None, None),
            P("hel", "rad", None, None),
            P(),
            P("hel", None, None),
            P("rad", None, None),
            P("hel", None),
            P(),
            P("rad"),
        ),
        out_specs=(P("hel", "rad", None, None), P("hel", "rad", None, None)),
        check_vma=False,
    )
```

time: 160 us -> 155 us (0.969)
  Pallas kernels: 24.1 us -> 18.6 us
  waiting for transfers between devices: 46.6 us -> 44.3 us
  local copies, waits for them, and re-layouts: 4.76 us -> 6.97 us
    pallas_call x7 -> x8, Pallas kernels: 24.1 us -> 18.6 us  [call(): pl.pallas_call(kernel, out_shape=shapes, in_specs=[pl.BlockSpec(memory_sp...]
    all_to_all x3, waiting for transfers between devices: 27.7 us -> 32.3 us  [exchange(): return lax.all_to_all(blocks, 'rad', 0, 0, tiled=True)]
    ppermute x4, waiting for transfers between devices: 15.7 us -> 11.5 us  [neighbours(): lax.ppermute(array, 'hel', up)]
    ppermute x4, waiting for transfers between devices: 3.16 us -> 0.51 us  [neighbours(): lax.ppermute(array, 'hel', [(j, i) for i, j in up])]
    unnamed x22 -> x32, local copies, waits for them, and re-layouts: 2.96 us -> 5.12 us
  transfers between devices with their start and end apart: 11 -> 11, of which waited for: 9 -> 7; matrix products, arithmetic and copies ran while one was open for 1% -> 1% of each run, Pallas kernels for 5% -> 7%
where the time goes in v3:
time: 155 us; the launch traced here: 154 us
  starting transfers between devices  44.6 us (29%)
  waiting for transfers between devices  44.3 us (29%)
  blocking collectives  38.6 us (25%)
  Pallas kernels  18.6 us (12%)
  local copies, waits for them, and re-layouts  6.97 us (4%)
    all_to_all x1, blocking collectives, exchange(): return lax.all_to_all(blocks, 'rad', 0, 0, tiled=True)  38.6 us
    all_to_all x3, waiting for transfers between devices, exchange(): return lax.all_to_all(blocks, 'rad', 0, 0, tiled=True)  32.3 us
    all_to_all x3, starting transfers between devices, exchange(): return lax.all_to_all(blocks, 'rad', 0, 0, tiled=True)  24.9 us
    pallas_call x8, Pallas kernels, call(): pl.pallas_call(kernel, out_shape=shapes, in_specs=[pl.BlockSpec(memory_sp...  18.6 us
    ppermute x4, waiting for transfers between devices, neighbours(): lax.ppermute(array, 'hel', up)  11.5 us
    ppermute x4, starting transfers between devices, neighbours(): lax.ppermute(array, 'hel', [(j, i) for i, j in up])  10.8 us
    ppermute x4, starting transfers between devices, neighbours(): lax.ppermute(array, 'hel', up)  8.87 us
    unnamed x32, local copies, waits for them, and re-layouts  5.12 us
  transfers between devices with their start and end apart: 11, of which 7 were waited for; matrix products, arithmetic and copies ran while one was open for 1% of the time, Pallas kernels for 7%

profile of v3, /device:TPU:6, one launch (start us, length us, event | category | flops | bytes accessed | tf_op | source)
XLA Modules:
  0.0 153.8 jit_solution(17431019422464338456)
XLA Ops:
  0.6 2.4 %pack.1 = (bf16[32,40,128]{2,1,0:T(8,128)(2,1)}, bf16[33,16,256]{2,1,0:T(8,128)(2,1)}) custom-call(f32[16]{0:T(128)} %d_ref.3, f32[16,8,1024]{2,1,0:T(8,128)} %bitcast.14, bf16[1,1024]{1,0:T(2,128)(2,1)} %c_ref.3), custom_call_target="tpu_custom_call" | custom-call | flops 8994816 | bytes 1124352 | tf_op jit(solution)/shard_map/pack/pallas_call | solution.py:20
  3.0 16.7 %all-to-all-start = ((bf16[32,40,128]{2,1,0:T(8,128)(2,1)}), bf16[32,40,128]{2,1,0:T(8,128)(2,1)S(1)}, u32[]{:S(2)}, u32[]{:S(2)}) async-start(bf16[32,40,128]{2,1,0:T(8,128)(2,1)} %get-tuple-element.18), calls=%async_computation | async-start | bytes 655360 | tf_op jit(solution)/shard_map/all_to_all | solution.py:222
  19.8 2.2 %collective-permute-start.1 = (bf16[33,16,256]{2,1,0:T(8,128)(2,1)}, bf16[33,16,256]{2,1,0:T(8,128)(2,1)S(1)}, u32[]{:S(2)}, u32[]{:S(2)}) collective-permute-start(bf16[33,16,256]{2,1,0:T(8,128)(2,1)} %get-tuple-element.19.x_ref.x0_ref), channel_id=1, source_target_pairs={{32,0},{64,32},{96,64},{128,96},{160,128},{192,160},{224,192},{256... | collective-permute-start | bytes 811016 | tf_op jit(solution)/shard_map/ppermute | solution.py:228
  22.0 2.1 %collective-permute-start = (bf16[33,16,256]{2,1,0:T(8,128)(2,1)}, bf16[33,16,256]{2,1,0:T(8,128)(2,1)S(1)}, u32[]{:S(2)}, u32[]{:S(2)}) collective-permute-start(bf16[33,16,256]{2,1,0:T(8,128)(2,1)} %get-tuple-element.19.x_ref.x0_ref), channel_id=1, source_target_pairs={{0,32},{32,64},{64,96},{96,128},{128,160},{160,192},{192,224},{224... | collective-permute-start | bytes 811016 | tf_op jit(solution)/shard_map/ppermute | solution.py:228
  24.1 1.9 %copy.10 = bf16[8,16,1024]{2,1,0:T(8,128)(2,1)} copy(bf16[8,16,1024]{2,0,1:T(8,128)(2,1)} %bitcast.17) | data formatting | bytes 524288 | tf_op jit(solution)/shard_map/transpose | solution.py:240
  26.5 6.2 %collective-permute-done.lo_ref = bf16[33,16,256]{2,1,0:T(8,128)(2,1)S(1)} collective-permute-done((bf16[33,16,256]{2,1,0:T(8,128)(2,1)}, bf16[33,16,256]{2,1,0:T(8,128)(2,1)S(1)}, u32[]{:S(2)}, u32[]{:S(2)}) %collective-permute-start) | collective-permute-done | bytes 270368 | tf_op jit(solution)/shard_map/ppermute | solution.py:228
  32.7 0.7 copy-done.15
  33.4 4.5 %first_rest.1 = (bf16[32,16,256]{2,1,0:T(8,128)(2,1)}, f32[32,16,128]{2,1,0:T(8,128)}, f32[13,16,256]{2,1,0:T(8,128)}) custom-call(s32[1]{0:T(128)} %bitcast.1.rank_ref, f32[16]{0:T(128)} %d_ref.3, f32[512]{0:T(512)} %w_ref.1, bf16[33,16,256]{2,1,0:T(8,128)(2,1)} %get-tuple-element.19.x_ref.x0_ref, bf16[1024,1024]{1,0:T(8,128)(2,1)} %bitcast.8, ...), custom_call_target="tpu_custom_call" | custom-call | flops 536870912 | bytes 4433920 | tf_op jit(solution)/shard_map/first_rest/pallas_call | solution.py:20
  37.9 6.2 %all-to-all-done.r_ref = bf16[32,40,128]{2,1,0:T(8,128)(2,1)S(1)} async-done(((bf16[32,40,128]{2,1,0:T(8,128)(2,1)}), bf16[32,40,128]{2,1,0:T(8,128)(2,1)S(1)}, u32[]{:S(2)}, u32[]{:S(2)}) %all-to-all-start) | async-done | bytes 327712 | tf_op jit(solution)/shard_map/all_to_all | solution.py:222
  44.1 1.0 copy-done.10
  45.4 38.6 %all_to_all.20.r_ref = bf16[32,32,256]{2,1,0:T(8,128)(2,1)S(1)} all-to-all(bf16[32,32,256]{2,1,0:T(8,128)(2,1)S(1)} %get-tuple-element.21.s_ref), channel_id=1, replica_groups=mesh['hel'=16,'rad'=32] {'rad'}, dimensions={0} | all-to-all | bytes 1048576 | tf_op jit(solution)/shard_map/all_to_all | solution.py:222
  84.1 2.1 %second.1 = (bf16[32,16,256]{2,1,0:T(8,128)(2,1)S(1)}, bf16[32,16,256]{2,1,0:T(8,128)(2,1)S(1)}, bf16[32,32,256]{2,1,0:T(8,128)(2,1)}, f32[32,16,128]{2,1,0:T(8,128)S(1)}) custom-call(bf16[32,32,256]{2,1,0:T(8,128)(2,1)S(1)} %all_to_all.20.r_ref, bf16[32,32,256]{2,1,0:T(8,128)(2,1)S(1)} %get-tuple-element.21.s_ref, bf16[512,512]{1,0:T(8,128)(2,1)S(1)} %copy-done.3, ...), custom_call_target="tpu_custom_call" | custom-call | flops 671088640 | bytes 6250496 | tf_op jit(solution)/shard_map/second/pallas_call | solution.py:20
  86.2 0.7 copy-done.11
  86.9 0.7 copy-done.13
  87.6 4.1 %all-to-all-start.2 = ((bf16[32,32,256]{2,1,0:T(8,128)(2,1)}), bf16[32,32,256]{2,1,0:T(8,128)(2,1)S(1)}, u32[]{:S(2)}, u32[]{:S(2)}) async-start(bf16[32,32,256]{2,1,0:T(8,128)(2,1)} %get-tuple-element.25.s_ref), calls=%async_computation.2 | async-start | bytes 1048576 | tf_op jit(solution)/shard_map/all_to_all | solution.py:222
  91.7 1.9 %collective-permute-start.3 = (bf16[32,16,256]{2,1,0:T(8,128)(2,1)S(1)}, bf16[32,16,256]{2,1,0:T(8,128)(2,1)S(1)}, u32[]{:S(2)}, u32[]{:S(2)}) collective-permute-start(bf16[32,16,256]{2,1,0:T(8,128)(2,1)S(1)} %get-tuple-element.26.x1_ref), channel_id=1, source_target_pairs={{32,0},{64,32},{96,64},{128,96},{160,128},{192,160},{224,192},{256... | collective-permute-start | bytes 786440 | tf_op jit(solution)/shard_map/ppermute | solution.py:228
  93.7 2.4 %collective-permute-start.2 = (bf16[32,16,256]{2,1,0:T(8,128)(2,1)S(1)}, bf16[32,16,256]{2,1,0:T(8,128)(2,1)S(1)}, u32[]{:S(2)}, u32[]{:S(2)}) collective-permute-start(bf16[32,16,256]{2,1,0:T(8,128)(2,1)S(1)} %get-tuple-element.26.x1_ref), channel_id=1, source_target_pairs={{0,32},{32,64},{64,96},{96,128},{128,160},{160,192},{192,224},{224... | collective-permute-start | bytes 786440 | tf_op jit(solution)/shard_map/ppermute | solution.py:228
  96.1 4.7 %collective-permute-start.5 = (bf16[32,16,256]{2,1,0:T(8,128)(2,1)}, bf16[32,16,256]{2,1,0:T(8,128)(2,1)S(1)}, u32[]{:S(2)}, u32[]{:S(2)}) collective-permute-start(bf16[32,16,256]{2,1,0:T(8,128)(2,1)} %copy-done.13), channel_id=1, source_target_pairs={{32,0},{64,32},{96,64},{128,96},{160,128},{192,160},{224,192},{256... | collective-permute-start | bytes 786440 | tf_op jit(solution)/shard_map/ppermute | solution.py:228
  100.7 1.9 %collective-permute-start.4 = (bf16[32,16,256]{2,1,0:T(8,128)(2,1)}, bf16[32,16,256]{2,1,0:T(8,128)(2,1)S(1)}, u32[]{:S(2)}, u32[]{:S(2)}) collective-permute-start(bf16[32,16,256]{2,1,0:T(8,128)(2,1)} %copy-done.13), channel_id=1, source_target_pairs={{0,32},{32,64},{64,96},{96,128},{128,160},{160,192},{192,224},{224... | collective-permute-start | bytes 786440 | tf_op jit(solution)/shard_map/ppermute | solution.py:228
  102.7 1.5 collective-permute-done.2.lo_ref
  104.2 19.7 %all-to-all-done.2.r_ref = bf16[32,32,256]{2,1,0:T(8,128)(2,1)S(1)} async-done(((bf16[32,32,256]{2,1,0:T(8,128)(2,1)}), bf16[32,32,256]{2,1,0:T(8,128)(2,1)S(1)}, u32[]{:S(2)}, u32[]{:S(2)}) %all-to-all-start.2) | async-done | bytes 524320 | tf_op jit(solution)/shard_map/all_to_all | solution.py:222
  123.9 0.9 copy-done.12
  124.8 2.2 %third_columns.1 = bf16[32,16,256]{2,1,0:T(8,128)(2,1)} custom-call(bf16[32,32,256]{2,1,0:T(8,128)(2,1)S(1)} %all-to-all-done.2.r_ref, bf16[32,32,256]{2,1,0:T(8,128)(2,1)} %get-tuple-element.25.s_ref, bf16[32,16,256]{2,1,0:T(8,128)(2,1)S(1)} %collective-permute-done.4.lo_ref, bf16[32,16,256]{2,1,0:T(8,128)(2,1)S(1)} %collective-permute-done.5.hi_ref, ...), custom_call_target="tpu_custom_call" | custom-call | flops 134217728 | bytes 2834432 | tf_op jit(solution)/shard_map/third_columns/pallas_call | solution.py:20
  127.0 4.1 %all-to-all-start.3 = ((bf16[32,16,256]{2,1,0:T(8,128)(2,1)}), bf16[32,16,256]{2,1,0:T(8,128)(2,1)S(1)}, u32[]{:S(2)}, u32[]{:S(2)}) async-start(bf16[32,16,256]{2,1,0:T(8,128)(2,1)} %third_columns.1), calls=%async_computation.3 | async-start | bytes 524288 | tf_op jit(solution)/shard_map/all_to_all | solution.py:222
  131.1 2.2 %third_rows.1 = (f32[16,8,1024]{2,1,0:T(8,128)}, bf16[32,16,256]{2,1,0:T(8,128)(2,1)S(1)}) custom-call(bf16[32,32,256]{2,1,0:T(8,128)(2,1)S(1)} %all-to-all-done.2.r_ref, bf16[32,32,256]{2,1,0:T(8,128)(2,1)} %get-tuple-element.25.s_ref, bf16[32,16,256]{2,1,0:T(8,128)(2,1)S(1)} %collective-permute-done.2.lo_ref, ...), custom_call_target="tpu_custom_call" | custom-call | flops 20578304 | bytes 2572288 | tf_op jit(solution)/shard_map/third_rows/pallas_call | solution.py:20
  133.3 2.0 %collective-permute-start.7 = (bf16[32,16,256]{2,1,0:T(8,128)(2,1)S(1)}, bf16[32,16,256]{2,1,0:T(8,128)(2,1)S(1)}, u32[]{:S(2)}, u32[]{:S(2)}) collective-permute-start(bf16[32,16,256]{2,1,0:T(8,128)(2,1)S(1)} %get-tuple-element.33.x_ref), channel_id=1, source_target_pairs={{32,0},{64,32},{96,64},{128,96},{160,128},{192,160},{224,192},{256... | collective-permute-start | bytes 786440 | tf_op jit(solution)/shard_map/ppermute | solution.py:228
  135.3 2.4 %collective-permute-start.6 = (bf16[32,16,256]{2,1,0:T(8,128)(2,1)S(1)}, bf16[32,16,256]{2,1,0:T(8,128)(2,1)S(1)}, u32[]{:S(2)}, u32[]{:S(2)}) collective-permute-start(bf16[32,16,256]{2,1,0:T(8,128)(2,1)S(1)} %get-tuple-element.33.x_ref), channel_id=1, source_target_pairs={{0,32},{32,64},{64,96},{96,128},{128,160},{160,192},{192,224},{224... | collective-permute-start | bytes 786440 | tf_op jit(solution)/shard_map/ppermute | solution.py:228
  137.8 3.7 %last_rest.1.z_ref = f32[32,16,256]{2,1,0:T(8,128)} custom-call(bf16[32,16,256]{2,1,0:T(8,128)(2,1)} %copy-done.9, bf16[1024,1024]{1,0:T(8,128)(2,1)} %bitcast.9, bf16[128,1024]{1,0:T(8,128)(2,1)} %bitcast.12, bf16[32,16,256]{2,1,0:T(8,128)(2,1)} %copy-done.7, f32[13,16,256]{2,1,0:T(8,128)} %get-tuple-element.24.consts_ref), custom_call_target="tpu_custom_call" | custom-call | flops 536870912 | bytes 3620864 | tf_op jit(solution)/shard_map/last_rest/pallas_call | solution.py:20
  141.5 3.7 %collective-permute-done.6.lo_ref = bf16[32,16,256]{2,1,0:T(8,128)(2,1)S(1)} collective-permute-done((bf16[32,16,256]{2,1,0:T(8,128)(2,1)S(1)}, bf16[32,16,256]{2,1,0:T(8,128)(2,1)S(1)}, u32[]{:S(2)}, u32[]{:S(2)}) %collective-permute-start.6) | collective-permute-done | bytes 262176 | tf_op jit(solution)/shard_map/ppermute | solution.py:228
  145.2 6.4 %all-to-all-done.3.r_ref = bf16[32,16,256]{2,1,0:T(8,128)(2,1)S(1)} async-done(((bf16[32,16,256]{2,1,0:T(8,128)(2,1)}), bf16[32,16,256]{2,1,0:T(8,128)(2,1)S(1)}, u32[]{:S(2)}, u32[]{:S(2)}) %all-to-all-start.3) | async-done | bytes 262176 | tf_op jit(solution)/shard_map/all_to_all | solution.py:222
  151.6 1.0 copy-done.5
  152.7 1.1 last.1
  (32 shorter events, 0.9 us)
Async XLA Ops:
  3.0 41.0 %all-to-all-start = ((bf16[32,40,128]{2,1,0:T(8,128)(2,1)}), bf16[32,40,128]{2,1,0:T(8,128)(2,1)S(1)}, u32[]{:S(2)}, u32[]{:S(2)}) async-start(bf16[32,40,128]{2,1,0:T(8,128)(2,1)} %get-tuple-element.18), calls=%async_computation | async-start | bytes 655360 | tf_op jit(solution)/shard_map/all_to_all | solution.py:222
  19.8 6.7 %collective-permute-start.1 = (bf16[33,16,256]{2,1,0:T(8,128)(2,1)}, bf16[33,16,256]{2,1,0:T(8,128)(2,1)S(1)}, u32[]{:S(2)}, u32[]{:S(2)}) collective-permute-start(bf16[33,16,256]{2,1,0:T(8,128)(2,1)} %get-tuple-element.19.x_ref.x0_ref), channel_id=1, source_target_pairs={{32,0},{64,32},{96,64},{128,96},{160,128},{192,160},{224,192},{256... | collective-permute-start | bytes 811016 | tf_op jit(solution)/shard_map/ppermute | solution.py:228
  22.0 10.7 %collective-permute-start = (bf16[33,16,256]{2,1,0:T(8,128)(2,1)}, bf16[33,16,256]{2,1,0:T(8,128)(2,1)S(1)}, u32[]{:S(2)}, u32[]{:S(2)}) collective-permute-start(bf16[33,16,256]{2,1,0:T(8,128)(2,1)} %get-tuple-element.19.x_ref.x0_ref), channel_id=1, source_target_pairs={{0,32},{32,64},{64,96},{96,128},{128,160},{160,192},{192,224},{224... | collective-permute-start | bytes 811016 | tf_op jit(solution)/shard_map/ppermute | solution.py:228
  24.1 20.0 %copy-start.3 = (bf16[512,512]{1,0:T(8,128)(2,1)S(1)}, bf16[512,512]{1,0:T(8,128)(2,1)}, u32[]{:S(2)}) copy-start(bf16[512,512]{1,0:T(8,128)(2,1)} %k_ref.5) | copy-start | bytes 1572868
  26.5 6.2 %copy-start.14 = (bf16[33,16,256]{2,1,0:T(8,128)(2,1)}, bf16[33,16,256]{2,1,0:T(8,128)(2,1)S(1)}, u32[]{:S(2)}) copy-start(bf16[33,16,256]{2,1,0:T(8,128)(2,1)S(1)} %collective-permute-done.1.hi_ref) | copy-start | bytes 811012
  32.7 0.7 copy-start.15
  33.4 50.7 %copy-start = (bf16[1,1024,1024]{2,1,0:T(8,128)(2,1)S(1)}, bf16[1,1024,1024]{2,1,0:T(8,128)(2,1)}, u32[]{:S(2)}) copy-start(bf16[1,1024,1024]{2,1,0:T(8,128)(2,1)} %param.11) | copy-start | bytes 6291460
  33.4 50.7 %copy-start.4 = (bf16[8,16,1024]{2,1,0:T(8,128)(2,1)S(1)}, bf16[8,16,1024]{2,1,0:T(8,128)(2,1)}, u32[]{:S(2)}) copy-start(bf16[8,16,1024]{2,1,0:T(8,128)(2,1)} %copy.10) | copy-start | bytes 786436
  37.9 46.2 %copy-start.1 = (f32[13,16,256]{2,1,0:T(8,128)S(1)}, f32[13,16,256]{2,1,0:T(8,128)}, u32[]{:S(2)}) copy-start(f32[13,16,256]{2,1,0:T(8,128)} %get-tuple-element.24.consts_ref) | copy-start | bytes 638980
  44.1 40.0 %copy-start.6 = (bf16[33,16,256]{2,1,0:T(8,128)(2,1)S(1)}, bf16[33,16,256]{2,1,0:T(8,128)(2,1)}, u32[]{:S(2)}) copy-start(bf16[33,16,256]{2,1,0:T(8,128)(2,1)} %get-tuple-element.19.x_ref.x0_ref) | copy-start | bytes 811012
  44.1 40.0 %copy-start.8 = (f32[32,16,128]{2,1,0:T(8,128)S(1)}, f32[32,16,128]{2,1,0:T(8,128)}, u32[]{:S(2)}) copy-start(f32[32,16,128]{2,1,0:T(8,128)} %get-tuple-element.23.wall_ref) | copy-start | bytes 786436
  44.1 1.0 copy-start.10
  86.2 0.7 copy-start.11
  86.9 0.7 copy-start.13
  87.6 39.4 %copy-start.7 = (bf16[32,16,256]{2,1,0:T(8,128)(2,1)}, bf16[32,16,256]{2,1,0:T(8,128)(2,1)S(1)}, u32[]{:S(2)}) copy-start(bf16[32,16,256]{2,1,0:T(8,128)(2,1)S(1)} %get-tuple-element.26.x1_ref) | copy-start | bytes 786436
  87.6 36.2 %all-to-all-start.2 = ((bf16[32,32,256]{2,1,0:T(8,128)(2,1)}), bf16[32,32,256]{2,1,0:T(8,128)(2,1)S(1)}, u32[]{:S(2)}, u32[]{:S(2)}) async-start(bf16[32,32,256]{2,1,0:T(8,128)(2,1)} %get-tuple-element.25.s_ref), calls=%async_computation.2 | async-start | bytes 1048576 | tf_op jit(solution)/shard_map/all_to_all | solution.py:222
  91.7 10.9 %collective-permute-start.3 = (bf16[32,16,256]{2,1,0:T(8,128)(2,1)S(1)}, bf16[32,16,256]{2,1,0:T(8,128)(2,1)S(1)}, u32[]{:S(2)}, u32[]{:S(2)}) collective-permute-start(bf16[32,16,256]{2,1,0:T(8,128)(2,1)S(1)} %get-tuple-element.26.x1_ref), channel_id=1, source_target_pairs={{32,0},{64,32},{96,64},{128,96},{160,128},{192,160},{224,192},{256... | collective-permute-start | bytes 786440 | tf_op jit(solution)/shard_map/ppermute | solution.py:228
  93.7 10.5 %collective-permute-start.2 = (bf16[32,16,256]{2,1,0:T(8,128)(2,1)S(1)}, bf16[32,16,256]{2,1,0:T(8,128)(2,1)S(1)}, u32[]{:S(2)}, u32[]{:S(2)}) collective-permute-start(bf16[32,16,256]{2,1,0:T(8,128)(2,1)S(1)} %get-tuple-element.26.x1_ref), channel_id=1, source_target_pairs={{0,32},{32,64},{64,96},{96,128},{128,160},{160,192},{192,224},{224... | collective-permute-start | bytes 786440 | tf_op jit(solution)/shard_map/ppermute | solution.py:228
  96.1 27.8 %collective-permute-start.5 = (bf16[32,16,256]{2,1,0:T(8,128)(2,1)}, bf16[32,16,256]{2,1,0:T(8,128)(2,1)S(1)}, u32[]{:S(2)}, u32[]{:S(2)}) collective-permute-start(bf16[32,16,256]{2,1,0:T(8,128)(2,1)} %copy-done.13), channel_id=1, source_target_pairs={{32,0},{64,32},{96,64},{128,96},{160,128},{192,160},{224,192},{256... | collective-permute-start | bytes 786440 | tf_op jit(solution)/shard_map/ppermute | solution.py:228
  100.7 23.1 %collective-permute-start.4 = (bf16[32,16,256]{2,1,0:T(8,128)(2,1)}, bf16[32,16,256]{2,1,0:T(8,128)(2,1)S(1)}, u32[]{:S(2)}, u32[]{:S(2)}) collective-permute-start(bf16[32,16,256]{2,1,0:T(8,128)(2,1)} %copy-done.13), channel_id=1, source_target_pairs={{0,32},{32,64},{64,96},{96,128},{128,160},{160,192},{192,224},{224... | collective-permute-start | bytes 786440 | tf_op jit(solution)/shard_map/ppermute | solution.py:228
  123.9 1.0 copy-start.12
  127.0 24.6 %all-to-all-start.3 = ((bf16[32,16,256]{2,1,0:T(8,128)(2,1)}), bf16[32,16,256]{2,1,0:T(8,128)(2,1)S(1)}, u32[]{:S(2)}, u32[]{:S(2)}) async-start(bf16[32,16,256]{2,1,0:T(8,128)(2,1)} %third_columns.1), calls=%async_computation.3 | async-start | bytes 524288 | tf_op jit(solution)/shard_map/all_to_all | solution.py:222
  133.3 4.5 %copy-start.9 = (bf16[32,16,256]{2,1,0:T(8,128)(2,1)}, bf16[32,16,256]{2,1,0:T(8,128)(2,1)S(1)}, u32[]{:S(2)}) copy-start(bf16[32,16,256]{2,1,0:T(8,128)(2,1)S(1)} %get-tuple-element.33.x_ref) | copy-start | bytes 786436
  133.3 18.4 %copy-start.2 = (f32[13,16,256]{2,1,0:T(8,128)S(1)}, f32[13,16,256]{2,1,0:T(8,128)}, u32[]{:S(2)}) copy-start(f32[13,16,256]{2,1,0:T(8,128)} %get-tuple-element.24.consts_ref) | copy-start | bytes 638980
  133.3 8.2 %collective-permute-start.7 = (bf16[32,16,256]{2,1,0:T(8,128)(2,1)S(1)}, bf16[32,16,256]{2,1,0:T(8,128)(2,1)S(1)}, u32[]{:S(2)}, u32[]{:S(2)}) collective-permute-start(bf16[32,16,256]{2,1,0:T(8,128)(2,1)S(1)} %get-tuple-element.33.x_ref), channel_id=1, source_target_pairs={{32,0},{64,32},{96,64},{128,96},{160,128},{192,160},{224,192},{256... | collective-permute-start | bytes 786440 | tf_op jit(solution)/shard_map/ppermute | solution.py:228
  135.3 9.9 %collective-permute-start.6 = (bf16[32,16,256]{2,1,0:T(8,128)(2,1)S(1)}, bf16[32,16,256]{2,1,0:T(8,128)(2,1)S(1)}, u32[]{:S(2)}, u32[]{:S(2)}) collective-permute-start(bf16[32,16,256]{2,1,0:T(8,128)(2,1)S(1)} %get-tuple-element.33.x_ref), channel_id=1, source_target_pairs={{0,32},{32,64},{64,96},{96,128},{128,160},{160,192},{192,224},{224... | collective-permute-start | bytes 786440 | tf_op jit(solution)/shard_map/ppermute | solution.py:228
  151.6 1.0 copy-start.5

commit v4 on v3

--- a/solution.py
+++ b/solution.py
@@ -92,12 +92,26 @@
     return consts_ref[5 + q] * lo_ref[p].astype(F32) + consts_ref[5 + quarters + q] * hi_ref[p].astype(F32)
 
 
-def first_rest(vib, rank_ref, d_ref, w_ref, x_ref, t_ref, v_ref, lo_ref, hi_ref, c_ref, old_ref, z_ref, wall_ref, consts_ref, grid_ref):
+def first_angular(vib, rank_ref, d_ref, w_ref, x_ref, t_ref, v_ref, old_ref, z_ref, wall_ref, rows_ref, grid_ref):
     pieces, rows, width = z_ref.shape
     quarters = pieces // vib
+    g, gw, dd = own_columns(rows, width, rank_ref, d_ref, w_ref)
+    rows_ref[0], rows_ref[1], rows_ref[2] = g, gw, dd
+    for p in range(pieces):
+        wall_ref[p] = column([w_ref[p * rows + i] for i in range(rows)], wall_ref.shape[1:])
+
+    def put(q, part):
+        for v in range(vib):
+            p = v * quarters + q
+            z_ref[p] = g * part[v * rows : (v + 1) * rows] - dd * old_ref[natural(quarters, p, width)]
+
+    angular(vib, x_ref, t_ref, v_ref, grid_ref, put)
+
+
+def first_coriolis(vib, rank_ref, za_ref, lo_ref, hi_ref, c_ref, rows_ref, z_ref, consts_ref):
+    pieces, rows, width = z_ref.shape
+    quarters = pieces // vib
     tile = (rows, width)
-    g, gw, dd = own_columns(rows, width, rank_ref, d_ref, w_ref)
-    consts_ref[0], consts_ref[1], consts_ref[2] = g, gw, dd
     below = lo_ref[pieces].astype(F32)
     own = lax.rem(rank_ref[0], quarters)
     under, over = jnp.zeros(tile, F32), jnp.zeros(tile, F32)
@@ -106,17 +120,11 @@
         upper = jnp.broadcast_to(c_ref[:, q * width : (q + 1) * width].astype(F32), tile)
         consts_ref[5 + q], consts_ref[5 + quarters + q] = lower, upper
         under, over = jnp.where(own == q, lower, under), jnp.where(own == q, upper, over)
+    for i in range(3):
+        consts_ref[i] = rows_ref[i]
     consts_ref[3], consts_ref[4] = under, over
     for p in range(pieces):
-        wall_ref[p] = column([w_ref[p * rows + i] for i in range(rows)], wall_ref.shape[1:])
-
-    def put(q, part):
-        for v in range(vib):
-            p = v * quarters + q
-            z = g * part[v * rows : (v + 1) * rows] + gw * mixed(consts_ref, p, quarters, lo_ref, hi_ref)
-            z_ref[p] = (z - dd * old_ref[natural(quarters, p, width)]).astype(BF16)
-
-    angular(vib, x_ref, t_ref, v_ref, grid_ref, put)
+        z_ref[p] = (za_ref[p] + consts_ref[1] * mixed(consts_ref, p, quarters, lo_ref, hi_ref)).astype(BF16)
 
 
 def radial(k_ref, x, pieces, put):
@@ -153,19 +161,20 @@
 
 
 def second(vib, r_ref, s_ref, k_ref, gall_ref, wall_ref, t_ref, v_ref, x0_ref, consts_ref,
-           xb_ref, cb_ref, out_ref, gwall_ref, grid_ref):
+           xb_ref, cw_ref, out_ref, cb_ref, grid_ref):
     pieces, rows, width = xb_ref.shape
-    gwall_ref[...] = gall_ref[...] * wall_ref[...]
     quarters = pieces // vib
     g, dd = consts_ref[0], consts_ref[2]
     for p in range(pieces):
         xb_ref[p] = (s_ref[p, rows:].astype(F32) + r_ref[p, :rows].astype(F32)).astype(BF16)
-        cb_ref[p] = (r_ref[p, rows:].astype(F32) + s_ref[p, :rows].astype(F32)).astype(BF16)
+        c = r_ref[p, rows:].astype(F32) + s_ref[p, :rows].astype(F32)
+        cb_ref[p * rows : (p + 1) * rows] = c.astype(BF16)
+        cw_ref[p] = (twice(gall_ref[p] * wall_ref[p]) * c).astype(BF16)
 
     def put_radial(p, y):
         out_ref[p, :rows] = (y * twice(gall_ref[p])).astype(BF16)
 
-    radial(k_ref, cb_ref[...].reshape(pieces * rows, width), pieces, put_radial)
+    radial(k_ref, cb_ref[...], pieces, put_radial)
 
     def put(q, part):
         for v in range(vib):
@@ -175,11 +184,11 @@
     angular(vib, xb_ref, t_ref, v_ref, grid_ref, put)
 
 
-def third_columns(r_ref, s_ref, lo_ref, hi_ref, consts_ref, gwall_ref, k_ref, out_ref, cb_ref):
+def third_columns(r_ref, s_ref, lo_ref, hi_ref, consts_ref, k_ref, out_ref, cb_ref):
     pieces, rows, _ = out_ref.shape
     for p in range(pieces):
         mix = consts_ref[3] * lo_ref[p].astype(F32) + consts_ref[4] * hi_ref[p].astype(F32)
-        c = r_ref[p, rows:].astype(F32) + s_ref[p, :rows].astype(F32) + twice(gwall_ref[p]) * mix
+        c = r_ref[p, rows:].astype(F32) + s_ref[p, :rows].astype(F32) + mix
         cb_ref[p * rows : (p + 1) * rows] = c.astype(BF16)
 
     def put(p, y):
@@ -250,23 +259,26 @@
     r1 = exchange(sent)
     lo, hi = neighbours(x0)
     quarters = pieces // vib
-    z0, wall, consts = call(
-        part(first_rest), [(packed, BF16), ((pieces, rows, width // 2), F32), ((5 + 2 * quarters, rows, width), F32)],
-        x0, table, pot, lo, hi, coupling, old, scalars=own, room=[grid], flops=a_flops)
+    za, wall, own_rows = call(
+        part(first_angular), [(packed, F32), ((pieces, rows, width // 2), F32), ((3, rows, width), F32)],
+        x0, table, pot, old, scalars=own, room=[grid], flops=a_flops)
+    z0, consts = call(
+        part(first_coriolis), [(packed, BF16), ((5 + 2 * quarters, rows, width), F32)],
+        za, lo, hi, coupling, own_rows, scalars=own[:1])
     gall, sent = call(
         functools.partial(first_radial), [((pieces, rows, width // 2), F32), (double, BF16)],
         kinetic, r1, z0, room=[((size, width), BF16)], flops=k_flops, grant=GRANT)
     r2 = exchange(sent)
-    x1, c1, sent, gwall = call(
-        part(second), [(packed, BF16), (packed, BF16), (double, BF16), (gall.shape, F32)],
-        r2, sent, kinetic, gall, wall, table, pot, x0, consts, room=[grid], flops=a_flops + k_flops, grant=GRANT)
+    x1, c1, sent = call(
+        part(second), [(packed, BF16), (packed, BF16), (double, BF16)],
+        r2, sent, kinetic, gall, wall, table, pot, x0, consts, room=[((size, width), BF16), grid], flops=a_flops + k_flops, grant=GRANT)
     r3 = exchange(sent)
     lo, hi = neighbours(x1)
     low, hiw = neighbours(c1)
     r3, lo, hi = lax.optimization_barrier((r3, lo, hi))
     (sent4,) = call(
         functools.partial(third_columns), [(packed, BF16)],
-        r3, sent, low, hiw, consts, gwall, kinetic, room=[((size, width), BF16)], flops=k_flops, grant=GRANT)
+        r3, sent, low, hiw, consts, kinetic, room=[((size, width), BF16)], flops=k_flops, grant=GRANT)
     r4 = exchange(sent4)
     x2, x2b = call(part(third_rows), [(old.shape, F32), (packed, BF16)], r3, sent, lo, hi, consts, grant=GRANT)
     lo, hi = neighbours(x2b)

time: 155 us -> 152 us (0.981)
  local copies, waits for them, and re-layouts: 6.97 us -> 4.59 us
  blocking collectives: 38.6 us -> 36.8 us
  Pallas kernels: 18.6 us -> 20.3 us
    ppermute x4, waiting for transfers between devices: 11.5 us -> 7.36 us  [neighbours(): lax.ppermute(array, 'hel', up)]
    all_to_all x3, waiting for transfers between devices: 32.3 us -> 36.3 us  [exchange(): return lax.all_to_all(blocks, 'rad', 0, 0, tiled=True)]
    unnamed x32 -> x24, local copies, waits for them, and re-layouts: 5.12 us -> 2.78 us
    all_to_all x1, blocking collectives: 38.6 us -> 36.8 us  [exchange(): return lax.all_to_all(blocks, 'rad', 0, 0, tiled=True)]
    pallas_call x8 -> x9, Pallas kernels: 18.6 us -> 20.3 us  [call(): pl.pallas_call(kernel, out_shape=shapes, in_specs=[pl.BlockSpec(memory_sp...]
  transfers between devices with their start and end apart: 11 -> 11, of which waited for: 7 -> 6; matrix products, arithmetic and copies ran while one was open for 1% -> 1% of each run, Pallas kernels for 7% -> 8%
where the time goes in v4:
time: 152 us; the launch traced here: 151 us
  starting transfers between devices  44.5 us (29%)
  waiting for transfers between devices  43.7 us (29%)
  blocking collectives  36.8 us (24%)
  Pallas kernels  20.3 us (13%)
  local copies, waits for them, and re-layouts  4.59 us (3%)
    all_to_all x1, blocking collectives, exchange(): return lax.all_to_all(blocks, 'rad', 0, 0, tiled=True)  36.8 us
    all_to_all x3, waiting for transfers between devices, exchange(): return lax.all_to_all(blocks, 'rad', 0, 0, tiled=True)  36.3 us
    all_to_all x3, starting transfers between devices, exchange(): return lax.all_to_all(blocks, 'rad', 0, 0, tiled=True)  24.9 us
    pallas_call x9, Pallas kernels, call(): pl.pallas_call(kernel, out_shape=shapes, in_specs=[pl.BlockSpec(memory_sp...  20.3 us
    ppermute x4, starting transfers between devices, neighbours(): lax.ppermute(array, 'hel', [(j, i) for i, j in up])  10.8 us
    ppermute x4, starting transfers between devices, neighbours(): lax.ppermute(array, 'hel', up)  8.87 us
    ppermute x4, waiting for transfers between devices, neighbours(): lax.ppermute(array, 'hel', up)  7.36 us
  transfers between devices with their start and end apart: 11, of which 6 were waited for; matrix products, arithmetic and copies ran while one was open for 1% of the time, Pallas kernels for 8%

profile of v4, /device:TPU:6, one launch (start us, length us, event | category | flops | bytes accessed | tf_op | source)
XLA Modules:
  0.0 150.8 jit_solution(10986662380798195963)
XLA Ops:
  0.6 2.4 %pack.1 = (bf16[32,40,128]{2,1,0:T(8,128)(2,1)}, bf16[33,16,256]{2,1,0:T(8,128)(2,1)}) custom-call(f32[16]{0:T(128)} %d_ref.3, f32[16,8,1024]{2,1,0:T(8,128)} %bitcast.15, bf16[1,1024]{1,0:T(2,128)(2,1)} %c_ref.3), custom_call_target="tpu_custom_call" | custom-call | flops 8994816 | bytes 1124352 | tf_op jit(solution)/shard_map/pack/pallas_call | solution.py:20
  3.0 16.7 %all-to-all-start = ((bf16[32,40,128]{2,1,0:T(8,128)(2,1)}), bf16[32,40,128]{2,1,0:T(8,128)(2,1)S(1)}, u32[]{:S(2)}, u32[]{:S(2)}) async-start(bf16[32,40,128]{2,1,0:T(8,128)(2,1)} %get-tuple-element.19), calls=%async_computation | async-start | bytes 655360 | tf_op jit(solution)/shard_map/all_to_all | solution.py:231
  19.8 2.2 %collective-permute-start.1 = (bf16[33,16,256]{2,1,0:T(8,128)(2,1)}, bf16[33,16,256]{2,1,0:T(8,128)(2,1)}, u32[]{:S(2)}, u32[]{:S(2)}) collective-permute-start(bf16[33,16,256]{2,1,0:T(8,128)(2,1)} %get-tuple-element.20.x_ref.x0_ref), channel_id=1, source_target_pairs={{32,0},{64,32},{96,64},{128,96},{160,128},{192,160},{224,192},{256... | collective-permute-start | bytes 811016 | tf_op jit(solution)/shard_map/ppermute | solution.py:237
  22.0 2.1 %collective-permute-start = (bf16[33,16,256]{2,1,0:T(8,128)(2,1)}, bf16[33,16,256]{2,1,0:T(8,128)(2,1)}, u32[]{:S(2)}, u32[]{:S(2)}) collective-permute-start(bf16[33,16,256]{2,1,0:T(8,128)(2,1)} %get-tuple-element.20.x_ref.x0_ref), channel_id=1, source_target_pairs={{0,32},{32,64},{64,96},{96,128},{128,160},{160,192},{192,224},{224... | collective-permute-start | bytes 811016 | tf_op jit(solution)/shard_map/ppermute | solution.py:237
  24.1 1.8 %copy.10 = bf16[8,16,1024]{2,1,0:T(8,128)(2,1)} copy(bf16[8,16,1024]{2,0,1:T(8,128)(2,1)} %bitcast.17) | data formatting | bytes 524288 | tf_op jit(solution)/shard_map/transpose | solution.py:249
  25.9 4.2 %first_angular.1 = (f32[32,16,256]{2,1,0:T(8,128)}, f32[32,16,128]{2,1,0:T(8,128)}, f32[3,16,256]{2,1,0:T(8,128)}) custom-call(s32[1]{0:T(128)} %bitcast.1.rank_ref, f32[16]{0:T(128)} %d_ref.3, f32[512]{0:T(512)} %w_ref.1, bf16[33,16,256]{2,1,0:T(8,128)(2,1)} %get-tuple-element.20.x_ref.x0_ref, bf16[1024,1024]{1,0:T(8,128)(2,1)} %bitcast.8, ...), custom_call_target="tpu_custom_call" | custom-call | flops 536870912 | bytes 3989504 | tf_op jit(solution)/shard_map/first_angular/pallas_call | solution.py:20
  30.1 0.0 collective-permute-done.1.hi_ref
  30.1 2.7 %collective-permute-done.lo_ref = bf16[33,16,256]{2,1,0:T(8,128)(2,1)} collective-permute-done((bf16[33,16,256]{2,1,0:T(8,128)(2,1)}, bf16[33,16,256]{2,1,0:T(8,128)(2,1)}, u32[]{:S(2)}, u32[]{:S(2)}) %collective-permute-start) | collective-permute-done | bytes 270368 | tf_op jit(solution)/shard_map/ppermute | solution.py:237
  32.8 2.0 %first_coriolis.1 = (bf16[32,16,256]{2,1,0:T(8,128)(2,1)}, f32[13,16,256]{2,1,0:T(8,128)}) custom-call(s32[1]{0:T(128)} %bitcast.1.rank_ref, f32[32,16,256]{2,1,0:T(8,128)} %get-tuple-element.21.za_ref, bf16[33,16,256]{2,1,0:T(8,128)(2,1)} %collective-permute-done.lo_ref, bf16[33,16,256]{2,1,0:T(8,128)(2,1)} %collective-permute-done.1.hi_ref, ...), custom_call_target="tpu_custom_call" | custom-call | flops 12730368 | bytes 1591296 | tf_op jit(solution)/shard_map/first_coriolis/pallas_call | solution.py:20
  34.9 9.2 %all-to-all-done.r_ref = bf16[32,40,128]{2,1,0:T(8,128)(2,1)S(1)} async-done(((bf16[32,40,128]{2,1,0:T(8,128)(2,1)}), bf16[32,40,128]{2,1,0:T(8,128)(2,1)S(1)}, u32[]{:S(2)}, u32[]{:S(2)}) %all-to-all-start) | async-done | bytes 327712 | tf_op jit(solution)/shard_map/all_to_all | solution.py:231
  44.1 1.0 copy-done.10
  45.1 0.3 first_radial.1
  45.4 36.8 %all_to_all.20.r_ref = bf16[32,32,256]{2,1,0:T(8,128)(2,1)S(1)} all-to-all(bf16[32,32,256]{2,1,0:T(8,128)(2,1)S(1)} %get-tuple-element.24.s_ref), channel_id=1, replica_groups=mesh['hel'=16,'rad'=32] {'rad'}, dimensions={0} | all-to-all | bytes 1048576 | tf_op jit(solution)/shard_map/all_to_all | solution.py:231
  82.3 2.1 %second.1 = (bf16[32,16,256]{2,1,0:T(8,128)(2,1)S(1)}, bf16[32,16,256]{2,1,0:T(8,128)(2,1)S(1)}, bf16[32,32,256]{2,1,0:T(8,128)(2,1)}) custom-call(bf16[32,32,256]{2,1,0:T(8,128)(2,1)S(1)} %all_to_all.20.r_ref, bf16[32,32,256]{2,1,0:T(8,128)(2,1)S(1)} %get-tuple-element.24.s_ref, bf16[512,512]{1,0:T(8,128)(2,1)S(1)} %copy-done.3, ...), custom_call_target="tpu_custom_call" | custom-call | flops 671088640 | bytes 5988352 | tf_op jit(solution)/shard_map/second/pallas_call | solution.py:20
  84.4 0.7 copy-done.11
  85.1 4.1 %all-to-all-start.2 = ((bf16[32,32,256]{2,1,0:T(8,128)(2,1)}), bf16[32,32,256]{2,1,0:T(8,128)(2,1)S(1)}, u32[]{:S(2)}, u32[]{:S(2)}) async-start(bf16[32,32,256]{2,1,0:T(8,128)(2,1)} %get-tuple-element.28.s_ref), calls=%async_computation.2 | async-start | bytes 1048576 | tf_op jit(solution)/shard_map/all_to_all | solution.py:231
  89.2 1.9 %collective-permute-start.3 = (bf16[32,16,256]{2,1,0:T(8,128)(2,1)S(1)}, bf16[32,16,256]{2,1,0:T(8,128)(2,1)S(1)}, u32[]{:S(2)}, u32[]{:S(2)}) collective-permute-start(bf16[32,16,256]{2,1,0:T(8,128)(2,1)S(1)} %get-tuple-element.29.x1_ref), channel_id=1, source_target_pairs={{32,0},{64,32},{96,64},{128,96},{160,128},{192,160},{224,192},{256... | collective-permute-start | bytes 786440 | tf_op jit(solution)/shard_map/ppermute | solution.py:237
  91.1 2.4 %collective-permute-start.2 = (bf16[32,16,256]{2,1,0:T(8,128)(2,1)S(1)}, bf16[32,16,256]{2,1,0:T(8,128)(2,1)S(1)}, u32[]{:S(2)}, u32[]{:S(2)}) collective-permute-start(bf16[32,16,256]{2,1,0:T(8,128)(2,1)S(1)} %get-tuple-element.29.x1_ref), channel_id=1, source_target_pairs={{0,32},{32,64},{64,96},{96,128},{128,160},{160,192},{192,224},{224... | collective-permute-start | bytes 786440 | tf_op jit(solution)/shard_map/ppermute | solution.py:237
  93.6 4.7 %collective-permute-start.5 = (bf16[32,16,256]{2,1,0:T(8,128)(2,1)}, bf16[32,16,256]{2,1,0:T(8,128)(2,1)S(1)}, u32[]{:S(2)}, u32[]{:S(2)}) collective-permute-start(bf16[32,16,256]{2,1,0:T(8,128)(2,1)} %copy-done.11), channel_id=1, source_target_pairs={{32,0},{64,32},{96,64},{128,96},{160,128},{192,160},{224,192},{256... | collective-permute-start | bytes 786440 | tf_op jit(solution)/shard_map/ppermute | solution.py:237
  98.2 1.9 %collective-permute-start.4 = (bf16[32,16,256]{2,1,0:T(8,128)(2,1)}, bf16[32,16,256]{2,1,0:T(8,128)(2,1)S(1)}, u32[]{:S(2)}, u32[]{:S(2)}) collective-permute-start(bf16[32,16,256]{2,1,0:T(8,128)(2,1)} %copy-done.11), channel_id=1, source_target_pairs={{0,32},{32,64},{64,96},{96,128},{128,160},{160,192},{192,224},{224... | collective-permute-start | bytes 786440 | tf_op jit(solution)/shard_map/ppermute | solution.py:237
  100.2 1.0 collective-permute-done.2.lo_ref
  101.1 20.6 %all-to-all-done.2.r_ref = bf16[32,32,256]{2,1,0:T(8,128)(2,1)S(1)} async-done(((bf16[32,32,256]{2,1,0:T(8,128)(2,1)}), bf16[32,32,256]{2,1,0:T(8,128)(2,1)S(1)}, u32[]{:S(2)}, u32[]{:S(2)}) %all-to-all-start.2) | async-done | bytes 524320 | tf_op jit(solution)/shard_map/all_to_all | solution.py:231
  121.7 2.2 %third_columns.1 = bf16[32,16,256]{2,1,0:T(8,128)(2,1)} custom-call(bf16[32,32,256]{2,1,0:T(8,128)(2,1)S(1)} %all-to-all-done.2.r_ref, bf16[32,32,256]{2,1,0:T(8,128)(2,1)} %get-tuple-element.28.s_ref, bf16[32,16,256]{2,1,0:T(8,128)(2,1)S(1)} %collective-permute-done.4.lo_ref, bf16[32,16,256]{2,1,0:T(8,128)(2,1)S(1)} %collective-permute-done.5.hi_ref, ...), custom_call_target="tpu_custom_call" | custom-call | flops 134217728 | bytes 2572288 | tf_op jit(solution)/shard_map/third_columns/pallas_call | solution.py:20
  123.9 4.1 %all-to-all-start.3 = ((bf16[32,16,256]{2,1,0:T(8,128)(2,1)}), bf16[32,16,256]{2,1,0:T(8,128)(2,1)S(1)}, u32[]{:S(2)}, u32[]{:S(2)}) async-start(bf16[32,16,256]{2,1,0:T(8,128)(2,1)} %third_columns.1), calls=%async_computation.3 | async-start | bytes 524288 | tf_op jit(solution)/shard_map/all_to_all | solution.py:231
  127.9 2.2 %third_rows.1 = (f32[16,8,1024]{2,1,0:T(8,128)}, bf16[32,16,256]{2,1,0:T(8,128)(2,1)S(1)}) custom-call(bf16[32,32,256]{2,1,0:T(8,128)(2,1)S(1)} %all-to-all-done.2.r_ref, bf16[32,32,256]{2,1,0:T(8,128)(2,1)} %get-tuple-element.28.s_ref, bf16[32,16,256]{2,1,0:T(8,128)(2,1)S(1)} %collective-permute-done.2.lo_ref, ...), custom_call_target="tpu_custom_call" | custom-call | flops 20578304 | bytes 2572288 | tf_op jit(solution)/shard_map/third_rows/pallas_call | solution.py:20
  130.1 2.0 %collective-permute-start.7 = (bf16[32,16,256]{2,1,0:T(8,128)(2,1)S(1)}, bf16[32,16,256]{2,1,0:T(8,128)(2,1)S(1)}, u32[]{:S(2)}, u32[]{:S(2)}) collective-permute-start(bf16[32,16,256]{2,1,0:T(8,128)(2,1)S(1)} %get-tuple-element.35.x_ref), channel_id=1, source_target_pairs={{32,0},{64,32},{96,64},{128,96},{160,128},{192,160},{224,192},{256... | collective-permute-start | bytes 786440 | tf_op jit(solution)/shard_map/ppermute | solution.py:237
  132.2 2.4 %collective-permute-start.6 = (bf16[32,16,256]{2,1,0:T(8,128)(2,1)S(1)}, bf16[32,16,256]{2,1,0:T(8,128)(2,1)S(1)}, u32[]{:S(2)}, u32[]{:S(2)}) collective-permute-start(bf16[32,16,256]{2,1,0:T(8,128)(2,1)S(1)} %get-tuple-element.35.x_ref), channel_id=1, source_target_pairs={{0,32},{32,64},{64,96},{96,128},{128,160},{160,192},{192,224},{224... | collective-permute-start | bytes 786440 | tf_op jit(solution)/shard_map/ppermute | solution.py:237
  134.6 3.7 %last_rest.1.z_ref = f32[32,16,256]{2,1,0:T(8,128)} custom-call(bf16[32,16,256]{2,1,0:T(8,128)(2,1)} %copy-done.9, bf16[1024,1024]{1,0:T(8,128)(2,1)} %bitcast.9, bf16[128,1024]{1,0:T(8,128)(2,1)} %bitcast.12, bf16[32,16,256]{2,1,0:T(8,128)(2,1)} %copy-done.7, f32[13,16,256]{2,1,0:T(8,128)} %get-tuple-element.27.consts_ref), custom_call_target="tpu_custom_call" | custom-call | flops 536870912 | bytes 3620864 | tf_op jit(solution)/shard_map/last_rest/pallas_call | solution.py:20
  138.3 3.7 %collective-permute-done.6.lo_ref = bf16[32,16,256]{2,1,0:T(8,128)(2,1)S(1)} collective-permute-done((bf16[32,16,256]{2,1,0:T(8,128)(2,1)S(1)}, bf16[32,16,256]{2,1,0:T(8,128)(2,1)S(1)}, u32[]{:S(2)}, u32[]{:S(2)}) %collective-permute-start.6) | collective-permute-done | bytes 262176 | tf_op jit(solution)/shard_map/ppermute | solution.py:237
  142.0 6.6 %all-to-all-done.3.r_ref = bf16[32,16,256]{2,1,0:T(8,128)(2,1)S(1)} async-done(((bf16[32,16,256]{2,1,0:T(8,128)(2,1)}), bf16[32,16,256]{2,1,0:T(8,128)(2,1)S(1)}, u32[]{:S(2)}, u32[]{:S(2)}) %all-to-all-start.3) | async-done | bytes 262176 | tf_op jit(solution)/shard_map/all_to_all | solution.py:231
  148.6 1.0 copy-done.5
  149.6 1.1 last.1
  (25 shorter events, 0.0 us)
Async XLA Ops:
  3.0 41.0 %all-to-all-start = ((bf16[32,40,128]{2,1,0:T(8,128)(2,1)}), bf16[32,40,128]{2,1,0:T(8,128)(2,1)S(1)}, u32[]{:S(2)}, u32[]{:S(2)}) async-start(bf16[32,40,128]{2,1,0:T(8,128)(2,1)} %get-tuple-element.19), calls=%async_computation | async-start | bytes 655360 | tf_op jit(solution)/shard_map/all_to_all | solution.py:231
  19.8 10.4 %collective-permute-start.1 = (bf16[33,16,256]{2,1,0:T(8,128)(2,1)}, bf16[33,16,256]{2,1,0:T(8,128)(2,1)}, u32[]{:S(2)}, u32[]{:S(2)}) collective-permute-start(bf16[33,16,256]{2,1,0:T(8,128)(2,1)} %get-tuple-element.20.x_ref.x0_ref), channel_id=1, source_target_pairs={{32,0},{64,32},{96,64},{128,96},{160,128},{192,160},{224,192},{256... | collective-permute-start | bytes 811016 | tf_op jit(solution)/shard_map/ppermute | solution.py:237
  22.0 10.9 %collective-permute-start = (bf16[33,16,256]{2,1,0:T(8,128)(2,1)}, bf16[33,16,256]{2,1,0:T(8,128)(2,1)}, u32[]{:S(2)}, u32[]{:S(2)}) collective-permute-start(bf16[33,16,256]{2,1,0:T(8,128)(2,1)} %get-tuple-element.20.x_ref.x0_ref), channel_id=1, source_target_pairs={{0,32},{32,64},{64,96},{96,128},{128,160},{160,192},{192,224},{224... | collective-permute-start | bytes 811016 | tf_op jit(solution)/shard_map/ppermute | solution.py:237
  25.9 18.2 %copy-start.3 = (bf16[512,512]{1,0:T(8,128)(2,1)S(1)}, bf16[512,512]{1,0:T(8,128)(2,1)}, u32[]{:S(2)}) copy-start(bf16[512,512]{1,0:T(8,128)(2,1)} %k_ref.5) | copy-start | bytes 1572868
  30.1 52.2 %copy-start = (bf16[1,1024,1024]{2,1,0:T(8,128)(2,1)S(1)}, bf16[1,1024,1024]{2,1,0:T(8,128)(2,1)}, u32[]{:S(2)}) copy-start(bf16[1,1024,1024]{2,1,0:T(8,128)(2,1)} %param.11) | copy-start | bytes 6291460
  30.1 52.2 %copy-start.4 = (bf16[8,16,1024]{2,1,0:T(8,128)(2,1)S(1)}, bf16[8,16,1024]{2,1,0:T(8,128)(2,1)}, u32[]{:S(2)}) copy-start(bf16[8,16,1024]{2,1,0:T(8,128)(2,1)} %copy.10) | copy-start | bytes 786436
  34.9 47.4 %copy-start.1 = (f32[13,16,256]{2,1,0:T(8,128)S(1)}, f32[13,16,256]{2,1,0:T(8,128)}, u32[]{:S(2)}) copy-start(f32[13,16,256]{2,1,0:T(8,128)} %get-tuple-element.27.consts_ref) | copy-start | bytes 638980
  44.1 38.2 %copy-start.6 = (bf16[33,16,256]{2,1,0:T(8,128)(2,1)S(1)}, bf16[33,16,256]{2,1,0:T(8,128)(2,1)}, u32[]{:S(2)}) copy-start(bf16[33,16,256]{2,1,0:T(8,128)(2,1)} %get-tuple-element.20.x_ref.x0_ref) | copy-start | bytes 811012
  44.1 38.2 %copy-start.8 = (f32[32,16,128]{2,1,0:T(8,128)S(1)}, f32[32,16,128]{2,1,0:T(8,128)}, u32[]{:S(2)}) copy-start(f32[32,16,128]{2,1,0:T(8,128)} %get-tuple-element.26.wall_ref) | copy-start | bytes 786436
  44.1 1.0 copy-start.10
  84.4 0.7 copy-start.11
  85.1 45.0 %copy-start.7 = (bf16[32,16,256]{2,1,0:T(8,128)(2,1)}, bf16[32,16,256]{2,1,0:T(8,128)(2,1)S(1)}, u32[]{:S(2)}) copy-start(bf16[32,16,256]{2,1,0:T(8,128)(2,1)S(1)} %get-tuple-element.29.x1_ref) | copy-start | bytes 786436
  85.1 36.5 %all-to-all-start.2 = ((bf16[32,32,256]{2,1,0:T(8,128)(2,1)}), bf16[32,32,256]{2,1,0:T(8,128)(2,1)S(1)}, u32[]{:S(2)}, u32[]{:S(2)}) async-start(bf16[32,32,256]{2,1,0:T(8,128)(2,1)} %get-tuple-element.28.s_ref), calls=%async_computation.2 | async-start | bytes 1048576 | tf_op jit(solution)/shard_map/all_to_all | solution.py:231
  89.2 10.9 %collective-permute-start.3 = (bf16[32,16,256]{2,1,0:T(8,128)(2,1)S(1)}, bf16[32,16,256]{2,1,0:T(8,128)(2,1)S(1)}, u32[]{:S(2)}, u32[]{:S(2)}) collective-permute-start(bf16[32,16,256]{2,1,0:T(8,128)(2,1)S(1)} %get-tuple-element.29.x1_ref), channel_id=1, source_target_pairs={{32,0},{64,32},{96,64},{128,96},{160,128},{192,160},{224,192},{256... | collective-permute-start | bytes 786440 | tf_op jit(solution)/shard_map/ppermute | solution.py:237
  91.1 10.0 %collective-permute-start.2 = (bf16[32,16,256]{2,1,0:T(8,128)(2,1)S(1)}, bf16[32,16,256]{2,1,0:T(8,128)(2,1)S(1)}, u32[]{:S(2)}, u32[]{:S(2)}) collective-permute-start(bf16[32,16,256]{2,1,0:T(8,128)(2,1)S(1)} %get-tuple-element.29.x1_ref), channel_id=1, source_target_pairs={{0,32},{32,64},{64,96},{96,128},{128,160},{160,192},{192,224},{224... | collective-permute-start | bytes 786440 | tf_op jit(solution)/shard_map/ppermute | solution.py:237
  93.6 28.1 %collective-permute-start.5 = (bf16[32,16,256]{2,1,0:T(8,128)(2,1)}, bf16[32,16,256]{2,1,0:T(8,128)(2,1)S(1)}, u32[]{:S(2)}, u32[]{:S(2)}) collective-permute-start(bf16[32,16,256]{2,1,0:T(8,128)(2,1)} %copy-done.11), channel_id=1, source_target_pairs={{32,0},{64,32},{96,64},{128,96},{160,128},{192,160},{224,192},{256... | collective-permute-start | bytes 786440 | tf_op jit(solution)/shard_map/ppermute | solution.py:237
  98.2 23.5 %collective-permute-start.4 = (bf16[32,16,256]{2,1,0:T(8,128)(2,1)}, bf16[32,16,256]{2,1,0:T(8,128)(2,1)S(1)}, u32[]{:S(2)}, u32[]{:S(2)}) collective-permute-start(bf16[32,16,256]{2,1,0:T(8,128)(2,1)} %copy-done.11), channel_id=1, source_target_pairs={{0,32},{32,64},{64,96},{96,128},{128,160},{160,192},{192,224},{224... | collective-permute-start | bytes 786440 | tf_op jit(solution)/shard_map/ppermute | solution.py:237
  123.9 24.7 %all-to-all-start.3 = ((bf16[32,16,256]{2,1,0:T(8,128)(2,1)}), bf16[32,16,256]{2,1,0:T(8,128)(2,1)S(1)}, u32[]{:S(2)}, u32[]{:S(2)}) async-start(bf16[32,16,256]{2,1,0:T(8,128)(2,1)} %third_columns.1), calls=%async_computation.3 | async-start | bytes 524288 | tf_op jit(solution)/shard_map/all_to_all | solution.py:231
  130.1 4.5 %copy-start.9 = (bf16[32,16,256]{2,1,0:T(8,128)(2,1)}, bf16[32,16,256]{2,1,0:T(8,128)(2,1)S(1)}, u32[]{:S(2)}) copy-start(bf16[32,16,256]{2,1,0:T(8,128)(2,1)S(1)} %get-tuple-element.35.x_ref) | copy-start | bytes 786436
  130.1 18.5 %copy-start.2 = (f32[13,16,256]{2,1,0:T(8,128)S(1)}, f32[13,16,256]{2,1,0:T(8,128)}, u32[]{:S(2)}) copy-start(f32[13,16,256]{2,1,0:T(8,128)} %get-tuple-element.27.consts_ref) | copy-start | bytes 638980
  130.1 8.2 %collective-permute-start.7 = (bf16[32,16,256]{2,1,0:T(8,128)(2,1)S(1)}, bf16[32,16,256]{2,1,0:T(8,128)(2,1)S(1)}, u32[]{:S(2)}, u32[]{:S(2)}) collective-permute-start(bf16[32,16,256]{2,1,0:T(8,128)(2,1)S(1)} %get-tuple-element.35.x_ref), channel_id=1, source_target_pairs={{32,0},{64,32},{96,64},{128,96},{160,128},{192,160},{224,192},{256... | collective-permute-start | bytes 786440 | tf_op jit(solution)/shard_map/ppermute | solution.py:237
  132.2 9.9 %collective-permute-start.6 = (bf16[32,16,256]{2,1,0:T(8,128)(2,1)S(1)}, bf16[32,16,256]{2,1,0:T(8,128)(2,1)S(1)}, u32[]{:S(2)}, u32[]{:S(2)}) collective-permute-start(bf16[32,16,256]{2,1,0:T(8,128)(2,1)S(1)} %get-tuple-element.35.x_ref), channel_id=1, source_target_pairs={{0,32},{32,64},{64,96},{96,128},{128,160},{160,192},{192,224},{224... | collective-permute-start | bytes 786440 | tf_op jit(solution)/shard_map/ppermute | solution.py:237
  148.6 1.0 copy-start.5

commit v5 on v4

--- a/solution.py
+++ b/solution.py
@@ -53,10 +53,11 @@
     pieces -= 1
     quarters, half = pieces // vib, width // 2
     for p in range(pieces):
-        x = x_ref[natural(quarters, p, width)].astype(BF16)
-        x0_ref[p] = x
-        sent_ref[p, :rows] = x[:, :half]
-        sent_ref[p, rows : 2 * rows] = x[:, half:]
+        for h in range(2):
+            first = (p % quarters * 2 + h) * vib + p // quarters
+            x = x_ref[pl.ds(first, rows, stride=2 * quarters * vib), :].astype(BF16)
+            x0_ref[p, :, h * half : (h + 1) * half] = x
+            sent_ref[p, h * rows : (h + 1) * rows] = x
     c = c_ref[...].astype(F32)
     x0_ref[pieces] = column([c[:, q * width : (q + 1) * width] for q in range(quarters)], (rows, width)).astype(BF16)
     tile = (rows // 2, half)
@@ -184,12 +185,20 @@
     angular(vib, xb_ref, t_ref, v_ref, grid_ref, put)
 
 
-def third_columns(r_ref, s_ref, lo_ref, hi_ref, consts_ref, k_ref, out_ref, cb_ref):
+def third_ahead(vib, s_ref, lo_ref, hi_ref, low_ref, hiw_ref, consts_ref, zr_ref, zc_ref):
+    pieces, rows, width = zr_ref.shape
+    quarters = pieces // vib
+    for p in range(pieces):
+        mix = mixed(consts_ref, p, quarters, lo_ref, hi_ref)
+        zr_ref[p] = (s_ref[p, rows:].astype(F32) + consts_ref[1] * mix).astype(BF16)
+        mix = consts_ref[3] * low_ref[p].astype(F32) + consts_ref[4] * hiw_ref[p].astype(F32)
+        zc_ref[p] = (s_ref[p, :rows].astype(F32) + mix).astype(BF16)
+
+
+def third_columns(r_ref, z_ref, k_ref, out_ref, cb_ref):
     pieces, rows, _ = out_ref.shape
     for p in range(pieces):
-        mix = consts_ref[3] * lo_ref[p].astype(F32) + consts_ref[4] * hi_ref[p].astype(F32)
-        c = r_ref[p, rows:].astype(F32) + s_ref[p, :rows].astype(F32) + mix
-        cb_ref[p * rows : (p + 1) * rows] = c.astype(BF16)
+        cb_ref[p * rows : (p + 1) * rows] = (r_ref[p, rows:].astype(F32) + z_ref[p].astype(F32)).astype(BF16)
 
     def put(p, y):
         out_ref[p] = y.astype(BF16)
@@ -197,13 +206,11 @@
     radial(k_ref, cb_ref[...], pieces, put)
 
 
-def third_rows(vib, r_ref, s_ref, lo_ref, hi_ref, consts_ref, x2_ref, xb_ref):
+def third_rows(vib, r_ref, z_ref, x2_ref, xb_ref):
     pieces, rows, width = xb_ref.shape
-    quarters = pieces // vib
-    for p in range(pieces):
-        x = s_ref[p, rows:].astype(F32) + r_ref[p, :rows].astype(F32)
-        x = x + consts_ref[1] * mixed(consts_ref, p, quarters, lo_ref, hi_ref)
-        x2_ref[natural(quarters, p, width)] = x
+    for p in range(pieces):
+        x = z_ref[p].astype(F32) + r_ref[p, :rows].astype(F32)
+        x2_ref[natural(pieces // vib, p, width)] = x
         xb_ref[p] = x.astype(BF16)
 
 
@@ -244,7 +251,8 @@
     size = rows * pieces
     flat = (rows * vib, ang)
     packed, double = (pieces, rows, width), (pieces, 2 * rows, width)
-    old, new = older[0], newer[0]
+    old = older[0]
+    tiles = newer.reshape(rows, vib, -1, width // 2).transpose(0, 2, 1, 3).reshape(-1, width // 2)
     table = transform[0]
     pot = jnp.swapaxes(potential, 0, 1).reshape(flat)
     own = (lax.axis_index("rad").astype(jnp.int32).reshape(1), damping, radial_weight)
@@ -255,7 +263,7 @@
 
     sent, x0 = call(
         part(pack), [((pieces, 5 * rows // 2, width // 2), BF16), ((pieces + 1, rows, width), BF16)],
-        new, coupling, scalars=(damping,))
+        tiles, coupling, scalars=(damping,))
     r1 = exchange(sent)
     lo, hi = neighbours(x0)
     quarters = pieces // vib
@@ -275,12 +283,14 @@
     r3 = exchange(sent)
     lo, hi = neighbours(x1)
     low, hiw = neighbours(c1)
-    r3, lo, hi = lax.optimization_barrier((r3, lo, hi))
+    zr, zc = call(
+        part(third_ahead), [(packed, BF16), (packed, BF16)], sent, lo, hi, low, hiw, consts, grant=GRANT)
+    r3, zr, zc = lax.optimization_barrier((r3, zr, zc))
     (sent4,) = call(
         functools.partial(third_columns), [(packed, BF16)],
-        r3, sent, low, hiw, consts, kinetic, room=[((size, width), BF16)], flops=k_flops, grant=GRANT)
+        r3, zc, kinetic, room=[((size, width), BF16)], flops=k_flops, grant=GRANT)
     r4 = exchange(sent4)
-    x2, x2b = call(part(third_rows), [(old.shape, F32), (packed, BF16)], r3, sent, lo, hi, consts, grant=GRANT)
+    x2, x2b = call(part(third_rows), [(old.shape, F32), (packed, BF16)], r3, zr, grant=GRANT)
     lo, hi = neighbours(x2b)
     (z2,) = call(part(last_rest), [(packed, F32)], x2b, table, pot, x1, consts, room=[grid], flops=a_flops)
     (x3,) = call(part(last), [(old.shape, F32)], r4, z2, lo, hi, consts, grant=GRANT)

time: 152 us -> 150 us (0.987)
  Pallas kernels: 20.3 us -> 17.3 us
  local copies, waits for them, and re-layouts: 4.59 us -> 6.41 us
    all_to_all x3, waiting for transfers between devices: 36.3 us -> 29.3 us  [exchange(): return lax.all_to_all(blocks, 'rad', 0, 0, tiled=True)]
    ppermute x4, waiting for transfers between devices: 7.36 us -> 11.6 us  [neighbours(): lax.ppermute(array, 'hel', up)]
    pallas_call x9 -> x10, Pallas kernels: 20.3 us -> 17.3 us  [call(): pl.pallas_call(kernel, out_shape=shapes, in_specs=[pl.BlockSpec(memory_sp...]
    ppermute x4, waiting for transfers between devices: 0.01 us -> 2.89 us  [neighbours(): lax.ppermute(array, 'hel', [(j, i) for i, j in up])]
    unnamed x24 -> x28, local copies, waits for them, and re-layouts: 2.78 us -> 4.61 us
  transfers between devices with their start and end apart: 11 -> 11, of which waited for: 6 -> 8; matrix products, arithmetic and copies ran while one was open for 1% -> 1% of each run, Pallas kernels for 8% -> 8%
where the time goes in v5:
time: 150 us; the launch traced here: 149 us
  starting transfers between devices  44.3 us (30%)
  waiting for transfers between devices  43.7 us (29%)
  blocking collectives  36.9 us (25%)
  Pallas kernels  17.3 us (12%)
  local copies, waits for them, and re-layouts  6.41 us (4%)
    all_to_all x1, blocking collectives, exchange(): return lax.all_to_all(blocks, 'rad', 0, 0, tiled=True)  36.9 us
    all_to_all x3, waiting for transfers between devices, exchange(): return lax.all_to_all(blocks, 'rad', 0, 0, tiled=True)  29.3 us
    all_to_all x3, starting transfers between devices, exchange(): return lax.all_to_all(blocks, 'rad', 0, 0, tiled=True)  24.8 us
    pallas_call x10, Pallas kernels, call(): pl.pallas_call(kernel, out_shape=shapes, in_specs=[pl.BlockSpec(memory_sp...  17.3 us
    ppermute x4, waiting for transfers between devices, neighbours(): lax.ppermute(array, 'hel', up)  11.6 us
    ppermute x4, starting transfers between devices, neighbours(): lax.ppermute(array, 'hel', [(j, i) for i, j in up])  10.7 us
    ppermute x4, starting transfers between devices, neighbours(): lax.ppermute(array, 'hel', up)  8.87 us
    unnamed x28, local copies, waits for them, and re-layouts  4.61 us
  transfers between devices with their start and end apart: 11, of which 8 were waited for; matrix products, arithmetic and copies ran while one was open for 1% of the time, Pallas kernels for 8%

profile of v5, /device:TPU:6, one launch (start us, length us, event | category | flops | bytes accessed | tf_op | source)
XLA Modules:
  0.0 149.5 jit_solution(335846816718797380)
XLA Ops:
  0.6 2.2 %pack.1 = (bf16[32,40,128]{2,1,0:T(8,128)(2,1)}, bf16[33,16,256]{2,1,0:T(8,128)(2,1)}) custom-call(f32[16]{0:T(128)} %d_ref.3, f32[1024,128]{1,0:T(8,128)} %bitcast.19, bf16[1,1024]{1,0:T(2,128)(2,1)} %c_ref.3), custom_call_target="tpu_custom_call" | custom-call | flops 8994816 | bytes 1124352 | tf_op jit(solution)/shard_map/pack/pallas_call | solution.py:20
  2.8 16.7 %all-to-all-start = ((bf16[32,40,128]{2,1,0:T(8,128)(2,1)}), bf16[32,40,128]{2,1,0:T(8,128)(2,1)S(1)}, u32[]{:S(2)}, u32[]{:S(2)}) async-start(bf16[32,40,128]{2,1,0:T(8,128)(2,1)} %get-tuple-element.21), calls=%async_computation | async-start | bytes 655360 | tf_op jit(solution)/shard_map/all_to_all | solution.py:238
  19.5 2.2 %collective-permute-start.1 = (bf16[33,16,256]{2,1,0:T(8,128)(2,1)}, bf16[33,16,256]{2,1,0:T(8,128)(2,1)}, u32[]{:S(2)}, u32[]{:S(2)}) collective-permute-start(bf16[33,16,256]{2,1,0:T(8,128)(2,1)} %get-tuple-element.22.x_ref.x0_ref), channel_id=1, source_target_pairs={{32,0},{64,32},{96,64},{128,96},{160,128},{192,160},{224,192},{256... | collective-permute-start | bytes 811016 | tf_op jit(solution)/shard_map/ppermute | solution.py:244
  21.7 2.1 %collective-permute-start = (bf16[33,16,256]{2,1,0:T(8,128)(2,1)}, bf16[33,16,256]{2,1,0:T(8,128)(2,1)}, u32[]{:S(2)}, u32[]{:S(2)}) collective-permute-start(bf16[33,16,256]{2,1,0:T(8,128)(2,1)} %get-tuple-element.22.x_ref.x0_ref), channel_id=1, source_target_pairs={{0,32},{32,64},{64,96},{96,128},{128,160},{160,192},{192,224},{224... | collective-permute-start | bytes 811016 | tf_op jit(solution)/shard_map/ppermute | solution.py:244
  23.9 1.8 %copy.10 = bf16[8,16,1024]{2,1,0:T(8,128)(2,1)} copy(bf16[8,16,1024]{2,0,1:T(8,128)(2,1)} %bitcast.21) | data formatting | bytes 524288 | tf_op jit(solution)/shard_map/transpose | solution.py:257
  25.7 4.2 %first_angular.1 = (f32[32,16,256]{2,1,0:T(8,128)}, f32[32,16,128]{2,1,0:T(8,128)}, f32[3,16,256]{2,1,0:T(8,128)}) custom-call(s32[1]{0:T(128)} %bitcast.3.rank_ref, f32[16]{0:T(128)} %d_ref.3, f32[512]{0:T(512)} %w_ref.1, bf16[33,16,256]{2,1,0:T(8,128)(2,1)} %get-tuple-element.22.x_ref.x0_ref, bf16[1024,1024]{1,0:T(8,128)(2,1)} %bitcast.12, ...), custom_call_target="tpu_custom_call" | custom-call | flops 536870912 | bytes 3989504 | tf_op jit(solution)/shard_map/first_angular/pallas_call | solution.py:20
  29.9 2.7 %collective-permute-done.lo_ref = bf16[33,16,256]{2,1,0:T(8,128)(2,1)} collective-permute-done((bf16[33,16,256]{2,1,0:T(8,128)(2,1)}, bf16[33,16,256]{2,1,0:T(8,128)(2,1)}, u32[]{:S(2)}, u32[]{:S(2)}) %collective-permute-start) | collective-permute-done | bytes 270368 | tf_op jit(solution)/shard_map/ppermute | solution.py:244
  32.6 2.0 %first_coriolis.1 = (bf16[32,16,256]{2,1,0:T(8,128)(2,1)}, f32[13,16,256]{2,1,0:T(8,128)}) custom-call(s32[1]{0:T(128)} %bitcast.3.rank_ref, f32[32,16,256]{2,1,0:T(8,128)} %get-tuple-element.23.za_ref, bf16[33,16,256]{2,1,0:T(8,128)(2,1)} %collective-permute-done.lo_ref, bf16[33,16,256]{2,1,0:T(8,128)(2,1)} %collective-permute-done.1.hi_ref, ...), custom_call_target="tpu_custom_call" | custom-call | flops 12730368 | bytes 1591296 | tf_op jit(solution)/shard_map/first_coriolis/pallas_call | solution.py:20
  34.6 9.2 %all-to-all-done.r_ref = bf16[32,40,128]{2,1,0:T(8,128)(2,1)S(1)} async-done(((bf16[32,40,128]{2,1,0:T(8,128)(2,1)}), bf16[32,40,128]{2,1,0:T(8,128)(2,1)S(1)}, u32[]{:S(2)}, u32[]{:S(2)}) %all-to-all-start) | async-done | bytes 327712 | tf_op jit(solution)/shard_map/all_to_all | solution.py:238
  43.9 1.0 copy-done.12
  45.2 36.9 %all_to_all.20.r_ref = bf16[32,32,256]{2,1,0:T(8,128)(2,1)S(1)} all-to-all(bf16[32,32,256]{2,1,0:T(8,128)(2,1)S(1)} %get-tuple-element.26.s_ref), channel_id=1, replica_groups=mesh['hel'=16,'rad'=32] {'rad'}, dimensions={0} | all-to-all | bytes 1048576 | tf_op jit(solution)/shard_map/all_to_all | solution.py:238
  82.2 1.3 second.1
  85.0 4.0 %all-to-all-start.2 = ((bf16[32,32,256]{2,1,0:T(8,128)(2,1)}), bf16[32,32,256]{2,1,0:T(8,128)(2,1)S(1)}, u32[]{:S(2)}, u32[]{:S(2)}) async-start(bf16[32,32,256]{2,1,0:T(8,128)(2,1)} %copy-done.5), calls=%async_computation.2 | async-start | bytes 1048576 | tf_op jit(solution)/shard_map/all_to_all | solution.py:238
  89.0 1.9 %collective-permute-start.5 = (bf16[32,16,256]{2,1,0:T(8,128)(2,1)}, bf16[32,16,256]{2,1,0:T(8,128)(2,1)S(1)}, u32[]{:S(2)}, u32[]{:S(2)}) collective-permute-start(bf16[32,16,256]{2,1,0:T(8,128)(2,1)} %copy-done.13), channel_id=1, source_target_pairs={{32,0},{64,32},{96,64},{128,96},{160,128},{192,160},{224,192},{256... | collective-permute-start | bytes 786440 | tf_op jit(solution)/shard_map/ppermute | solution.py:244
  90.9 2.4 %collective-permute-start.4 = (bf16[32,16,256]{2,1,0:T(8,128)(2,1)}, bf16[32,16,256]{2,1,0:T(8,128)(2,1)S(1)}, u32[]{:S(2)}, u32[]{:S(2)}) collective-permute-start(bf16[32,16,256]{2,1,0:T(8,128)(2,1)} %copy-done.13), channel_id=1, source_target_pairs={{0,32},{32,64},{64,96},{96,128},{128,160},{160,192},{192,224},{224... | collective-permute-start | bytes 786440 | tf_op jit(solution)/shard_map/ppermute | solution.py:244
  93.4 4.7 %collective-permute-start.3 = (bf16[32,16,256]{2,1,0:T(8,128)(2,1)S(1)}, bf16[32,16,256]{2,1,0:T(8,128)(2,1)S(1)}, u32[]{:S(2)}, u32[]{:S(2)}) collective-permute-start(bf16[32,16,256]{2,1,0:T(8,128)(2,1)S(1)} %get-tuple-element.31.x1_ref), channel_id=1, source_target_pairs={{32,0},{64,32},{96,64},{128,96},{160,128},{192,160},{224,192},{256... | collective-permute-start | bytes 786440 | tf_op jit(solution)/shard_map/ppermute | solution.py:244
  98.0 1.9 %collective-permute-start.2 = (bf16[32,16,256]{2,1,0:T(8,128)(2,1)S(1)}, bf16[32,16,256]{2,1,0:T(8,128)(2,1)S(1)}, u32[]{:S(2)}, u32[]{:S(2)}) collective-permute-start(bf16[32,16,256]{2,1,0:T(8,128)(2,1)S(1)} %get-tuple-element.31.x1_ref), channel_id=1, source_target_pairs={{0,32},{32,64},{64,96},{96,128},{128,160},{160,192},{192,224},{224... | collective-permute-start | bytes 786440 | tf_op jit(solution)/shard_map/ppermute | solution.py:244
  100.0 1.1 collective-permute-done.4.low_ref
  101.0 2.9 %collective-permute-done.3.hi_ref = bf16[32,16,256]{2,1,0:T(8,128)(2,1)S(1)} collective-permute-done((bf16[32,16,256]{2,1,0:T(8,128)(2,1)S(1)}, bf16[32,16,256]{2,1,0:T(8,128)(2,1)S(1)}, u32[]{:S(2)}, u32[]{:S(2)}) %collective-permute-start.3) | collective-permute-done | bytes 262176 | tf_op jit(solution)/shard_map/ppermute | solution.py:244
  103.9 4.1 %collective-permute-done.2.lo_ref = bf16[32,16,256]{2,1,0:T(8,128)(2,1)S(1)} collective-permute-done((bf16[32,16,256]{2,1,0:T(8,128)(2,1)S(1)}, bf16[32,16,256]{2,1,0:T(8,128)(2,1)S(1)}, u32[]{:S(2)}, u32[]{:S(2)}) %collective-permute-start.2) | collective-permute-done | bytes 262176 | tf_op jit(solution)/shard_map/ppermute | solution.py:244
  108.0 1.0 copy-done.6
  109.3 12.2 %all-to-all-done.2.r_ref = bf16[32,32,256]{2,1,0:T(8,128)(2,1)S(1)} async-done(((bf16[32,32,256]{2,1,0:T(8,128)(2,1)}), bf16[32,32,256]{2,1,0:T(8,128)(2,1)S(1)}, u32[]{:S(2)}, u32[]{:S(2)}) %all-to-all-start.2) | async-done | bytes 524320 | tf_op jit(solution)/shard_map/all_to_all | solution.py:238
  121.5 1.0 third_columns.1
  122.5 4.1 %all-to-all-start.3 = ((bf16[32,16,256]{2,1,0:T(8,128)(2,1)}), bf16[32,16,256]{2,1,0:T(8,128)(2,1)S(1)}, u32[]{:S(2)}, u32[]{:S(2)}) async-start(bf16[32,16,256]{2,1,0:T(8,128)(2,1)} %third_columns.1), calls=%async_computation.3 | async-start | bytes 524288 | tf_op jit(solution)/shard_map/all_to_all | solution.py:238
  126.6 1.1 third_rows.1
  127.7 1.9 %collective-permute-start.7 = (bf16[32,16,256]{2,1,0:T(8,128)(2,1)S(1)}, bf16[32,16,256]{2,1,0:T(8,128)(2,1)S(1)}, u32[]{:S(2)}, u32[]{:S(2)}) collective-permute-start(bf16[32,16,256]{2,1,0:T(8,128)(2,1)S(1)} %get-tuple-element.39.x_ref), channel_id=1, source_target_pairs={{32,0},{64,32},{96,64},{128,96},{160,128},{192,160},{224,192},{256... | collective-permute-start | bytes 786440 | tf_op jit(solution)/shard_map/ppermute | solution.py:244
  129.6 2.4 %collective-permute-start.6 = (bf16[32,16,256]{2,1,0:T(8,128)(2,1)S(1)}, bf16[32,16,256]{2,1,0:T(8,128)(2,1)S(1)}, u32[]{:S(2)}, u32[]{:S(2)}) collective-permute-start(bf16[32,16,256]{2,1,0:T(8,128)(2,1)S(1)} %get-tuple-element.39.x_ref), channel_id=1, source_target_pairs={{0,32},{32,64},{64,96},{96,128},{128,160},{160,192},{192,224},{224... | collective-permute-start | bytes 786440 | tf_op jit(solution)/shard_map/ppermute | solution.py:244
  132.0 3.7 %last_rest.1.z_ref = f32[32,16,256]{2,1,0:T(8,128)} custom-call(bf16[32,16,256]{2,1,0:T(8,128)(2,1)} %copy-done.11, bf16[1024,1024]{1,0:T(8,128)(2,1)} %bitcast.13, bf16[128,1024]{1,0:T(8,128)(2,1)} %bitcast.16, bf16[32,16,256]{2,1,0:T(8,128)(2,1)} %copy-done.9, f32[13,16,256]{2,1,0:T(8,128)} %get-tuple-element.29.consts_ref), custom_call_target="tpu_custom_call" | custom-call | flops 536870912 | bytes 3620864 | tf_op jit(solution)/shard_map/last_rest/pallas_call | solution.py:20
  135.7 3.7 %collective-permute-done.6.lo_ref = bf16[32,16,256]{2,1,0:T(8,128)(2,1)S(1)} collective-permute-done((bf16[32,16,256]{2,1,0:T(8,128)(2,1)S(1)}, bf16[32,16,256]{2,1,0:T(8,128)(2,1)S(1)}, u32[]{:S(2)}, u32[]{:S(2)}) %collective-permute-start.6) | collective-permute-done | bytes 262176 | tf_op jit(solution)/shard_map/ppermute | solution.py:244
  139.4 7.9 %all-to-all-done.3.r_ref = bf16[32,16,256]{2,1,0:T(8,128)(2,1)S(1)} async-done(((bf16[32,16,256]{2,1,0:T(8,128)(2,1)}), bf16[32,16,256]{2,1,0:T(8,128)(2,1)S(1)}, u32[]{:S(2)}, u32[]{:S(2)}) %all-to-all-start.3) | async-done | bytes 262176 | tf_op jit(solution)/shard_map/all_to_all | solution.py:238
  147.3 1.0 copy-done.7
  148.4 1.1 last.1
  (30 shorter events, 2.1 us)
Async XLA Ops:
  2.8 41.0 %all-to-all-start = ((bf16[32,40,128]{2,1,0:T(8,128)(2,1)}), bf16[32,40,128]{2,1,0:T(8,128)(2,1)S(1)}, u32[]{:S(2)}, u32[]{:S(2)}) async-start(bf16[32,40,128]{2,1,0:T(8,128)(2,1)} %get-tuple-element.21), calls=%async_computation | async-start | bytes 655360 | tf_op jit(solution)/shard_map/all_to_all | solution.py:238
  19.5 10.4 %collective-permute-start.1 = (bf16[33,16,256]{2,1,0:T(8,128)(2,1)}, bf16[33,16,256]{2,1,0:T(8,128)(2,1)}, u32[]{:S(2)}, u32[]{:S(2)}) collective-permute-start(bf16[33,16,256]{2,1,0:T(8,128)(2,1)} %get-tuple-element.22.x_ref.x0_ref), channel_id=1, source_target_pairs={{32,0},{64,32},{96,64},{128,96},{160,128},{192,160},{224,192},{256... | collective-permute-start | bytes 811016 | tf_op jit(solution)/shard_map/ppermute | solution.py:244
  21.7 10.9 %collective-permute-start = (bf16[33,16,256]{2,1,0:T(8,128)(2,1)}, bf16[33,16,256]{2,1,0:T(8,128)(2,1)}, u32[]{:S(2)}, u32[]{:S(2)}) collective-permute-start(bf16[33,16,256]{2,1,0:T(8,128)(2,1)} %get-tuple-element.22.x_ref.x0_ref), channel_id=1, source_target_pairs={{0,32},{32,64},{64,96},{96,128},{128,160},{160,192},{192,224},{224... | collective-permute-start | bytes 811016 | tf_op jit(solution)/shard_map/ppermute | solution.py:244
  25.7 18.2 %copy-start.1 = (bf16[512,512]{1,0:T(8,128)(2,1)S(1)}, bf16[512,512]{1,0:T(8,128)(2,1)}, u32[]{:S(2)}) copy-start(bf16[512,512]{1,0:T(8,128)(2,1)} %k_ref.5) | copy-start | bytes 1572868
  29.9 52.2 %copy-start = (bf16[1,1024,1024]{2,1,0:T(8,128)(2,1)S(1)}, bf16[1,1024,1024]{2,1,0:T(8,128)(2,1)}, u32[]{:S(2)}) copy-start(bf16[1,1024,1024]{2,1,0:T(8,128)(2,1)} %param.11) | copy-start | bytes 6291460
  29.9 52.2 %copy-start.2 = (bf16[8,16,1024]{2,1,0:T(8,128)(2,1)S(1)}, bf16[8,16,1024]{2,1,0:T(8,128)(2,1)}, u32[]{:S(2)}) copy-start(bf16[8,16,1024]{2,1,0:T(8,128)(2,1)} %copy.10) | copy-start | bytes 786436
  34.6 47.5 %copy-start.3 = (f32[13,16,256]{2,1,0:T(8,128)S(1)}, f32[13,16,256]{2,1,0:T(8,128)}, u32[]{:S(2)}) copy-start(f32[13,16,256]{2,1,0:T(8,128)} %get-tuple-element.29.consts_ref) | copy-start | bytes 638980
  43.9 38.3 %copy-start.8 = (bf16[33,16,256]{2,1,0:T(8,128)(2,1)S(1)}, bf16[33,16,256]{2,1,0:T(8,128)(2,1)}, u32[]{:S(2)}) copy-start(bf16[33,16,256]{2,1,0:T(8,128)(2,1)} %get-tuple-element.22.x_ref.x0_ref) | copy-start | bytes 811012
  43.9 38.3 %copy-start.10 = (f32[32,16,128]{2,1,0:T(8,128)S(1)}, f32[32,16,128]{2,1,0:T(8,128)}, u32[]{:S(2)}) copy-start(f32[32,16,128]{2,1,0:T(8,128)} %get-tuple-element.28.wall_ref) | copy-start | bytes 786436
  43.9 1.0 copy-start.12
  83.5 0.8 copy-start.5
  84.3 0.7 copy-start.13
  85.0 37.5 %copy-start.9 = (bf16[32,16,256]{2,1,0:T(8,128)(2,1)}, bf16[32,16,256]{2,1,0:T(8,128)(2,1)S(1)}, u32[]{:S(2)}) copy-start(bf16[32,16,256]{2,1,0:T(8,128)(2,1)S(1)} %get-tuple-element.31.x1_ref) | copy-start | bytes 786436
  85.0 36.5 %all-to-all-start.2 = ((bf16[32,32,256]{2,1,0:T(8,128)(2,1)}), bf16[32,32,256]{2,1,0:T(8,128)(2,1)S(1)}, u32[]{:S(2)}, u32[]{:S(2)}) async-start(bf16[32,32,256]{2,1,0:T(8,128)(2,1)} %copy-done.5), calls=%async_computation.2 | async-start | bytes 1048576 | tf_op jit(solution)/shard_map/all_to_all | solution.py:238
  89.0 10.9 %collective-permute-start.5 = (bf16[32,16,256]{2,1,0:T(8,128)(2,1)}, bf16[32,16,256]{2,1,0:T(8,128)(2,1)S(1)}, u32[]{:S(2)}, u32[]{:S(2)}) collective-permute-start(bf16[32,16,256]{2,1,0:T(8,128)(2,1)} %copy-done.13), channel_id=1, source_target_pairs={{32,0},{64,32},{96,64},{128,96},{160,128},{192,160},{224,192},{256... | collective-permute-start | bytes 786440 | tf_op jit(solution)/shard_map/ppermute | solution.py:244
  90.9 10.1 %collective-permute-start.4 = (bf16[32,16,256]{2,1,0:T(8,128)(2,1)}, bf16[32,16,256]{2,1,0:T(8,128)(2,1)S(1)}, u32[]{:S(2)}, u32[]{:S(2)}) collective-permute-start(bf16[32,16,256]{2,1,0:T(8,128)(2,1)} %copy-done.13), channel_id=1, source_target_pairs={{0,32},{32,64},{64,96},{96,128},{128,160},{160,192},{192,224},{224... | collective-permute-start | bytes 786440 | tf_op jit(solution)/shard_map/ppermute | solution.py:244
  93.4 10.6 %collective-permute-start.3 = (bf16[32,16,256]{2,1,0:T(8,128)(2,1)S(1)}, bf16[32,16,256]{2,1,0:T(8,128)(2,1)S(1)}, u32[]{:S(2)}, u32[]{:S(2)}) collective-permute-start(bf16[32,16,256]{2,1,0:T(8,128)(2,1)S(1)} %get-tuple-element.31.x1_ref), channel_id=1, source_target_pairs={{32,0},{64,32},{96,64},{128,96},{160,128},{192,160},{224,192},{256... | collective-permute-start | bytes 786440 | tf_op jit(solution)/shard_map/ppermute | solution.py:244
  98.0 10.0 %collective-permute-start.2 = (bf16[32,16,256]{2,1,0:T(8,128)(2,1)S(1)}, bf16[32,16,256]{2,1,0:T(8,128)(2,1)S(1)}, u32[]{:S(2)}, u32[]{:S(2)}) collective-permute-start(bf16[32,16,256]{2,1,0:T(8,128)(2,1)S(1)} %get-tuple-element.31.x1_ref), channel_id=1, source_target_pairs={{0,32},{32,64},{64,96},{96,128},{128,160},{160,192},{192,224},{224... | collective-permute-start | bytes 786440 | tf_op jit(solution)/shard_map/ppermute | solution.py:244
  108.0 1.0 copy-start.6
  122.5 24.8 %all-to-all-start.3 = ((bf16[32,16,256]{2,1,0:T(8,128)(2,1)}), bf16[32,16,256]{2,1,0:T(8,128)(2,1)S(1)}, u32[]{:S(2)}, u32[]{:S(2)}) async-start(bf16[32,16,256]{2,1,0:T(8,128)(2,1)} %third_columns.1), calls=%async_computation.3 | async-start | bytes 524288 | tf_op jit(solution)/shard_map/all_to_all | solution.py:238
  126.6 20.7 %copy-start.4 = (f32[13,16,256]{2,1,0:T(8,128)S(1)}, f32[13,16,256]{2,1,0:T(8,128)}, u32[]{:S(2)}) copy-start(f32[13,16,256]{2,1,0:T(8,128)} %get-tuple-element.29.consts_ref) | copy-start | bytes 638980
  127.7 4.3 %copy-start.11 = (bf16[32,16,256]{2,1,0:T(8,128)(2,1)}, bf16[32,16,256]{2,1,0:T(8,128)(2,1)S(1)}, u32[]{:S(2)}) copy-start(bf16[32,16,256]{2,1,0:T(8,128)(2,1)S(1)} %get-tuple-element.39.x_ref) | copy-start | bytes 786436
  127.7 8.1 %collective-permute-start.7 = (bf16[32,16,256]{2,1,0:T(8,128)(2,1)S(1)}, bf16[32,16,256]{2,1,0:T(8,128)(2,1)S(1)}, u32[]{:S(2)}, u32[]{:S(2)}) collective-permute-start(bf16[32,16,256]{2,1,0:T(8,128)(2,1)S(1)} %get-tuple-element.39.x_ref), channel_id=1, source_target_pairs={{32,0},{64,32},{96,64},{128,96},{160,128},{192,160},{224,192},{256... | collective-permute-start | bytes 786440 | tf_op jit(solution)/shard_map/ppermute | solution.py:244
  129.6 9.9 %collective-permute-start.6 = (bf16[32,16,256]{2,1,0:T(8,128)(2,1)S(1)}, bf16[32,16,256]{2,1,0:T(8,128)(2,1)S(1)}, u32[]{:S(2)}, u32[]{:S(2)}) collective-permute-start(bf16[32,16,256]{2,1,0:T(8,128)(2,1)S(1)} %get-tuple-element.39.x_ref), channel_id=1, source_target_pairs={{0,32},{32,64},{64,96},{96,128},{128,160},{160,192},{192,224},{224... | collective-permute-start | bytes 786440 | tf_op jit(solution)/shard_map/ppermute | solution.py:244
  147.3 1.0 copy-start.7

commit v6 on v5

--- a/solution.py
+++ b/solution.py
@@ -221,7 +221,8 @@
     def put(q, part):
         for v in range(vib):
             p = v * quarters + q
-            z_ref[p] = consts_ref[0] * part[v * rows : (v + 1) * rows] - consts_ref[2] * x1_ref[p].astype(F32)
+            z = consts_ref[0] * part[v * rows : (v + 1) * rows] - consts_ref[2] * x1_ref[p].astype(F32)
+            z_ref[p] = z.astype(BF16)
 
     angular(vib, x_ref, t_ref, v_ref, grid_ref, put)
 
@@ -230,7 +231,7 @@
     pieces, rows, width = z_ref.shape
     quarters = pieces // vib
     for p in range(pieces):
-        x = z_ref[p] + consts_ref[0] * r_ref[p].astype(F32) + consts_ref[1] * mixed(consts_ref, p, quarters, lo_ref, hi_ref)
+        x = z_ref[p].astype(F32) + consts_ref[0] * r_ref[p].astype(F32) + consts_ref[1] * mixed(consts_ref, p, quarters, lo_ref, hi_ref)
         x3_ref[natural(quarters, p, width)] = x
 
 
@@ -292,7 +293,7 @@
     r4 = exchange(sent4)
     x2, x2b = call(part(third_rows), [(old.shape, F32), (packed, BF16)], r3, zr, grant=GRANT)
     lo, hi = neighbours(x2b)
-    (z2,) = call(part(last_rest), [(packed, F32)], x2b, table, pot, x1, consts, room=[grid], flops=a_flops)
+    (z2,) = call(part(last_rest), [(packed, BF16)], x2b, table, pot, x1, consts, room=[grid], flops=a_flops)
     (x3,) = call(part(last), [(old.shape, F32)], r4, z2, lo, hi, consts, grant=GRANT)
     return x2.reshape(newer.shape), x3.reshape(newer.shape)
 

time: 150 us -> 150 us (level)
  no operation moved by 1% of the time
where the time goes in v6:
time: 150 us; the launch traced here: 149 us
  starting transfers between devices  44.3 us (30%)
  waiting for transfers between devices  43.8 us (29%)
  blocking collectives  36.9 us (25%)
  Pallas kernels  17.2 us (11%)
  local copies, waits for them, and re-layouts  6.32 us (4%)
    all_to_all x1, blocking collectives, exchange(): return lax.all_to_all(blocks, 'rad', 0, 0, tiled=True)  36.9 us
    all_to_all x3, waiting for transfers between devices, exchange(): return lax.all_to_all(blocks, 'rad', 0, 0, tiled=True)  29.3 us
    all_to_all x3, starting transfers between devices, exchange(): return lax.all_to_all(blocks, 'rad', 0, 0, tiled=True)  24.8 us
    pallas_call x10, Pallas kernels, call(): pl.pallas_call(kernel, out_shape=shapes, in_specs=[pl.BlockSpec(memory_sp...  17.2 us
    ppermute x4, waiting for transfers between devices, neighbours(): lax.ppermute(array, 'hel', up)  11.6 us
    ppermute x4, starting transfers between devices, neighbours(): lax.ppermute(array, 'hel', [(j, i) for i, j in up])  10.7 us
    ppermute x4, starting transfers between devices, neighbours(): lax.ppermute(array, 'hel', up)  8.87 us
    unnamed x28, local copies, waits for them, and re-layouts  4.52 us
  transfers between devices with their start and end apart: 11, of which 8 were waited for; matrix products, arithmetic and copies ran while one was open for 1% of the time, Pallas kernels for 8%

profile of v6, /device:TPU:6, one launch (start us, length us, event | category | flops | bytes accessed | tf_op | source)
XLA Modules:
  0.0 149.4 jit_solution(5634445240592866273)
XLA Ops:
  0.6 2.2 %pack.1 = (bf16[32,40,128]{2,1,0:T(8,128)(2,1)}, bf16[33,16,256]{2,1,0:T(8,128)(2,1)}) custom-call(f32[16]{0:T(128)} %d_ref.3, f32[1024,128]{1,0:T(8,128)} %bitcast.20, bf16[1,1024]{1,0:T(2,128)(2,1)} %c_ref.3), custom_call_target="tpu_custom_call" | custom-call | flops 8994816 | bytes 1124352 | tf_op jit(solution)/shard_map/pack/pallas_call | solution.py:20
  2.8 16.7 %all-to-all-start = ((bf16[32,40,128]{2,1,0:T(8,128)(2,1)}), bf16[32,40,128]{2,1,0:T(8,128)(2,1)S(1)}, u32[]{:S(2)}, u32[]{:S(2)}) async-start(bf16[32,40,128]{2,1,0:T(8,128)(2,1)} %get-tuple-element.21), calls=%async_computation | async-start | bytes 655360 | tf_op jit(solution)/shard_map/all_to_all | solution.py:239
  19.5 2.2 %collective-permute-start.1 = (bf16[33,16,256]{2,1,0:T(8,128)(2,1)}, bf16[33,16,256]{2,1,0:T(8,128)(2,1)}, u32[]{:S(2)}, u32[]{:S(2)}) collective-permute-start(bf16[33,16,256]{2,1,0:T(8,128)(2,1)} %get-tuple-element.22.x_ref.x0_ref), channel_id=1, source_target_pairs={{32,0},{64,32},{96,64},{128,96},{160,128},{192,160},{224,192},{256... | collective-permute-start | bytes 811016 | tf_op jit(solution)/shard_map/ppermute | solution.py:245
  21.7 2.1 %collective-permute-start = (bf16[33,16,256]{2,1,0:T(8,128)(2,1)}, bf16[33,16,256]{2,1,0:T(8,128)(2,1)}, u32[]{:S(2)}, u32[]{:S(2)}) collective-permute-start(bf16[33,16,256]{2,1,0:T(8,128)(2,1)} %get-tuple-element.22.x_ref.x0_ref), channel_id=1, source_target_pairs={{0,32},{32,64},{64,96},{96,128},{128,160},{160,192},{192,224},{224... | collective-permute-start | bytes 811016 | tf_op jit(solution)/shard_map/ppermute | solution.py:245
  23.9 1.8 %copy.10 = bf16[8,16,1024]{2,1,0:T(8,128)(2,1)} copy(bf16[8,16,1024]{2,0,1:T(8,128)(2,1)} %bitcast.21) | data formatting | bytes 524288 | tf_op jit(solution)/shard_map/transpose | solution.py:258
  25.7 4.2 %first_angular.1 = (f32[32,16,256]{2,1,0:T(8,128)}, f32[32,16,128]{2,1,0:T(8,128)}, f32[3,16,256]{2,1,0:T(8,128)}) custom-call(s32[1]{0:T(128)} %bitcast.3.rank_ref, f32[16]{0:T(128)} %d_ref.3, f32[512]{0:T(512)} %w_ref.1, bf16[33,16,256]{2,1,0:T(8,128)(2,1)} %get-tuple-element.22.x_ref.x0_ref, bf16[1024,1024]{1,0:T(8,128)(2,1)} %bitcast.12, ...), custom_call_target="tpu_custom_call" | custom-call | flops 536870912 | bytes 3989504 | tf_op jit(solution)/shard_map/first_angular/pallas_call | solution.py:20
  29.9 2.7 %collective-permute-done.lo_ref = bf16[33,16,256]{2,1,0:T(8,128)(2,1)} collective-permute-done((bf16[33,16,256]{2,1,0:T(8,128)(2,1)}, bf16[33,16,256]{2,1,0:T(8,128)(2,1)}, u32[]{:S(2)}, u32[]{:S(2)}) %collective-permute-start) | collective-permute-done | bytes 270368 | tf_op jit(solution)/shard_map/ppermute | solution.py:245
  32.6 2.0 %first_coriolis.1 = (bf16[32,16,256]{2,1,0:T(8,128)(2,1)}, f32[13,16,256]{2,1,0:T(8,128)}) custom-call(s32[1]{0:T(128)} %bitcast.3.rank_ref, f32[32,16,256]{2,1,0:T(8,128)} %get-tuple-element.23.za_ref, bf16[33,16,256]{2,1,0:T(8,128)(2,1)} %collective-permute-done.lo_ref, bf16[33,16,256]{2,1,0:T(8,128)(2,1)} %collective-permute-done.1.hi_ref, ...), custom_call_target="tpu_custom_call" | custom-call | flops 12730368 | bytes 1591296 | tf_op jit(solution)/shard_map/first_coriolis/pallas_call | solution.py:20
  34.6 9.2 %all-to-all-done.r_ref = bf16[32,40,128]{2,1,0:T(8,128)(2,1)S(1)} async-done(((bf16[32,40,128]{2,1,0:T(8,128)(2,1)}), bf16[32,40,128]{2,1,0:T(8,128)(2,1)S(1)}, u32[]{:S(2)}, u32[]{:S(2)}) %all-to-all-start) | async-done | bytes 327712 | tf_op jit(solution)/shard_map/all_to_all | solution.py:239
  43.9 1.0 copy-done.12
  45.2 36.9 %all_to_all.20.r_ref = bf16[32,32,256]{2,1,0:T(8,128)(2,1)S(1)} all-to-all(bf16[32,32,256]{2,1,0:T(8,128)(2,1)S(1)} %get-tuple-element.26.s_ref), channel_id=1, replica_groups=mesh['hel'=16,'rad'=32] {'rad'}, dimensions={0} | all-to-all | bytes 1048576 | tf_op jit(solution)/shard_map/all_to_all | solution.py:239
  82.2 1.3 second.1
  85.0 4.0 %all-to-all-start.2 = ((bf16[32,32,256]{2,1,0:T(8,128)(2,1)}), bf16[32,32,256]{2,1,0:T(8,128)(2,1)S(1)}, u32[]{:S(2)}, u32[]{:S(2)}) async-start(bf16[32,32,256]{2,1,0:T(8,128)(2,1)} %copy-done.5), calls=%async_computation.2 | async-start | bytes 1048576 | tf_op jit(solution)/shard_map/all_to_all | solution.py:239
  89.0 1.9 %collective-permute-start.5 = (bf16[32,16,256]{2,1,0:T(8,128)(2,1)}, bf16[32,16,256]{2,1,0:T(8,128)(2,1)S(1)}, u32[]{:S(2)}, u32[]{:S(2)}) collective-permute-start(bf16[32,16,256]{2,1,0:T(8,128)(2,1)} %copy-done.13), channel_id=1, source_target_pairs={{32,0},{64,32},{96,64},{128,96},{160,128},{192,160},{224,192},{256... | collective-permute-start | bytes 786440 | tf_op jit(solution)/shard_map/ppermute | solution.py:245
  90.9 2.4 %collective-permute-start.4 = (bf16[32,16,256]{2,1,0:T(8,128)(2,1)}, bf16[32,16,256]{2,1,0:T(8,128)(2,1)S(1)}, u32[]{:S(2)}, u32[]{:S(2)}) collective-permute-start(bf16[32,16,256]{2,1,0:T(8,128)(2,1)} %copy-done.13), channel_id=1, source_target_pairs={{0,32},{32,64},{64,96},{96,128},{128,160},{160,192},{192,224},{224... | collective-permute-start | bytes 786440 | tf_op jit(solution)/shard_map/ppermute | solution.py:245
  93.4 4.7 %collective-permute-start.3 = (bf16[32,16,256]{2,1,0:T(8,128)(2,1)S(1)}, bf16[32,16,256]{2,1,0:T(8,128)(2,1)S(1)}, u32[]{:S(2)}, u32[]{:S(2)}) collective-permute-start(bf16[32,16,256]{2,1,0:T(8,128)(2,1)S(1)} %get-tuple-element.31.x1_ref), channel_id=1, source_target_pairs={{32,0},{64,32},{96,64},{128,96},{160,128},{192,160},{224,192},{256... | collective-permute-start | bytes 786440 | tf_op jit(solution)/shard_map/ppermute | solution.py:245
  98.0 1.9 %collective-permute-start.2 = (bf16[32,16,256]{2,1,0:T(8,128)(2,1)S(1)}, bf16[32,16,256]{2,1,0:T(8,128)(2,1)S(1)}, u32[]{:S(2)}, u32[]{:S(2)}) collective-permute-start(bf16[32,16,256]{2,1,0:T(8,128)(2,1)S(1)} %get-tuple-element.31.x1_ref), channel_id=1, source_target_pairs={{0,32},{32,64},{64,96},{96,128},{128,160},{160,192},{192,224},{224... | collective-permute-start | bytes 786440 | tf_op jit(solution)/shard_map/ppermute | solution.py:245
  100.0 1.1 collective-permute-done.4.low_ref
  101.0 2.9 %collective-permute-done.3.hi_ref = bf16[32,16,256]{2,1,0:T(8,128)(2,1)S(1)} collective-permute-done((bf16[32,16,256]{2,1,0:T(8,128)(2,1)S(1)}, bf16[32,16,256]{2,1,0:T(8,128)(2,1)S(1)}, u32[]{:S(2)}, u32[]{:S(2)}) %collective-permute-start.3) | collective-permute-done | bytes 262176 | tf_op jit(solution)/shard_map/ppermute | solution.py:245
  103.9 4.1 %collective-permute-done.2.lo_ref = bf16[32,16,256]{2,1,0:T(8,128)(2,1)S(1)} collective-permute-done((bf16[32,16,256]{2,1,0:T(8,128)(2,1)S(1)}, bf16[32,16,256]{2,1,0:T(8,128)(2,1)S(1)}, u32[]{:S(2)}, u32[]{:S(2)}) %collective-permute-start.2) | collective-permute-done | bytes 262176 | tf_op jit(solution)/shard_map/ppermute | solution.py:245
  108.0 1.0 copy-done.6
  109.3 12.2 %all-to-all-done.2.r_ref = bf16[32,32,256]{2,1,0:T(8,128)(2,1)S(1)} async-done(((bf16[32,32,256]{2,1,0:T(8,128)(2,1)}), bf16[32,32,256]{2,1,0:T(8,128)(2,1)S(1)}, u32[]{:S(2)}, u32[]{:S(2)}) %all-to-all-start.2) | async-done | bytes 524320 | tf_op jit(solution)/shard_map/all_to_all | solution.py:239
  121.5 1.0 third_columns.1
  122.5 4.1 %all-to-all-start.3 = ((bf16[32,16,256]{2,1,0:T(8,128)(2,1)}), bf16[32,16,256]{2,1,0:T(8,128)(2,1)S(1)}, u32[]{:S(2)}, u32[]{:S(2)}) async-start(bf16[32,16,256]{2,1,0:T(8,128)(2,1)} %third_columns.1), calls=%async_computation.3 | async-start | bytes 524288 | tf_op jit(solution)/shard_map/all_to_all | solution.py:239
  126.6 1.1 third_rows.1
  127.7 1.9 %collective-permute-start.7 = (bf16[32,16,256]{2,1,0:T(8,128)(2,1)S(1)}, bf16[32,16,256]{2,1,0:T(8,128)(2,1)S(1)}, u32[]{:S(2)}, u32[]{:S(2)}) collective-permute-start(bf16[32,16,256]{2,1,0:T(8,128)(2,1)S(1)} %get-tuple-element.39.x_ref), channel_id=1, source_target_pairs={{32,0},{64,32},{96,64},{128,96},{160,128},{192,160},{224,192},{256... | collective-permute-start | bytes 786440 | tf_op jit(solution)/shard_map/ppermute | solution.py:245
  129.6 2.4 %collective-permute-start.6 = (bf16[32,16,256]{2,1,0:T(8,128)(2,1)S(1)}, bf16[32,16,256]{2,1,0:T(8,128)(2,1)S(1)}, u32[]{:S(2)}, u32[]{:S(2)}) collective-permute-start(bf16[32,16,256]{2,1,0:T(8,128)(2,1)S(1)} %get-tuple-element.39.x_ref), channel_id=1, source_target_pairs={{0,32},{32,64},{64,96},{96,128},{128,160},{160,192},{192,224},{224... | collective-permute-start | bytes 786440 | tf_op jit(solution)/shard_map/ppermute | solution.py:245
  132.0 3.6 %last_rest.1.z_ref = bf16[32,16,256]{2,1,0:T(8,128)(2,1)} custom-call(bf16[32,16,256]{2,1,0:T(8,128)(2,1)} %copy-done.11, bf16[1024,1024]{1,0:T(8,128)(2,1)} %bitcast.13, bf16[128,1024]{1,0:T(8,128)(2,1)} %bitcast.16, bf16[32,16,256]{2,1,0:T(8,128)(2,1)} %copy-done.9, f32[13,16,256]{2,1,0:T(8,128)} %get-tuple-element.29.consts_ref), custom_call_target="tpu_custom_call" | custom-call | flops 536870912 | bytes 3358720 | tf_op jit(solution)/shard_map/last_rest/pallas_call | solution.py:20
  135.7 3.8 %collective-permute-done.6.lo_ref = bf16[32,16,256]{2,1,0:T(8,128)(2,1)S(1)} collective-permute-done((bf16[32,16,256]{2,1,0:T(8,128)(2,1)S(1)}, bf16[32,16,256]{2,1,0:T(8,128)(2,1)S(1)}, u32[]{:S(2)}, u32[]{:S(2)}) %collective-permute-start.6) | collective-permute-done | bytes 262176 | tf_op jit(solution)/shard_map/ppermute | solution.py:245
  139.5 7.9 %all-to-all-done.3.r_ref = bf16[32,16,256]{2,1,0:T(8,128)(2,1)S(1)} async-done(((bf16[32,16,256]{2,1,0:T(8,128)(2,1)}), bf16[32,16,256]{2,1,0:T(8,128)(2,1)S(1)}, u32[]{:S(2)}, u32[]{:S(2)}) %all-to-all-start.3) | async-done | bytes 262176 | tf_op jit(solution)/shard_map/all_to_all | solution.py:239
  147.3 0.9 copy-done.8
  148.3 1.1 last.1
  (30 shorter events, 2.1 us)
Async XLA Ops:
  2.8 41.0 %all-to-all-start = ((bf16[32,40,128]{2,1,0:T(8,128)(2,1)}), bf16[32,40,128]{2,1,0:T(8,128)(2,1)S(1)}, u32[]{:S(2)}, u32[]{:S(2)}) async-start(bf16[32,40,128]{2,1,0:T(8,128)(2,1)} %get-tuple-element.21), calls=%async_computation | async-start | bytes 655360 | tf_op jit(solution)/shard_map/all_to_all | solution.py:239
  19.5 10.4 %collective-permute-start.1 = (bf16[33,16,256]{2,1,0:T(8,128)(2,1)}, bf16[33,16,256]{2,1,0:T(8,128)(2,1)}, u32[]{:S(2)}, u32[]{:S(2)}) collective-permute-start(bf16[33,16,256]{2,1,0:T(8,128)(2,1)} %get-tuple-element.22.x_ref.x0_ref), channel_id=1, source_target_pairs={{32,0},{64,32},{96,64},{128,96},{160,128},{192,160},{224,192},{256... | collective-permute-start | bytes 811016 | tf_op jit(solution)/shard_map/ppermute | solution.py:245
  21.7 10.9 %collective-permute-start = (bf16[33,16,256]{2,1,0:T(8,128)(2,1)}, bf16[33,16,256]{2,1,0:T(8,128)(2,1)}, u32[]{:S(2)}, u32[]{:S(2)}) collective-permute-start(bf16[33,16,256]{2,1,0:T(8,128)(2,1)} %get-tuple-element.22.x_ref.x0_ref), channel_id=1, source_target_pairs={{0,32},{32,64},{64,96},{96,128},{128,160},{160,192},{192,224},{224... | collective-permute-start | bytes 811016 | tf_op jit(solution)/shard_map/ppermute | solution.py:245
  25.7 18.2 %copy-start.1 = (bf16[512,512]{1,0:T(8,128)(2,1)S(1)}, bf16[512,512]{1,0:T(8,128)(2,1)}, u32[]{:S(2)}) copy-start(bf16[512,512]{1,0:T(8,128)(2,1)} %k_ref.5) | copy-start | bytes 1572868
  29.9 52.2 %copy-start = (bf16[1,1024,1024]{2,1,0:T(8,128)(2,1)S(1)}, bf16[1,1024,1024]{2,1,0:T(8,128)(2,1)}, u32[]{:S(2)}) copy-start(bf16[1,1024,1024]{2,1,0:T(8,128)(2,1)} %param.11) | copy-start | bytes 6291460
  29.9 52.2 %copy-start.2 = (bf16[8,16,1024]{2,1,0:T(8,128)(2,1)S(1)}, bf16[8,16,1024]{2,1,0:T(8,128)(2,1)}, u32[]{:S(2)}) copy-start(bf16[8,16,1024]{2,1,0:T(8,128)(2,1)} %copy.10) | copy-start | bytes 786436
  34.6 47.5 %copy-start.3 = (f32[13,16,256]{2,1,0:T(8,128)S(1)}, f32[13,16,256]{2,1,0:T(8,128)}, u32[]{:S(2)}) copy-start(f32[13,16,256]{2,1,0:T(8,128)} %get-tuple-element.29.consts_ref) | copy-start | bytes 638980
  43.9 38.3 %copy-start.7 = (bf16[33,16,256]{2,1,0:T(8,128)(2,1)S(1)}, bf16[33,16,256]{2,1,0:T(8,128)(2,1)}, u32[]{:S(2)}) copy-start(bf16[33,16,256]{2,1,0:T(8,128)(2,1)} %get-tuple-element.22.x_ref.x0_ref) | copy-start | bytes 811012
  43.9 38.3 %copy-start.10 = (f32[32,16,128]{2,1,0:T(8,128)S(1)}, f32[32,16,128]{2,1,0:T(8,128)}, u32[]{:S(2)}) copy-start(f32[32,16,128]{2,1,0:T(8,128)} %get-tuple-element.28.wall_ref) | copy-start | bytes 786436
  43.9 1.0 copy-start.12
  83.5 0.8 copy-start.5
  84.3 0.7 copy-start.13
  85.0 37.5 %copy-start.9 = (bf16[32,16,256]{2,1,0:T(8,128)(2,1)}, bf16[32,16,256]{2,1,0:T(8,128)(2,1)S(1)}, u32[]{:S(2)}) copy-start(bf16[32,16,256]{2,1,0:T(8,128)(2,1)S(1)} %get-tuple-element.31.x1_ref) | copy-start | bytes 786436
  85.0 36.5 %all-to-all-start.2 = ((bf16[32,32,256]{2,1,0:T(8,128)(2,1)}), bf16[32,32,256]{2,1,0:T(8,128)(2,1)S(1)}, u32[]{:S(2)}, u32[]{:S(2)}) async-start(bf16[32,32,256]{2,1,0:T(8,128)(2,1)} %copy-done.5), calls=%async_computation.2 | async-start | bytes 1048576 | tf_op jit(solution)/shard_map/all_to_all | solution.py:239
  89.0 10.9 %collective-permute-start.5 = (bf16[32,16,256]{2,1,0:T(8,128)(2,1)}, bf16[32,16,256]{2,1,0:T(8,128)(2,1)S(1)}, u32[]{:S(2)}, u32[]{:S(2)}) collective-permute-start(bf16[32,16,256]{2,1,0:T(8,128)(2,1)} %copy-done.13), channel_id=1, source_target_pairs={{32,0},{64,32},{96,64},{128,96},{160,128},{192,160},{224,192},{256... | collective-permute-start | bytes 786440 | tf_op jit(solution)/shard_map/ppermute | solution.py:245
  90.9 10.1 %collective-permute-start.4 = (bf16[32,16,256]{2,1,0:T(8,128)(2,1)}, bf16[32,16,256]{2,1,0:T(8,128)(2,1)S(1)}, u32[]{:S(2)}, u32[]{:S(2)}) collective-permute-start(bf16[32,16,256]{2,1,0:T(8,128)(2,1)} %copy-done.13), channel_id=1, source_target_pairs={{0,32},{32,64},{64,96},{96,128},{128,160},{160,192},{192,224},{224... | collective-permute-start | bytes 786440 | tf_op jit(solution)/shard_map/ppermute | solution.py:245
  93.4 10.6 %collective-permute-start.3 = (bf16[32,16,256]{2,1,0:T(8,128)(2,1)S(1)}, bf16[32,16,256]{2,1,0:T(8,128)(2,1)S(1)}, u32[]{:S(2)}, u32[]{:S(2)}) collective-permute-start(bf16[32,16,256]{2,1,0:T(8,128)(2,1)S(1)} %get-tuple-element.31.x1_ref), channel_id=1, source_target_pairs={{32,0},{64,32},{96,64},{128,96},{160,128},{192,160},{224,192},{256... | collective-permute-start | bytes 786440 | tf_op jit(solution)/shard_map/ppermute | solution.py:245
  98.0 10.0 %collective-permute-start.2 = (bf16[32,16,256]{2,1,0:T(8,128)(2,1)S(1)}, bf16[32,16,256]{2,1,0:T(8,128)(2,1)S(1)}, u32[]{:S(2)}, u32[]{:S(2)}) collective-permute-start(bf16[32,16,256]{2,1,0:T(8,128)(2,1)S(1)} %get-tuple-element.31.x1_ref), channel_id=1, source_target_pairs={{0,32},{32,64},{64,96},{96,128},{128,160},{160,192},{192,224},{224... | collective-permute-start | bytes 786440 | tf_op jit(solution)/shard_map/ppermute | solution.py:245
  108.0 1.0 copy-start.6
  122.5 24.8 %all-to-all-start.3 = ((bf16[32,16,256]{2,1,0:T(8,128)(2,1)}), bf16[32,16,256]{2,1,0:T(8,128)(2,1)S(1)}, u32[]{:S(2)}, u32[]{:S(2)}) async-start(bf16[32,16,256]{2,1,0:T(8,128)(2,1)} %third_columns.1), calls=%async_computation.3 | async-start | bytes 524288 | tf_op jit(solution)/shard_map/all_to_all | solution.py:239
  126.6 20.7 %copy-start.4 = (f32[13,16,256]{2,1,0:T(8,128)S(1)}, f32[13,16,256]{2,1,0:T(8,128)}, u32[]{:S(2)}) copy-start(f32[13,16,256]{2,1,0:T(8,128)} %get-tuple-element.29.consts_ref) | copy-start | bytes 638980
  127.7 4.3 %copy-start.11 = (bf16[32,16,256]{2,1,0:T(8,128)(2,1)}, bf16[32,16,256]{2,1,0:T(8,128)(2,1)S(1)}, u32[]{:S(2)}) copy-start(bf16[32,16,256]{2,1,0:T(8,128)(2,1)S(1)} %get-tuple-element.39.x_ref) | copy-start | bytes 786436
  127.7 8.0 %collective-permute-start.7 = (bf16[32,16,256]{2,1,0:T(8,128)(2,1)S(1)}, bf16[32,16,256]{2,1,0:T(8,128)(2,1)S(1)}, u32[]{:S(2)}, u32[]{:S(2)}) collective-permute-start(bf16[32,16,256]{2,1,0:T(8,128)(2,1)S(1)} %get-tuple-element.39.x_ref), channel_id=1, source_target_pairs={{32,0},{64,32},{96,64},{128,96},{160,128},{192,160},{224,192},{256... | collective-permute-start | bytes 786440 | tf_op jit(solution)/shard_map/ppermute | solution.py:245
  129.6 9.8 %collective-permute-start.6 = (bf16[32,16,256]{2,1,0:T(8,128)(2,1)S(1)}, bf16[32,16,256]{2,1,0:T(8,128)(2,1)S(1)}, u32[]{:S(2)}, u32[]{:S(2)}) collective-permute-start(bf16[32,16,256]{2,1,0:T(8,128)(2,1)S(1)} %get-tuple-element.39.x_ref), channel_id=1, source_target_pairs={{0,32},{32,64},{64,96},{96,128},{128,160},{160,192},{192,224},{224... | collective-permute-start | bytes 786440 | tf_op jit(solution)/shard_map/ppermute | solution.py:245
  147.3 1.0 copy-start.8
